TPU v7x, 32 devices: a whole 2x2x4 slice. The times are simulated.
32 devices in a mesh: dp: 4 (over z), tp: 8 (over y, x, core).
Axes of the slice: x: 2, y: 2, z: 4, core: 2. Of those that a mesh axis runs over, the one named last changes fastest.
Arguments:
- img: bfloat16 [8, 2048, 3072], P('dp'), parts along dimension 0
- txt: bfloat16 [8, 256, 3072], P('dp'), parts along dimension 0
- vec: bfloat16 [8, 3072], P('dp'), parts along dimension 0
- ids: int32 [8, 2304, 3], P('dp'), parts along dimension 0
- img_mod_w: bfloat16 [3072, 6, 3072], P(None, None, 'tp')
- img_mod_b: bfloat16 [6, 3072], P(None, 'tp')
- img_qkv_w: bfloat16 [3072, 3, 3072], P(None, None, 'tp')
- img_qkv_b: bfloat16 [3, 3072], P(None, 'tp')
- img_q_gain: bfloat16 [128], replicated
- img_k_gain: bfloat16 [128], replicated
- img_proj_w: bfloat16 [3072, 3072], P('tp')
- img_proj_b: bfloat16 [3072], replicated
- img_fc1_w: bfloat16 [3072, 12288], P(None, 'tp')
- img_fc1_b: bfloat16 [12288], P('tp')
- img_fc2_w: bfloat16 [12288, 3072], P('tp')
- img_fc2_b: bfloat16 [3072], replicated
- txt_mod_w: bfloat16 [3072, 6, 3072], P(None, None, 'tp')
- txt_mod_b: bfloat16 [6, 3072], P(None, 'tp')
- txt_qkv_w: bfloat16 [3072, 3, 3072], P(None, None, 'tp')
- txt_qkv_b: bfloat16 [3, 3072], P(None, 'tp')
- txt_q_gain: bfloat16 [128], replicated
- txt_k_gain: bfloat16 [128], replicated
- txt_proj_w: bfloat16 [3072, 3072], P('tp')
- txt_proj_b: bfloat16 [3072], replicated
- txt_fc1_w: bfloat16 [3072, 12288], P(None, 'tp')
- txt_fc1_b: bfloat16 [12288], P('tp')
- txt_fc2_w: bfloat16 [12288, 3072], P('tp')
- txt_fc2_b: bfloat16 [3072], replicated
Outputs:
- output 1: bfloat16 [8, 2048, 3072], P('dp'), parts along dimension 0
- output 2: bfloat16 [8, 256, 3072], P('dp'), parts along dimension 0
There are 4 independent parts. A program takes and returns all parts, laid end to end along the dimension named above; an argument that names none is the same for every part.
All inputs are finite; a program needn't handle non-finite values.
Results may differ from a plain program's by a relative error of at most 0.014405.
Values are sent between devices in bfloat16 or wider.
A program may use at most 1 GiB of HBM per device.

v0:
```python
import jax
import jax.numpy as jnp
from jax import lax
from jax.sharding import PartitionSpec as P

HEAD = 128
NORM_EPS = 1e-6
ROPE_THETA = 10000.0
AXES_DIM = (16, 56, 56)
PATH_SPECS = (P(None, None, 'tp'), P(None, 'tp'), P(None, None, 'tp'), P(None, 'tp'), P(None), P(None), P('tp', None), P(None), P(None, 'tp'), P('tp'), P('tp', None), P(None))


def layer_norm(tokens):
    values = tokens.astype(jnp.float32)
    centered = values - jnp.mean(values, axis=-1, keepdims=True)
    variance = jnp.mean(centered * centered, axis=-1, keepdims=True)
    return centered * lax.rsqrt(variance + NORM_EPS)


def modulate(tokens, shift_vec, scale_vec):
    scaled = (1.0 + scale_vec.astype(jnp.float32)[:, None, :]) * layer_norm(tokens)
    return (scaled + shift_vec.astype(jnp.float32)[:, None, :]).astype(jnp.bfloat16)


def rope_tables(ids):
    pieces = []
    for axis_idx, axis_dim in enumerate(AXES_DIM):
        inv_freq = ROPE_THETA ** (-jnp.arange(0, axis_dim, 2, dtype=jnp.float32) / axis_dim)
        pieces.append(ids[:, :, axis_idx, None].astype(jnp.float32) * inv_freq)
    angles = jnp.concatenate(pieces, axis=-1)
    return jnp.cos(angles), jnp.sin(angles)


def apply_rope(values, cos_t, sin_t):
    value_pairs = values.reshape(values.shape[:-1] + (values.shape[-1] // 2, 2))
    even_part = value_pairs[..., 0]
    odd_part = value_pairs[..., 1]
    cos_b = cos_t[:, :, None, :]
    sin_b = sin_t[:, :, None, :]
    rotated = jnp.stack([cos_b * even_part - sin_b * odd_part, sin_b * even_part + cos_b * odd_part], axis=-1)
    return rotated.reshape(values.shape)


def rms_gain(values, gain_vec):
    mean_sq = jnp.mean(values * values, axis=-1, keepdims=True)
    return values * lax.rsqrt(mean_sq + NORM_EPS) * gain_vec.astype(jnp.float32)


def modulation(silu_vec, weights):
    flat_mods = jnp.einsum('bd,dke->bke', silu_vec, weights[0], preferred_element_type=jnp.float32)
    return (flat_mods + weights[1].astype(jnp.float32)).astype(jnp.bfloat16)


def path_qkv(tokens, mod_vecs, weights, cos_t, sin_t):
    normed = modulate(tokens, mod_vecs[:, 0], mod_vecs[:, 1])
    proj_qkv = jnp.einsum('bld,dke->blke', normed, weights[2], preferred_element_type=jnp.float32)
    proj_qkv = proj_qkv + weights[3].astype(jnp.float32)
    proj_qkv = proj_qkv.reshape(proj_qkv.shape[:3] + (proj_qkv.shape[3] // HEAD, HEAD))
    query_h = apply_rope(rms_gain(proj_qkv[:, :, 0], weights[4]), cos_t, sin_t).astype(jnp.bfloat16)
    key_h = apply_rope(rms_gain(proj_qkv[:, :, 1], weights[5]), cos_t, sin_t).astype(jnp.bfloat16)
    value_h = proj_qkv[:, :, 2].astype(jnp.bfloat16)
    return query_h, key_h, value_h


def joint_attention(query_h, key_h, value_h):
    scores = jnp.einsum('bqhd,bkhd->bhqk', query_h, key_h, preferred_element_type=jnp.float32) * (HEAD ** -0.5)
    attn_probs = jax.nn.softmax(scores, axis=-1).astype(jnp.bfloat16)
    head_out = jnp.einsum('bhqk,bkhd->bqhd', attn_probs, value_h, preferred_element_type=jnp.float32).astype(jnp.bfloat16)
    return head_out.reshape(head_out.shape[:2] + (head_out.shape[2] * HEAD,))


def project(tokens, weight):
    return jnp.einsum('blk,kd->bld', tokens, weight, preferred_element_type=jnp.float32)


def add_branch(tokens, gate_vec, summed, bias_vec):
    branch = summed.astype(jnp.float32) + bias_vec.astype(jnp.float32)
    return (tokens.astype(jnp.float32) + gate_vec.astype(jnp.float32)[:, None, :] * branch).astype(jnp.bfloat16)


def mlp_hidden(tokens, mod_vecs, weights):
    normed = modulate(tokens, mod_vecs[:, 3], mod_vecs[:, 4])
    pre_act = project(normed, weights[8]) + weights[9].astype(jnp.float32)
    return jax.nn.gelu(pre_act, approximate=True).astype(jnp.bfloat16)


def local_block(img, txt, vec, ids, img_w, txt_w):
    txt_len = txt.shape[1]
    silu_vec = jax.nn.silu(vec.astype(jnp.float32)).astype(jnp.bfloat16)
    own_mods = jnp.stack([modulation(silu_vec, img_w), modulation(silu_vec, txt_w)])
    full_mods = lax.all_gather(own_mods, 'tp', axis=3, tiled=True)
    img_mods = full_mods[0]
    txt_mods = full_mods[1]
    cos_t, sin_t = rope_tables(ids)
    img_q, img_k, img_v = path_qkv(img, img_mods, img_w, cos_t[:, txt_len:], sin_t[:, txt_len:])
    txt_q, txt_k, txt_v = path_qkv(txt, txt_mods, txt_w, cos_t[:, :txt_len], sin_t[:, :txt_len])
    attn_out = joint_attention(jnp.concatenate([txt_q, img_q], axis=1), jnp.concatenate([txt_k, img_k], axis=1), jnp.concatenate([txt_v, img_v], axis=1))
    img_part = project(attn_out[:, txt_len:], img_w[6]).astype(jnp.bfloat16)
    txt_part = project(attn_out[:, :txt_len], txt_w[6]).astype(jnp.bfloat16)
    img_sum, txt_sum = lax.psum((img_part, txt_part), 'tp')
    img_mid = add_branch(img, img_mods[:, 2], img_sum, img_w[7])
    txt_mid = add_branch(txt, txt_mods[:, 2], txt_sum, txt_w[7])
    img_part = project(mlp_hidden(img_mid, img_mods, img_w), img_w[10]).astype(jnp.bfloat16)
    txt_part = project(mlp_hidden(txt_mid, txt_mods, txt_w), txt_w[10]).astype(jnp.bfloat16)
    img_sum, txt_sum = lax.psum((img_part, txt_part), 'tp')
    img_out = add_branch(img_mid, img_mods[:, 5], img_sum, img_w[11])
    txt_out = add_branch(txt_mid, txt_mods[:, 5], txt_sum, txt_w[11])
    return img_out, txt_out


def solution(mesh):
    act_spec = P('dp', None, None)
    mapped = jax.shard_map(local_block, mesh=mesh, in_specs=(act_spec, act_spec, P('dp', None), act_spec, PATH_SPECS, PATH_SPECS), out_specs=(act_spec, act_spec), check_vma=False)

    def forward(img, txt, vec, ids, *weights):
        return mapped(img, txt, vec, ids, weights[:12], weights[12:])

    return forward
```

profile of v0, /device:TPU:0, one launch (start us, length us, event | category | flops | bytes accessed | tf_op | source)
XLA Modules:
  0.0 1249.7 jit_solution(5016566724583936872)
XLA Ops:
  8.8 7.1 fusion.131
  19.8 11.5 all_gather.3
  33.3 16.9 %fusion.165 = (f32[2,2304,64]{1,0,2:T(2,128)S(1)}, f32[2,2304,64]{1,0,2:T(2,128)S(1)}) fusion(f32[2,2304,28]{1,0,2:T(2,128)S(1)} %get-tuple-element.50, f32[2,2304,28]{1,0,2:T(2,128)S(1)} %get-tuple-element.49, f32[2,2304,8]{1,0,2:T(2,128)S(1)} %broadcast_multiply_fusion.2), kind=kLoop, calls=%fused_computation.214 | loop fusion | flops 589824 | bytes 3538944 | tf_op jit(solution)/shard_map/cos | solution.py:31
  53.7 5.7 fusion.114
  62.2 3.0 copy.55
  65.8 9.8 convert_reduce_fusion.1
  75.6 11.3 fusion.14
  87.5 39.3 %broadcast_add_fusion = f32[2,2048,3,384]{1,3,2,0:T(8,128)} fusion(f32[3,384]{1,0:T(4,128)} %convert_element_type.204, bf16[2,2048,3072]{2,1,0:T(8,128)(2,1)} %param.28, f32[2,3072]{1,0:T(2,128)} %get-tuple-element.56, f32[2,2048]{1,0:T(2,128)} %add_rsqrt_fusion.3, f32[2,2048]{1,0:T(2,128)S(1)} %broadcast_multiply_fusion.4, ...), kind=kOutput, calls=%fused_computation.63 | convolution fusion | flops 29071245312 | bytes 51204608 | tf_op jit(solution)/shard_map/bld,dke->blke/dot_general | solution.py:56
  126.8 4.9 fusion.93
  131.7 9.5 multiply_reduce_fusion.2
  160.9 10.3 copy.61
  171.2 10.2 copy.67
  181.5 11.8 multiply_multiply_fusion.2
  193.3 11.7 multiply_multiply_fusion.1
  204.9 10.6 subtract_convert_fusion.1
  215.6 5.8 pad_maximum_fusion.2
  221.3 9.1 copy.64
  230.4 7.7 pad_maximum_fusion.3
  238.1 8.7 copy.70
  246.7 51.8 %fusion.168 = (f32[2,3,2304]{2,1,0:T(4,128)}, f32[2,3,2304,2304]{2,3,1,0:T(8,128)}) fusion(bf16[2,2048,3,128]{3,1,2,0:T(8,128)(2,1)} %copy.70, bf16[2,256,3,128]{3,1,2,0:T(8,128)(2,1)S(1)} %copy-done.11, bf16[2,2048,3,128]{3,1,2,0:T(8,128)(2,1)} %copy.64, bf16[2,256,3,128]{3,1,2,0:T(8,128)(2,1)S(1)} %copy-done.10), kind=kOutput, calls=%fused_computation.215 | convolution fusion | flops 8263436288 | bytes 134535168 | tf_op jit(solution)/shard_map/sub | solution.py:67
  298.6 42.1 %fusion.74 = bf16[2,3,128,2304]{3,2,1,0:T(8,128)(2,1)} fusion(f32[2,3,2304,2304]{2,3,1,0:T(8,128)} %get-tuple-element.52, f32[2,3,2304]{2,1,0:T(4,128)} %get-tuple-element.51, bf16[2,2048,3,128]{1,3,2,0:T(8,128)(2,1)} %fusion.93, bf16[2,256,3,128]{1,3,2,0:T(8,128)(2,1)S(1)} %copy-done.9), kind=kOutput, calls=%fused_computation.86 | convolution fusion | flops 8226275328 | bytes 134535168 | tf_op jit(solution)/shard_map/bhqk,bkhd->bqhd/dot_general | solution.py:68
  340.6 5.3 convolution_convert_fusion.2
  345.9 19.0 %convolution_convert_fusion.1 = bf16[2,2048,3072]{2,1,0:T(8,128)(2,1)} fusion(bf16[2,2304,384]{1,2,0:T(8,128)(2,1)} %bitcast.159, bf16[384,3072]{1,0:T(8,128)(2,1)S(1)} %copy-done), kind=kOutput, calls=%fused_computation.44 | convolution fusion | flops 9676259328 | bytes 30670848 | tf_op jit(solution)/shard_map/blk,kd->bld/dot_general | solution.py:73
  366.3 339.5 %all-reduce.7.cloned.1.call-done = (bf16[2,2048,3072]{2,1,0:T(8,128)(2,1)}, bf16[2,256,3072]{2,1,0:T(8,128)(2,1)}) async-done(((bf16[2,2048,3072]{2,1,0:T(8,128)(2,1)}, bf16[2,256,3072]{2,1,0:T(8,128)(2,1)}), (bf16[2,2048,3072]{2,1,0:T(8,128)(2,1)}, bf16[2,256,3072]{2,1,0:T(8,128)(2,1)})) %all-reduce.7.cloned.1.call-update) | async-done | bytes 28311568 | tf_op jit(solution)/shard_map/psum | solution.py:100
  705.8 26.0 %convert_reduce_fusion = (f32[2,2048]{1,0:T(2,128)S(1)}, bf16[2,2048,3072]{2,1,0:T(8,128)(2,1)}) fusion(f32[3072]{0:T(1024)S(1)} %convert_element_type.218, bf16[2,2048,3072]{2,1,0:T(8,128)(2,1)} %get-tuple-element.8, f32[2,3072]{1,0:T(2,128)S(1)} %copy-done.16, bf16[2,2048,3072]{2,1,0:T(8,128)(2,1)} %param.28), kind=kLoop, calls=%fused_computation.7 | loop fusion | flops 100659200 | bytes 75550720 | tf_op jit(solution)/shard_map/reduce_sum | solution.py:15
  731.9 13.6 %fusion.10 = f32[2,2048]{1,0:T(2,128)S(1)} fusion(bf16[2,2048,3072]{2,1,0:T(8,128)(2,1)} %get-tuple-element.13, f32[2,2048]{1,0:T(2,128)S(1)} %broadcast_multiply_fusion.3), kind=kLoop, calls=%fused_computation.17 | loop fusion | flops 50327552 | bytes 25198592 | tf_op jit(solution)/shard_map/reduce_sum | solution.py:16
  750.6 50.6 %fusion.27.clone.4 = bf16[2,2048,1536]{2,1,0:T(8,128)(2,1)} fusion(bf16[2,2048,3072]{2,1,0:T(8,128)(2,1)} %get-tuple-element.13, f32[2,3072]{1,0:T(2,128)S(1)} %copy-done.25, f32[2,2048]{1,0:T(2,128)S(1)} %add_rsqrt_fusion.2, f32[2,2048]{1,0:T(2,128)S(1)} %broadcast_multiply_fusion.3, f32[2,3072]{1,0:T(2,128)S(1)} %copy-done.24, ...), kind=kOutput, calls=%fused_computation.35.clone.clone.clone.1 | convolution fusion | flops 38793117696 | bytes 47273984 | tf_op jit(solution)/shard_map/blk,kd->bld/dot_general | solution.py:73
  801.3 46.6 %convolution_convert_fusion = bf16[2,2048,3072]{2,1,0:T(8,128)(2,1)} fusion(bf16[1536,3072]{1,0:T(8,128)(2,1)} %param.42, bf16[2,2048,1536]{2,1,0:T(8,128)(2,1)} %fusion.27.clone.4), kind=kOutput, calls=%fused_computation.43 | convolution fusion | flops 38667288576 | bytes 47185920 | tf_op jit(solution)/shard_map/blk,kd->bld/dot_general | solution.py:73
  847.9 19.5 %fusion.75 = bf16[2,256,3072]{2,1,0:T(8,128)(2,1)} fusion(bf16[1536,3072]{1,0:T(8,128)(2,1)} %param.54, bf16[3072,1536]{1,0:T(8,128)(2,1)} %param.52, bf16[2,256,3072]{2,1,0:T(8,128)(2,1)} %copy-done.4, f32[2,3072]{1,0:T(2,128)S(1)} %copy-done.23, f32[2,256]{1,0:T(2,128)S(1)} %copy-done.37, f32[2,256]{1,0:T(2,128)S(1)} %copy-done.27, ...), kind=kOutput, calls=%fused_computation.89 | convolution fusion | flops 9682550784 | bytes 25225216 | tf_op jit(solution)/shard_map/blk,kd->bld/dot_general | solution.py:73
  868.1 339.9 %all-reduce.5.cloned.1.call-done = (bf16[2,2048,3072]{2,1,0:T(8,128)(2,1)}, bf16[2,256,3072]{2,1,0:T(8,128)(2,1)}) async-done(((bf16[2,2048,3072]{2,1,0:T(8,128)(2,1)}, bf16[2,256,3072]{2,1,0:T(8,128)(2,1)}), (bf16[2,2048,3072]{2,1,0:T(8,128)(2,1)}, bf16[2,256,3072]{2,1,0:T(8,128)(2,1)})) %all-reduce.5.cloned.1.call-update) | async-done | bytes 28311568 | tf_op jit(solution)/shard_map/psum | solution.py:105
  1208.0 5.8 fusion.73
  1213.9 28.7 %fusion.19 = bf16[2,2048,3072]{2,1,0:T(8,128)(2,1)} fusion(bf16[2,2048,3072]{2,1,0:T(8,128)(2,1)} %get-tuple-element.13, bf16[2,2048,3072]{2,1,0:T(8,128)(2,1)} %get-tuple-element.6, f32[3072]{0:T(1024)S(1)} %convert_element_type.227, f32[2,3072]{1,0:T(2,128)S(1)} %copy-done.17), kind=kLoop, calls=%fused_computation.26 | loop fusion | flops 75497472 | bytes 75534336 | tf_op jit(solution)/shard_map/convert_element_type | solution.py:78
  (160 shorter events, 41.5 us)
Async XLA Ops:
  7.2 338.8 %copy-start = (bf16[384,3072]{1,0:T(8,128)(2,1)S(1)}, bf16[384,3072]{1,0:T(8,128)(2,1)}, u32[]{:S(2)}) copy-start(bf16[384,3072]{1,0:T(8,128)(2,1)} %param.38) | copy-start | bytes 7077892
  7.2 698.6 %all-reduce.7.cloned.1.call-start = ((), (), s32[]{:S(2)}) async-start(), calls=%async_computation.1 | async-start | bytes 56623104 | tf_op jit(solution)/shard_map/psum | solution.py:100
  8.8 9.1 copy-start.5
  8.8 9.1 copy-start.21
  17.9 15.0 %copy-start.20 = (s32[2,2304,3]{1,0,2:T(2,128)S(1)}, s32[2,2304,3]{1,0,2:T(2,128)}, u32[]{:S(2)}) copy-start(s32[2,2304,3]{1,0,2:T(2,128)} %param.31) | copy-start | bytes 165892
  19.8 32.4 %copy-start.2 = (bf16[2,256,3072]{2,1,0:T(8,128)(2,1)S(1)}, bf16[2,256,3072]{2,1,0:T(8,128)(2,1)}, u32[]{:S(2)}) copy-start(bf16[2,256,3072]{2,1,0:T(8,128)(2,1)} %param.29) | copy-start | bytes 9437188
  33.3 20.4 %slice-start.3 = ((s8[7077888]{0:T(1024)(128)(4,1)}), s8[4194304]{0:T(1024)(128)(4,1)S(1)}, s32[]{:S(2)}) async-start(s8[7077888]{0:T(1024)(128)(4,1)} %bitcast.156), calls=%async_computation.5 | async-start | bytes 8388608
  131.7 9.5 copy-start.38
  131.7 10.3 copy-start.39
  131.7 11.0 copy-start.40
  131.7 11.8 copy-start.41
  171.2 10.2 copy-start.13
  181.5 11.8 copy-start.12
  193.3 11.7 copy-start.6
  230.4 16.4 %copy-start.10 = (bf16[2,256,3,128]{3,1,2,0:T(8,128)(2,1)S(1)}, bf16[2,256,3,128]{3,1,2,0:T(8,128)(2,1)}, u32[]{:S(2)}) copy-start(bf16[2,256,3,128]{3,1,2,0:T(8,128)(2,1)} %copy.63) | copy-start | bytes 1179652
  230.4 16.3 %copy-start.11 = (bf16[2,256,3,128]{3,1,2,0:T(8,128)(2,1)S(1)}, bf16[2,256,3,128]{3,1,2,0:T(8,128)(2,1)}, u32[]{:S(2)}) copy-start(bf16[2,256,3,128]{3,1,2,0:T(8,128)(2,1)} %copy.69) | copy-start | bytes 1179652
  246.7 51.8 %copy-start.9 = (bf16[2,256,3,128]{1,3,2,0:T(8,128)(2,1)S(1)}, bf16[2,256,3,128]{1,3,2,0:T(8,128)(2,1)}, u32[]{:S(2)}) copy-start(bf16[2,256,3,128]{1,3,2,0:T(8,128)(2,1)} %fusion.132) | copy-start | bytes 1179652
  365.0 340.8 %copy-start.16 = (f32[2,3072]{1,0:T(2,128)S(1)}, f32[2,3072]{1,0:T(2,128)}, u32[]{:S(2)}) copy-start(f32[2,3072]{1,0:T(2,128)} %get-tuple-element.55) | copy-start | bytes 73732
  365.0 843.0 %all-reduce.5.cloned.1.call-start = ((), (), s32[]{:S(2)}) async-start(), calls=%async_computation | async-start | bytes 56623104 | tf_op jit(solution)/shard_map/psum | solution.py:105
  731.8 13.7 %copy-start.3 = (bf16[2,256,3072]{2,1,0:T(8,128)(2,1)S(1)}, bf16[2,256,3072]{2,1,0:T(8,128)(2,1)}, u32[]{:S(2)}) copy-start(bf16[2,256,3072]{2,1,0:T(8,128)(2,1)} %param.29) | copy-start | bytes 9437188
  731.8 13.7 %copy-start.7 = (bf16[2,256,3072]{2,1,0:T(8,128)(2,1)S(1)}, bf16[2,256,3072]{2,1,0:T(8,128)(2,1)}, u32[]{:S(2)}) copy-start(bf16[2,256,3072]{2,1,0:T(8,128)(2,1)} %get-tuple-element.9) | copy-start | bytes 9437188
  731.8 13.7 %copy-start.18 = (f32[2,3072]{1,0:T(2,128)S(1)}, f32[2,3072]{1,0:T(2,128)}, u32[]{:S(2)}) copy-start(f32[2,3072]{1,0:T(2,128)} %get-tuple-element.36) | copy-start | bytes 73732
  731.8 18.8 %slice-start = ((s8[9437184]{0:T(1024)(128)(4,1)}), s8[4194304]{0:T(1024)(128)(4,1)S(1)}, s32[]{:S(2)}) async-start(s8[9437184]{0:T(1024)(128)(4,1)} %bitcast.154), calls=%async_computation.2 | async-start | bytes 8388608
  731.8 18.8 %slice-start.1 = ((s8[9437184]{0:T(1024)(128)(4,1)}), s8[4194304]{0:T(1024)(128)(4,1)S(1)}, s32[]{:S(2)}) async-start(s8[9437184]{0:T(1024)(128)(4,1)} %bitcast.154), calls=%async_computation.3 | async-start | bytes 8388608
  801.3 46.6 %copy-start.22 = (f32[2,3072]{1,0:T(2,128)S(1)}, f32[2,3072]{1,0:T(2,128)}, u32[]{:S(2)}) copy-start(f32[2,3072]{1,0:T(2,128)} %get-tuple-element.42) | copy-start | bytes 73732
  801.3 46.6 %copy-start.23 = (f32[2,3072]{1,0:T(2,128)S(1)}, f32[2,3072]{1,0:T(2,128)}, u32[]{:S(2)}) copy-start(f32[2,3072]{1,0:T(2,128)} %get-tuple-element.35) | copy-start | bytes 73732
  801.3 46.6 %copy-start.27 = (f32[2,256]{1,0:T(2,128)S(1)}, f32[2,256]{1,0:T(2,128)}, u32[]{:S(2)}) copy-start(f32[2,256]{1,0:T(2,128)} %copy-done.26) | copy-start | bytes 6148
  801.3 46.6 %copy-start.28 = (f32[1536]{0:T(1024)S(1)}, f32[1536]{0:T(1024)}, u32[]{:S(2)}) copy-start(f32[1536]{0:T(1024)} %convert_element_type.236) | copy-start | bytes 18436
  801.3 46.6 %copy-start.37 = (f32[2,256]{1,0:T(2,128)S(1)}, f32[2,256]{1,0:T(2,128)}, u32[]{:S(2)}) copy-start(f32[2,256]{1,0:T(2,128)} %add_rsqrt_fusion.6) | copy-start | bytes 6148
  867.4 340.6 %copy-start.19 = (f32[2,3072]{1,0:T(2,128)S(1)}, f32[2,3072]{1,0:T(2,128)}, u32[]{:S(2)}) copy-start(f32[2,3072]{1,0:T(2,128)} %get-tuple-element.34) | copy-start | bytes 73732
  868.1 345.8 %copy-start.17 = (f32[2,3072]{1,0:T(2,128)S(1)}, f32[2,3072]{1,0:T(2,128)}, u32[]{:S(2)}) copy-start(f32[2,3072]{1,0:T(2,128)} %get-tuple-element.58) | copy-start | bytes 73732
  1213.9 28.8 %copy-start.1 = (bf16[384,3072]{1,0:T(8,128)(2,1)S(1)}, bf16[384,3072]{1,0:T(8,128)(2,1)}, u32[]{:S(2)}) copy-start(bf16[384,3072]{1,0:T(8,128)(2,1)} %param.38) | copy-start | bytes 7077892
  (17 other events, 52.6 us)
Sparse Core Ops, SparseCore 0:
  365.1 340.6 all-reduce.6
  867.5 340.4 all-reduce.4
where the time goes:
time: 1250 us
  waiting for transfers between devices  679 us (54%)
  matrix products  289 us (23%)
  other arithmetic  189 us (15%)
  local copies, waits for them, and re-layouts  66.4 us (5%)
  between operations  14.8 us (1%)
    psum x2, waiting for transfers between devices, local_block(): img_sum, txt_sum = lax.psum((img_part, txt_part), 'tp')  679 us
    dot_general x5, matrix products, project(): jnp.einsum('blk,kd->bld', tokens, weight, preferred_element_type=jnp.floa...  141 us
    sub x1, matrix products, joint_attention(): attn_probs = jax.nn.softmax(scores, axis=-1).astype(jnp.bfloat16)  51.8 us
    dot_general x2, matrix products, path_qkv(): jnp.einsum('bld,dke->blke', normed, weights[2], preferred_element_type=jn...  45 us
    dot_general x1, matrix products, joint_attention(): jnp.einsum('bhqk,bkhd->bqhd', attn_probs, value_h, preferred_element_type...  42.1 us
    reduce_sum x4, other arithmetic, layer_norm(): centered = values - jnp.mean(values, axis=-1, keepdims=True)  38.1 us
    convert_element_type x2, other arithmetic, add_branch(): (tokens.astype(jnp.float32) + gate_vec.astype(jnp.float32)[:, None, :] *...  34.6 us
    reduce_sum x4, other arithmetic, layer_norm(): variance = jnp.mean(centered * centered, axis=-1, keepdims=True)  26.8 us
  transfers between devices with their start and end apart: 2, of which 2 were waited for; matrix products, arithmetic and copies ran while one was open for 0% of the time, Pallas kernels for 0%

commit v1 on v0

v1 whole, which is shorter than its diff:
```python
import functools

import jax
import jax.numpy as jnp
import numpy as np
from jax import lax
from jax.experimental import pallas as pl
from jax.experimental.pallas import tpu as pltpu
from jax.sharding import PartitionSpec as P

HEAD = 128
NORM_EPS = 1e-6
ROPE_THETA = 10000.0
AXES_DIM = (16, 56, 56)
N_IDS = 64
PATH_SPECS = (P(None, None, 'tp'), P(None, 'tp'), P(None, None, 'tp'), P(None, 'tp'), P(None), P(None), P('tp', None), P(None), P(None, 'tp'), P('tp'), P('tp', None), P(None))
F32 = jnp.float32
BF16 = jnp.bfloat16


def rope_table():
    cos = np.zeros((3 * N_IDS, HEAD), np.float32)
    sin = np.zeros((3 * N_IDS, HEAD), np.float32)
    lane = 0
    for axis, dim in enumerate(AXES_DIM):
        inv_freq = np.float32(ROPE_THETA) ** (-np.arange(0, dim, 2, dtype=np.float32) / np.float32(dim))
        angles = np.arange(N_IDS, dtype=np.float32)[:, None] * inv_freq.astype(np.float32)
        rows = slice(axis * N_IDS, (axis + 1) * N_IDS)
        c = np.cos(angles.astype(np.float64)).astype(np.float32)
        s = np.sin(angles.astype(np.float64)).astype(np.float32)
        cos[rows, lane:lane + dim:2] = c
        cos[rows, lane + 1:lane + dim:2] = c
        sin[rows, lane:lane + dim:2] = -s
        sin[rows, lane + 1:lane + dim:2] = s
        lane += dim
    parts = []
    for table in (cos, sin):
        rest = table
        for _ in range(3):
            part = rest.astype(jnp.bfloat16)
            parts.append(np.asarray(part))
            rest = rest - np.asarray(part).astype(np.float32)
    return np.concatenate(parts, axis=1)


def qkv_kernel(heads, x_ref, mod_ref, w_ref, b_ref, gain_ref, ids_ref, tab_ref, *rest):
    out_ref = rest[-1]
    width = heads * HEAD
    rows = x_ref.shape[1]
    x = x_ref[0].astype(F32)
    centered = x - jnp.mean(x, axis=-1, keepdims=True)
    variance = jnp.mean(centered * centered, axis=-1, keepdims=True)
    normed = centered * lax.rsqrt(variance + NORM_EPS)
    shift = mod_ref[0, 0:1, :].astype(F32)
    scale = mod_ref[0, 1:2, :].astype(F32)
    u = ((1.0 + scale) * normed + shift).astype(BF16)

    code = lax.broadcasted_iota(jnp.int32, (N_IDS, rows), 0)
    hot = jnp.concatenate([(ids_ref[0, axis:axis + 1, :] == code).astype(F32).astype(BF16) for axis in range(3)], axis=0)
    parts = lax.dot_general(hot, tab_ref[...], (((0,), (0,)), ((), ())), preferred_element_type=F32)
    cos_t = parts[:, 0:128] + parts[:, 128:256] + parts[:, 256:384]
    sin_t = parts[:, 384:512] + parts[:, 512:640] + parts[:, 640:768]
    even = lax.broadcasted_iota(jnp.int32, (rows, HEAD), 1) % 2 == 0

    for j in range(3):
        a = jnp.dot(u, w_ref[j], preferred_element_type=F32) + b_ref[j:j + 1, :].astype(F32)
        for h in range(heads):
            t = a[:, h * HEAD:(h + 1) * HEAD]
            if j < 2:
                mean_sq = jnp.mean(t * t, axis=-1, keepdims=True)
                t = t * lax.rsqrt(mean_sq + NORM_EPS) * gain_ref[j:j + 1, :]
                swapped = jnp.where(even, pltpu.roll(t, HEAD - 1, 1), pltpu.roll(t, 1, 1))
                t = t * cos_t + swapped * sin_t
            col = j * width + h * HEAD
            out_ref[0, :, col:col + HEAD] = t.astype(BF16)


def qkv_call(x, mods, w3, bias, gains, ids_t, table, base, row_block, first_block, total_rows):
    batch, length, dim = x.shape
    width = w3.shape[2]
    heads = width // HEAD
    steps = length // row_block
    in_specs = [
        pl.BlockSpec((1, row_block, dim), lambda b, r: (b, r, 0)),
        pl.BlockSpec((1, 6, dim), lambda b, r: (b, 0, 0)),
        pl.BlockSpec((3, dim, width), lambda b, r: (0, 0, 0)),
        pl.BlockSpec((3, width), lambda b, r: (0, 0)),
        pl.BlockSpec((2, HEAD), lambda b, r: (0, 0)),
        pl.BlockSpec((1, 3, row_block), lambda b, r: (b, 0, r + first_block)),
        pl.BlockSpec(table.shape, lambda b, r: (0, 0)),
    ]
    args = [x, mods, w3, bias, gains, ids_t, table]
    aliases = {}
    if base is not None:
        in_specs.append(pl.BlockSpec(memory_space=pl.ANY))
        args.append(base)
        aliases = {7: 0}
    flops = 2 * batch * length * dim * 3 * width
    return pl.pallas_call(
        functools.partial(qkv_kernel, heads),
        grid=(batch, steps),
        in_specs=in_specs,
        out_specs=pl.BlockSpec((1, row_block, 3 * width), lambda b, r: (b, r + first_block, 0)),
        out_shape=jax.ShapeDtypeStruct((batch, total_rows, 3 * width), BF16),
        input_output_aliases=aliases,
        compiler_params=pltpu.CompilerParams(dimension_semantics=("arbitrary", "arbitrary"), vmem_limit_bytes=60 * 2**20),
        cost_estimate=pl.CostEstimate(flops=flops, bytes_accessed=2 * batch * length * (dim + 3 * width) + 6 * dim * width, transcendentals=0),
        name="qkv",
    )(*args)


LOG2E = 1.4426950408889634


def attention_kernel(sub, q_ref, k_ref, v_ref, out_ref):
    rows = q_ref.shape[1]
    k = k_ref[0]
    v = v_ref[0]
    factor = HEAD ** -0.5 * LOG2E
    for r in range(0, rows, sub):
        q = q_ref[0, r:r + sub, :]
        s = lax.dot_general(q, k, (((1,), (1,)), ((), ())), preferred_element_type=F32)
        top = jnp.max(s, axis=-1, keepdims=True)
        p = jnp.exp2((s - top) * factor)
        total = jnp.sum(p, axis=-1, keepdims=True)
        o = jnp.dot(p.astype(BF16), v, preferred_element_type=F32)
        out_ref[0, r:r + sub, :] = (o * (1.0 / total)).astype(BF16)


def attention_call(qkv, heads, row_block, sub, first_row, rows):
    batch, total_rows, width3 = qkv.shape
    first = first_row // row_block
    return pl.pallas_call(
        functools.partial(attention_kernel, sub),
        grid=(batch, heads, rows // row_block),
        in_specs=[
            pl.BlockSpec((1, row_block, HEAD), lambda b, h, r: (b, r + first, h)),
            pl.BlockSpec((1, total_rows, HEAD), lambda b, h, r: (b, 0, heads + h)),
            pl.BlockSpec((1, total_rows, HEAD), lambda b, h, r: (b, 0, 2 * heads + h)),
        ],
        out_specs=pl.BlockSpec((1, row_block, HEAD), lambda b, h, r: (b, r, h)),
        out_shape=jax.ShapeDtypeStruct((batch, rows, heads * HEAD), BF16),
        compiler_params=pltpu.CompilerParams(dimension_semantics=("arbitrary",) * 3, vmem_limit_bytes=60 * 2**20),
        cost_estimate=pl.CostEstimate(flops=4 * batch * heads * rows * total_rows * HEAD * 2, bytes_accessed=batch * heads * (2 * rows + 2 * total_rows) * HEAD * 2, transcendentals=batch * heads * rows * total_rows),
        name="attention",
    )(qkv, qkv, qkv)


def layer_norm(tokens):
    values = tokens.astype(F32)
    centered = values - jnp.mean(values, axis=-1, keepdims=True)
    variance = jnp.mean(centered * centered, axis=-1, keepdims=True)
    return centered * lax.rsqrt(variance + NORM_EPS)


def modulate(tokens, shift_vec, scale_vec):
    scaled = (1.0 + scale_vec.astype(F32)[:, None, :]) * layer_norm(tokens)
    return (scaled + shift_vec.astype(F32)[:, None, :]).astype(BF16)


def modulation(silu_vec, weights):
    flat_mods = jnp.einsum('bd,dke->bke', silu_vec, weights[0], preferred_element_type=F32)
    return (flat_mods + weights[1].astype(F32)).astype(BF16)


def project(tokens, weight):
    return jnp.einsum('blk,kd->bld', tokens, weight, preferred_element_type=F32)


def add_branch(tokens, gate_vec, summed, bias_vec):
    branch = summed.astype(F32) + bias_vec.astype(F32)
    return (tokens.astype(F32) + gate_vec.astype(F32)[:, None, :] * branch).astype(BF16)


MESH = pl.DeviceIdType.MESH
(O_CORE, O_FIRST, O_SECOND, O_RELAY, U_CORE, PART_CORE, RS_FIRST, RS_SECOND, OUT_FIRST, OUT_SECOND, OUT_RELAY, CORE_OWN, CORE_FIRST, CORE_SECOND, CORE_RELAY) = range(15)
(L_O, L_X, L_OUT) = range(3)
SLOTS = 4
SEMS = 8


def block_kernel(cfg, o_hbm, x_hbm, ut_hbm, x1t_hbm, wp_hbm, w1t_hbm, w2t_hbm, w1i_hbm, w2i_hbm, vec_ref, fb_ref, out_hbm,
                 wp, w1, w2, obuf, xbuf, x1buf, x1keep, u2, hid, psend, precv, own, chip_sum, rs1, keep2, rs2_out, rs2_in, outb,
                 wsem, lsem, tsem, ssem, rsem):
    batch, txt_chunks, img_chunks, per_img, rows, tile = cfg
    half, quarter, eighth = rows // 2, rows // 4, rows // 8
    dim = wp.shape[0]
    ff = w1.shape[1]
    cols = o_hbm.shape[2]
    total = txt_chunks + img_chunks
    per_txt = txt_chunks // batch

    me = lax.axis_index('tp')
    core = me % 2
    xi = (me // 2) % 2
    yi = me // 4
    partner = me + 1 - 2 * core
    x_next = me + 2 - 4 * xi
    y_next = me + 4 - 8 * yi
    first = x_next * (1 - core) + y_next * core
    second = x_next * core + y_next * (1 - core)
    bit1 = xi * (1 - core) + yi * core
    bit2 = xi * core + yi * (1 - core)

    barrier = pltpu.get_barrier_semaphore()
    for dev in (partner, first, second):
        pl.semaphore_signal(barrier, inc=1, device_id={'tp': dev}, device_id_type=MESH)
    pl.semaphore_wait(barrier, 3)

    def remote(kind, g, src, dst, dev):
        return pltpu.make_async_remote_copy(src_ref=src, dst_ref=dst, send_sem=ssem.at[kind, g % SEMS], recv_sem=rsem.at[kind, g % SEMS], device_id={'tp': dev}, device_id_type=MESH)

    def rows_at(start, size):
        return pl.ds(pl.multiple_of(start, size), size)

    def img_pos(g):
        k = g - txt_chunks
        return k // per_img, (k % per_img) * rows

    def chip_cols(dev):
        return rows_at((dev // 2) * (2 * cols), 2 * cols)

    def own_rows(b1, b2):
        return core * half + b1 * quarter + b2 * eighth

    def o_local(g):
        b, r0 = img_pos(g)
        return pltpu.make_async_copy(o_hbm.at[b, rows_at(r0 + core * half, half), :], obuf.at[g % SLOTS, :, rows_at(me * cols, cols)], lsem.at[L_O, g % SEMS])

    def o_core(g):
        b, r0 = img_pos(g)
        return remote(O_CORE, g, o_hbm.at[b, rows_at(r0 + (1 - core) * half, half), :], obuf.at[g % SLOTS, :, rows_at(me * cols, cols)], partner)

    def o_send(kind, g, owner, dev):
        ref = obuf.at[g % SLOTS, :, chip_cols(owner)]
        return remote(kind, g, ref, ref, dev)

    def x_load(g):
        b, r0 = img_pos(g)
        return pltpu.make_async_copy(x_hbm.at[b, rows_at(r0 + core * half, half), :], xbuf.at[g % 2], lsem.at[L_X, g % SEMS])

    def u_core(g):
        ref = u2.at[g % 2, rows_at(core * half, half), :]
        return remote(U_CORE, g, ref, ref, partner)

    def part_core(g):
        return remote(PART_CORE, g, psend, precv.at[g % 2], partner)

    def rs_first(g):
        return remote(RS_FIRST, g, chip_sum.at[rows_at((1 - bit1) * quarter, quarter), :], rs1.at[g % 2], first)

    def rs_second(g):
        return remote(RS_SECOND, g, rs2_out.at[g % 2], rs2_in.at[g % SLOTS], second)

    def out_ref(g, b1, b2):
        return out_hbm.at[rows_at(g * rows + own_rows(b1, b2), eighth), :]

    def out_send(kind, g, b1, b2, dev):
        ref = out_ref(g, b1, b2)
        mine = kind in (OUT_FIRST, OUT_SECOND, CORE_OWN)
        return remote(kind, g, outb.at[g % SLOTS] if mine else ref, ref, dev)

    def out_local(g):
        return pltpu.make_async_copy(outb.at[g % SLOTS], out_ref(g, bit1, bit2), lsem.at[L_OUT, g % SEMS])

    def txt_load(g):
        b, r0 = g // per_txt, (g % per_txt) * rows
        return (pltpu.make_async_copy(ut_hbm.at[b, rows_at(r0, rows), :], u2.at[g % 2], tsem.at[0, g % 2]),
                pltpu.make_async_copy(x1t_hbm.at[b, rows_at(r0 + own_rows(bit1, bit2), eighth), :], x1keep.at[g % SLOTS], tsem.at[1, g % 2]))

    def w_load(k, src, dst):
        return pltpu.make_async_copy(src, dst, wsem.at[k])

    def select(g):
        txt = (g < txt_chunks).astype(jnp.int32)
        return txt * (g // per_txt) + (1 - txt) * (batch + (g - txt_chunks) // per_img)

    def start_o(g):
        o_local(g).start()
        o_core(g).start()

    def send_o(g):
        o_local(g).wait()
        o_core(g).wait()
        o_send(O_FIRST, g, me, first).start()
        o_send(O_SECOND, g, me, second).start()

    def relay_o(g):
        o_send(O_FIRST, g, first, first).wait_recv()
        o_send(O_RELAY, g, first, second).start()
        x_load(g).start()

    def project(g):
        o_send(O_FIRST, g, me, first).wait_send()
        o_send(O_SECOND, g, me, second).wait_send()
        o_send(O_RELAY, g, first, second).wait_send()
        o_send(O_SECOND, g, second, second).wait_recv()
        o_send(O_RELAY, g, second, second).wait_recv()
        x_load(g).wait()

        @pl.when(g == txt_chunks)
        def _():
            w_load(2, wp_hbm, wp).wait()

        sel = select(g)
        slot = g % SLOTS

        def columns(n, carry):
            at = rows_at(n * tile, tile)
            acc = jnp.dot(obuf[slot], wp[:, at], preferred_element_type=F32)
            branch = acc + vec_ref[sel, 1:2, at]
            x1buf[:, at] = (xbuf[g % 2, :, at].astype(F32) + vec_ref[sel, 0:1, at] * branch).astype(BF16)
            return carry

        lax.fori_loop(0, dim // tile, columns, 0)

        def norm(n, carry):
            at = rows_at(n * 16, 16)
            x = x1buf[at, :].astype(F32)
            centered = x - jnp.mean(x, axis=-1, keepdims=True)
            variance = jnp.mean(centered * centered, axis=-1, keepdims=True)
            normed = centered * lax.rsqrt(variance + NORM_EPS)
            u2[g % 2, rows_at(core * half + n * 16, 16), :] = ((1.0 + vec_ref[sel, 2:3, :]) * normed + vec_ref[sel, 3:4, :]).astype(BF16)
            return carry

        lax.fori_loop(0, half // 16, norm, 0)
        u_core(g).start()
        x1keep[slot] = x1buf[rows_at(bit1 * quarter + bit2 * eighth, eighth), :]

    def mlp(g):
        @pl.when(g < txt_chunks)
        def _():
            for copy in txt_load(g):
                copy.wait()

        @pl.when(g >= txt_chunks)
        def _():
            u_core(g).wait()

        @pl.when(g == 0)
        def _():
            w_load(0, w1t_hbm, w1).wait()
            w_load(1, w2t_hbm, w2).wait()

        @pl.when(g == txt_chunks)
        def _():
            w_load(0, w1i_hbm, w1).wait()
            w_load(1, w2i_hbm, w2).wait()

        path = (g >= txt_chunks).astype(jnp.int32)

        def hidden(n, carry):
            at = rows_at(n * tile, tile)
            acc = jnp.dot(u2[g % 2], w1[:, at], preferred_element_type=F32)
            pre = acc + fb_ref[path, 0:1, at]
            hid[:, at] = jax.nn.gelu(pre, approximate=True).astype(BF16)
            return carry

        lax.fori_loop(0, ff // tile, hidden, 0)

        def theirs(n, carry):
            at = rows_at(n * tile, tile)
            psend[:, at] = jnp.dot(hid[rows_at((1 - core) * half, half), :], w2[:, at], preferred_element_type=F32).astype(BF16)
            return carry

        lax.fori_loop(0, dim // tile, theirs, 0)
        part_core(g).start()

        def mine(n, carry):
            at = rows_at(n * tile, tile)
            own[:, at] = jnp.dot(hid[rows_at(core * half, half), :], w2[:, at], preferred_element_type=F32)
            return carry

        lax.fori_loop(0, dim // tile, mine, 0)

        @pl.when(g == txt_chunks - 1)
        def _():
            w_load(0, w1i_hbm, w1).start()
            w_load(1, w2i_hbm, w2).start()

        part_core(g).wait()

        def add(n, carry):
            at = rows_at(n * 16, 16)
            chip_sum[at, :] = (own[at, :] + precv[g % 2, at, :].astype(F32)).astype(BF16)
            return carry

        lax.fori_loop(0, half // 16, add, 0)
        rs_first(g).start()

    def add_first(g):
        rs_first(g).wait()
        rs2_out[g % 2] = (chip_sum[rows_at(bit1 * quarter + (1 - bit2) * eighth, eighth), :].astype(F32) + rs1[g % 2, rows_at((1 - bit2) * eighth, eighth), :].astype(F32)).astype(BF16)
        rs_second(g).start()
        keep2[g % 2] = chip_sum[rows_at(bit1 * quarter + bit2 * eighth, eighth), :].astype(F32) + rs1[g % 2, rows_at(bit2 * eighth, eighth), :].astype(F32)

    def finish(g):
        rs_second(g).wait()
        sel = select(g)
        branch = keep2[g % 2] + rs2_in[g % SLOTS].astype(F32) + vec_ref[sel, 5:6, :]
        outb[g % SLOTS] = (x1keep[g % SLOTS].astype(F32) + vec_ref[sel, 4:5, :] * branch).astype(BF16)
        out_send(OUT_FIRST, g, bit1, bit2, first).start()
        out_send(OUT_SECOND, g, bit1, bit2, second).start()
        out_send(CORE_OWN, g, bit1, bit2, partner).start()
        out_local(g).start()

    def relay_out(g):
        out_send(OUT_FIRST, g, 1 - bit1, bit2, first).wait_recv()
        out_send(OUT_RELAY, g, 1 - bit1, bit2, second).start()
        out_send(CORE_FIRST, g, 1 - bit1, bit2, partner).start()
        out_send(OUT_SECOND, g, bit1, 1 - bit2, second).wait_recv()
        out_send(CORE_SECOND, g, bit1, 1 - bit2, partner).start()

    def relay_core(g):
        out_send(OUT_RELAY, g, 1 - bit1, 1 - bit2, second).wait_recv()
        out_send(CORE_RELAY, g, 1 - bit1, 1 - bit2, partner).start()

    def drain(g):
        out_local(g).wait()
        out_send(OUT_FIRST, g, bit1, bit2, first).wait_send()
        out_send(OUT_SECOND, g, bit1, bit2, second).wait_send()
        out_send(OUT_RELAY, g, 1 - bit1, bit2, second).wait_send()
        out_send(CORE_OWN, g, bit1, bit2, partner).wait()
        out_send(CORE_FIRST, g, 1 - bit1, bit2, partner).wait()
        out_send(CORE_SECOND, g, bit1, 1 - bit2, partner).wait()
        out_send(CORE_RELAY, g, 1 - bit1, 1 - bit2, partner).wait()

    w_load(0, w1t_hbm, w1).start()
    w_load(1, w2t_hbm, w2).start()
    for g in range(txt_chunks):
        for copy in txt_load(g):
            copy.start()
    w_load(2, wp_hbm, wp).start()

    stages = ((start_o, 4, txt_chunks), (send_o, 3, txt_chunks), (relay_o, 2, txt_chunks), (relay_out, -3, 0), (relay_core, -4, 0), (drain, -5, 0),
              (project, 1, txt_chunks), (add_first, -1, 0), (finish, -2, 0), (mlp, 0, 0))
    lead = 4 - txt_chunks

    def step(i, carry):
        for stage, ahead, lowest in stages:
            g = i - lead + ahead

            @pl.when((g >= lowest) & (g < total))
            def _():
                stage(g)
        return carry

    lax.fori_loop(0, total + lead + 5, step, 0)


def block_call(img_o, x, u_txt, x1_txt, wp, w1t, w2t, w1i, w2i, vecs, fb, rows):
    batch, img_len, dim = x.shape
    txt_len = u_txt.shape[1]
    ff = w1t.shape[1]
    txt_chunks = batch * (txt_len // rows)
    per_img = img_len // rows
    img_chunks = batch * per_img
    assert txt_chunks == 2
    half, quarter, eighth = rows // 2, rows // 4, rows // 8
    cfg = (batch, txt_chunks, img_chunks, per_img, rows, 512)
    total = txt_chunks + img_chunks
    anywhere = pl.BlockSpec(memory_space=pl.ANY)
    flops = 2 * total * rows * 2 * dim * ff + 2 * img_chunks * half * dim * dim
    return pl.pallas_call(
        functools.partial(block_kernel, cfg),
        in_specs=[anywhere] * 9 + [pl.BlockSpec(memory_space=pltpu.VMEM)] * 2,
        out_specs=anywhere,
        out_shape=jax.ShapeDtypeStruct((total * rows, dim), BF16),
        scratch_shapes=[
            pltpu.VMEM((dim, dim), BF16),
            pltpu.VMEM((dim, ff), BF16),
            pltpu.VMEM((ff, dim), BF16),
            pltpu.VMEM((SLOTS, half, dim), BF16),
            pltpu.VMEM((2, half, dim), BF16),
            pltpu.VMEM((half, dim), BF16),
            pltpu.VMEM((SLOTS, eighth, dim), BF16),
            pltpu.VMEM((2, rows, dim), BF16),
            pltpu.VMEM((rows, ff), BF16),
            pltpu.VMEM((half, dim), BF16),
            pltpu.VMEM((2, half, dim), BF16),
            pltpu.VMEM((half, dim), F32),
            pltpu.VMEM((half, dim), BF16),
            pltpu.VMEM((2, quarter, dim), BF16),
            pltpu.VMEM((2, eighth, dim), F32),
            pltpu.VMEM((2, eighth, dim), BF16),
            pltpu.VMEM((SLOTS, eighth, dim), BF16),
            pltpu.VMEM((SLOTS, eighth, dim), BF16),
            pltpu.SemaphoreType.DMA((3,)),
            pltpu.SemaphoreType.DMA((3, SEMS)),
            pltpu.SemaphoreType.DMA((2, 2)),
            pltpu.SemaphoreType.DMA((15, SEMS)),
            pltpu.SemaphoreType.DMA((15, SEMS)),
        ],
        compiler_params=pltpu.CompilerParams(collective_id=0, has_side_effects=True, vmem_limit_bytes=67043328),
        cost_estimate=pl.CostEstimate(flops=flops, bytes_accessed=4 * dim * dim + 8 * dim * ff + 4 * total * rows * dim, transcendentals=0),
        name="block",
    )(img_o, x, u_txt, x1_txt, wp, w1t, w2t, w1i, w2i, vecs, fb)


def local_block(img, txt, vec, ids, img_w, txt_w):
    batch, txt_len = txt.shape[:2]
    img_len = img.shape[1]
    width = img_w[6].shape[0]
    heads = width // HEAD
    proj_w = lax.all_gather(img_w[6], 'tp', axis=0, tiled=True)
    silu_vec = jax.nn.silu(vec.astype(F32)).astype(BF16)
    own_mods = jnp.stack([modulation(silu_vec, img_w), modulation(silu_vec, txt_w)])
    full_mods = lax.all_gather(own_mods, 'tp', axis=3, tiled=True)
    img_mods = full_mods[0]
    txt_mods = full_mods[1]
    table = jnp.asarray(rope_table())
    ids_t = jnp.swapaxes(ids, 1, 2)
    block = min(256, txt_len)
    total = txt_len + img_len

    def gains(w):
        return jnp.stack([w[4], w[5]]).astype(F32)

    def w3(w):
        return jnp.transpose(w[2], (1, 0, 2))

    qkv = qkv_call(txt, txt_mods, w3(txt_w), txt_w[3], gains(txt_w), ids_t, table, None, block, 0, total)
    qkv = qkv_call(img, img_mods, w3(img_w), img_w[3], gains(img_w), ids_t, table, qkv, block, txt_len // block, total)
    txt_o = attention_call(qkv, heads, block, block // 2, 0, txt_len)
    img_o = attention_call(qkv, heads, block, block // 2, txt_len, img_len)
    txt_part = project(txt_o, txt_w[6]).astype(BF16)
    txt_sum = lax.psum(txt_part, 'tp')
    txt_mid = add_branch(txt, txt_mods[:, 2], txt_sum, txt_w[7])
    txt_u = modulate(txt_mid, txt_mods[:, 3], txt_mods[:, 4])

    def vectors(mods, w):
        def rep(bias):
            return jnp.broadcast_to(bias.astype(F32), (batch, bias.shape[0]))
        m = mods.astype(F32)
        zero = jnp.zeros_like(m[:, 0])
        return jnp.stack([m[:, 2], rep(w[7]), m[:, 4], m[:, 3], m[:, 5], rep(w[11]), zero, zero], axis=1)

    vecs = jnp.concatenate([vectors(txt_mods, txt_w), vectors(img_mods, img_w)], axis=0)
    fb = jnp.stack([txt_w[9], img_w[9]]).astype(F32)[:, None, :]
    flat = block_call(img_o, img, txt_u, txt_mid, proj_w, txt_w[8], txt_w[10], img_w[8], img_w[10], vecs, fb, block)
    split = batch * txt_len
    return flat[split:].reshape(img.shape), flat[:split].reshape(txt.shape)


def solution(mesh):
    act_spec = P('dp', None, None)
    mapped = jax.shard_map(local_block, mesh=mesh, in_specs=(act_spec, act_spec, P('dp', None), act_spec, PATH_SPECS, PATH_SPECS), out_specs=(act_spec, act_spec), check_vma=False)

    def forward(img, txt, vec, ids, *weights):
        return mapped(img, txt, vec, ids, weights[:12], weights[12:])

    return forward
```

time: 1250 us -> 703 us (0.56)
  waiting for transfers between devices: 679 us -> 90.2 us
  Pallas kernels: 0 us -> 532 us
  matrix products: 289 us -> 13.6 us
  other arithmetic: 189 us -> 12.9 us
  local copies, waits for them, and re-layouts: 66.4 us -> 28.5 us
    psum x2 -> x1, waiting for transfers between devices: 679 us -> 0.01 us  [local_block(): txt_sum = lax.psum(txt_part, 'tp')]
    pallas_call x0 -> x5, Pallas kernels: none -> 532 us  [the longest x1 381 us: block_call(): pl.pallas_call(functools.partial(block_kernel, cfg), in_specs=[anywhere]...]
    dot_general x10 -> x3, matrix products: 237 us -> 13.6 us  [the longest x2 9.05 us: modulation(): jnp.einsum('bd,dke->bke', silu_vec, weights[0], preferred_element_type=F32)]
    all_gather x0 -> x1, waiting for transfers between devices: none -> 89.7 us  [local_block(): proj_w = lax.all_gather(img_w[6], 'tp', axis=0, tiled=True)]
    sub x1 -> x0, matrix products: 51.8 us -> none  [joint_attention(): attn_probs = jax.nn.softmax(scores, axis=-1).astype(jnp.bfloat16)]
    reduce_sum x4 -> x1, other arithmetic: 38.1 us -> 3.66 us  [layer_norm(): centered = values - jnp.mean(values, axis=-1, keepdims=True)]
    convert_element_type x12 -> x8, other arithmetic: 37.3 us -> 7.41 us  [the longest x1 3.5 us: modulate(): return (scaled + shift_vec.astype(F32)[:, None, :]).astype(BF16)]
    another operation x6 -> x0, other arithmetic: 29.2 us -> none  [the longest x4 17 us: apply_rope(): jnp.stack([cos_b * even_part - sin_b * odd_part, sin_b * even_part + cos_...]
  transfers between devices with their start and end apart: 2 -> 2, of which waited for: 2 -> 1; matrix products, arithmetic and copies ran while one was open for 0% -> 1% of each run, Pallas kernels for 0% -> 10%
where the time goes in v1:
time: 703 us
  Pallas kernels  532 us (76%)
  waiting for transfers between devices  90.2 us (13%)
  local copies, waits for them, and re-layouts  28.5 us (4%)
  between operations  14.3 us (2%)
  matrix products  13.6 us (2%)
  other arithmetic  12.9 us (2%)
  blocking collectives  11 us (2%)
    pallas_call x1, Pallas kernels, block_call(): pl.pallas_call(functools.partial(block_kernel, cfg), in_specs=[anywhere]...  381 us
    all_gather x1, waiting for transfers between devices, local_block(): proj_w = lax.all_gather(img_w[6], 'tp', axis=0, tiled=True)  89.7 us
    pallas_call x2, Pallas kernels, attention_call(): pl.pallas_call(functools.partial(attention_kernel, sub), grid=(batch, hea...  78.5 us
    pallas_call x2, Pallas kernels, qkv_call(): pl.pallas_call(functools.partial(qkv_kernel, heads), grid=(batch, steps),...  71.7 us
    slice x2, local copies, waits for them, and re-layouts, local_block(): return (flat[split:].reshape(img.shape), flat[:split].reshape(txt.shape))  24.4 us
  transfers between devices with their start and end apart: 2, of which 1 were waited for; matrix products, arithmetic and copies ran while one was open for 1% of the time, Pallas kernels for 10%

profile of v1, /device:TPU:0, one launch (start us, length us, event | category | flops | bytes accessed | tf_op | source)
XLA Modules:
  0.0 702.6 jit_solution(12792579047099673984)
XLA Ops:
  7.2 0.0 all-reduce.2.cloned.1.call-start
  7.2 0.7 convert_element_type.81
  7.9 0.7 convert_element_type.83
  8.6 7.1 %fusion.18 = f32[2,6,384]{2,0,1:T(2,128)S(1)} fusion(bf16[3072,6,384]{2,0,1:T(8,128)(2,1)} %param.33, bf16[2,3072]{1,0:T(2,128)(2,1)} %param.31), kind=kOutput, calls=%fused_computation.39 | convolution fusion | flops 28348416 | bytes 14186496 | tf_op jit(solution)/shard_map/bd,dke->bke/dot_general | solution.py:162
  15.7 1.9 copy-done.1
  17.7 1.9 fusion.16
  19.6 0.6 copy.52
  20.3 11.0 %all_gather.6 = bf16[2,2,6,3072]{3,2,1,0:T(8,128)(2,1)S(1)} all-gather(bf16[2,2,6,384]{3,2,1,0:T(8,128)(2,1)S(1)} %pad_maximum_fusion.1), channel_id=1, replica_groups=mesh['dp'=4,'tp'=8] {'tp'}, dimensions={3}, use_global_device_ids=true | all-gather | bytes 165888 | tf_op jit(solution)/shard_map/all_gather | solution.py:508
  31.3 0.7 fusion.23
  32.0 0.6 maximum_convert_fusion.1.gain_ref
  32.6 0.6 maximum_convert_fusion.2.gain_ref
  33.2 11.3 %qkv.2.rest_0_ = bf16[2,2304,1152]{2,1,0:T(8,128)(2,1)} custom-call(bf16[2,256,3072]{2,1,0:T(8,128)(2,1)} %x_ref.2, bf16[2,6,3072]{2,1,0:T(8,128)(2,1)} %get-tuple-element.10.mod_ref, bf16[3,3072,384]{2,1,0:T(8,128)(2,1)} %bitcast.43, bf16[3,384]{1,0:T(4,128)(2,1)} %b_ref.2, f32[2,128]{1,0:T(2,128)} %maximum_convert_fusion.2.gain_ref, ...), custom_call_target="tpu_custom_call" | custom-call | flops 3623878656 | bytes 11403264 | tf_op jit(solution)/shard_map/qkv/pallas_call | solution.py:99
  44.5 60.4 %qkv.3.q_ref.k_ref.v_ref = bf16[2,2304,1152]{2,1,0:T(8,128)(2,1)} custom-call(bf16[2,2048,3072]{2,1,0:T(8,128)(2,1)} %x_hbm.1, bf16[2,6,3072]{2,1,0:T(8,128)(2,1)} %get-tuple-element.11.mod_ref, bf16[3,3072,384]{2,1,0:T(8,128)(2,1)} %bitcast.54, bf16[3,384]{1,0:T(4,128)(2,1)} %b_ref.3, ...), custom_call_target="tpu_custom_call", output_to_operand_aliasing={{}: (7, {})} | custom-call | flops 28991029248 | bytes 41680896 | tf_op jit(solution)/shard_map/qkv/pallas_call | solution.py:99
  105.0 10.2 %attention.3 = bf16[2,256,384]{2,1,0:T(8,128)(2,1)} custom-call(bf16[2,2304,1152]{2,1,0:T(8,128)(2,1)} %qkv.3.q_ref.k_ref.v_ref, bf16[2,2304,1152]{2,1,0:T(8,128)(2,1)} %qkv.3.q_ref.k_ref.v_ref, bf16[2,2304,1152]{2,1,0:T(8,128)(2,1)} %qkv.3.q_ref.k_ref.v_ref), custom_call_target="tpu_custom_call" | custom-call | flops 3623878656 | bytes 7864320 | tf_op jit(solution)/shard_map/attention/pallas_call | solution.py:133
  115.2 4.6 convolution_convert_fusion
  119.9 0.3 all-gather.2.cloned.1.call-start
  120.1 0.5 all-gather.2.cloned.1.call-update
  120.9 0.1 fusion.24
  121.0 0.3 stack.51
  121.3 0.1 fusion.25
  121.4 0.3 stack.52
  121.7 0.6 maximum_convert_fusion.fb_ref
  122.3 0.8 pad_maximum_fusion.vec_ref
  123.1 68.3 %attention.2.o_hbm = bf16[2,2048,384]{2,1,0:T(8,128)(2,1)} custom-call(bf16[2,2304,1152]{2,1,0:T(8,128)(2,1)} %qkv.3.q_ref.k_ref.v_ref, bf16[2,2304,1152]{2,1,0:T(8,128)(2,1)} %qkv.3.q_ref.k_ref.v_ref, bf16[2,2304,1152]{2,1,0:T(8,128)(2,1)} %qkv.3.q_ref.k_ref.v_ref), custom_call_target="tpu_custom_call" | custom-call | flops 28991029248 | bytes 13369344 | tf_op jit(solution)/shard_map/attention/pallas_call | solution.py:133
  191.4 3.7 convert_reduce_fusion
  195.1 1.0 fusion.2
  196.1 0.6 copy-done
  196.7 3.5 fusion.5.ut_hbm
  200.2 89.7 %all-gather.2.cloned.1.call-done.wp_hbm = bf16[3072,3072]{1,0:T(8,128)(2,1)} async-done(((bf16[384,3072]{1,0:T(8,128)(2,1)}), bf16[3072,3072]{1,0:T(8,128)(2,1)}) %all-gather.2.cloned.1.call-update) | async-done | bytes 18874384 | tf_op jit(solution)/shard_map/all_gather | solution.py:505
  289.9 381.4 %block.1 = bf16[4608,3072]{1,0:T(8,128)(2,1)} custom-call(bf16[2,2048,384]{2,1,0:T(8,128)(2,1)} %attention.2.o_hbm, bf16[2,2048,3072]{2,1,0:T(8,128)(2,1)} %x_hbm.1, bf16[2,256,3072]{2,1,0:T(8,128)(2,1)} %fusion.5.ut_hbm, bf16[2,256,3072]{2,1,0:T(8,128)(2,1)} %copy-done, bf16[3072,3072]{1,0:T(8,128)(2,1)} %all-gather.2.cloned.1.call-done.wp_hbm, ...), custom_call_target="tpu_custom_call" | custom-call | flops 125627793408 | bytes 132120576 | tf_op jit(solution)/shard_map/block/pallas_call | solution.py:464
  671.3 3.8 slice.59
  675.1 20.7 %slice.58 = bf16[4096,3072]{1,0:T(8,128)(2,1)} slice(bf16[4608,3072]{1,0:T(8,128)(2,1)} %block.1), slice={[512:4608], [0:3072]} | slice | bytes 50331648 | tf_op jit(solution)/shard_map/slice | solution.py:542
  (51 shorter events, 0.3 us)
Async XLA Ops:
  7.2 184.2 %all-reduce.2.cloned.1.call-start = ((), (), s32[]{:S(2)}) async-start(), calls=%async_computation | async-start | bytes 6291456 | tf_op jit(solution)/shard_map/psum | solution.py:527
  8.6 9.1 %copy-start.1 = (bf16[3072,6,384]{2,0,1:T(8,128)(2,1)S(1)}, bf16[3072,6,384]{2,0,1:T(8,128)(2,1)}, u32[]{:S(2)}) copy-start(bf16[3072,6,384]{2,0,1:T(8,128)(2,1)} %param.45) | copy-start | bytes 42467332
  8.6 9.1 %copy-start.5 = (bf16[2,3072]{1,0:T(2,128)(2,1)S(1)}, bf16[2,3072]{1,0:T(2,128)(2,1)}, u32[]{:S(2)}) copy-start(bf16[2,3072]{1,0:T(2,128)(2,1)} %param.31) | copy-start | bytes 36868
  17.7 2.0 copy-start.4
  17.7 14.4 %copy-start.12 = (bf16[128]{0:T(256)(128)(2,1)S(1)}, bf16[128]{0:T(256)(128)(2,1)}, u32[]{:S(2)}) copy-start(bf16[128]{0:T(256)(128)(2,1)} %param.38) | copy-start | bytes 772
  17.7 14.4 %copy-start.13 = (bf16[128]{0:T(256)(128)(2,1)S(1)}, bf16[128]{0:T(256)(128)(2,1)}, u32[]{:S(2)}) copy-start(bf16[128]{0:T(256)(128)(2,1)} %param.37) | copy-start | bytes 772
  17.7 14.9 %copy-start.14 = (bf16[128]{0:T(256)(128)(2,1)S(1)}, bf16[128]{0:T(256)(128)(2,1)}, u32[]{:S(2)}) copy-start(bf16[128]{0:T(256)(128)(2,1)} %param.50) | copy-start | bytes 772
  17.7 14.9 %copy-start.15 = (bf16[128]{0:T(256)(128)(2,1)S(1)}, bf16[128]{0:T(256)(128)(2,1)}, u32[]{:S(2)}) copy-start(bf16[128]{0:T(256)(128)(2,1)} %param.49) | copy-start | bytes 772
  105.0 10.2 %copy-start.16 = (bf16[384,3072]{1,0:T(8,128)(2,1)S(1)}, bf16[384,3072]{1,0:T(8,128)(2,1)}, u32[]{:S(2)}) copy-start(bf16[384,3072]{1,0:T(8,128)(2,1)} %param.51) | copy-start | bytes 7077892
  115.2 5.4 copy-start.10
  115.2 5.5 copy-start.11
  115.2 5.5 copy-start.6
  115.2 5.5 copy-start.3
  115.2 5.7 copy-start.7
  115.2 6.2 copy-start.8
  115.2 6.2 copy-start.9
  119.9 170.1 %all-gather.2.cloned.1.call-start = ((), (), s32[]{:S(2)}) async-start(), calls=%async_computation.1 | async-start | bytes 21233664 | tf_op jit(solution)/shard_map/all_gather | solution.py:505
  123.1 68.3 %copy-start.2 = (bf16[2,256,3072]{2,1,0:T(8,128)(2,1)S(1)}, bf16[2,256,3072]{2,1,0:T(8,128)(2,1)}, u32[]{:S(2)}) copy-start(bf16[2,256,3072]{2,1,0:T(8,128)(2,1)} %x_ref.2) | copy-start | bytes 9437188
  195.1 1.6 copy-start
Sparse Core Ops, SparseCore 0:
  120.0 69.4 all-reduce.1
  191.3 98.5 all-gather.1

commit v2 on v1

v2 whole, which is shorter than its diff:
```python
import functools

import jax
import jax.numpy as jnp
import numpy as np
from jax import lax
from jax.experimental import pallas as pl
from jax.experimental.pallas import tpu as pltpu
from jax.sharding import PartitionSpec as P

HEAD = 128
NORM_EPS = 1e-6
ROPE_THETA = 10000.0
AXES_DIM = (16, 56, 56)
N_IDS = 64
WHOLE = None
PATH_SPECS = (P(WHOLE, WHOLE, 'tp'), P(WHOLE, 'tp'), P(WHOLE, WHOLE, 'tp'), P(WHOLE, 'tp'), P(WHOLE), P(WHOLE), P('tp', WHOLE), P(WHOLE), P(WHOLE, 'tp'), P('tp'), P('tp', WHOLE), P(WHOLE))
F32 = jnp.float32
BF16 = jnp.bfloat16


def rope_table():
    cos = np.zeros((3 * N_IDS, HEAD), np.float32)
    sin = np.zeros((3 * N_IDS, HEAD), np.float32)
    lane = 0
    for axis, dim in enumerate(AXES_DIM):
        inv_freq = np.float32(ROPE_THETA) ** (-np.arange(0, dim, 2, dtype=np.float32) / np.float32(dim))
        angles = np.arange(N_IDS, dtype=np.float32)[:, None] * inv_freq.astype(np.float32)
        rows = slice(axis * N_IDS, (axis + 1) * N_IDS)
        c = np.cos(angles.astype(np.float64)).astype(np.float32)
        s = np.sin(angles.astype(np.float64)).astype(np.float32)
        cos[rows, lane:lane + dim:2] = c
        cos[rows, lane + 1:lane + dim:2] = c
        sin[rows, lane:lane + dim:2] = -s
        sin[rows, lane + 1:lane + dim:2] = s
        lane += dim
    parts = []
    for table in (cos, sin):
        rest = table
        for _ in range(3):
            part = rest.astype(jnp.bfloat16)
            parts.append(np.asarray(part))
            rest = rest - np.asarray(part).astype(np.float32)
    return np.concatenate(parts, axis=1)


MESH = pl.DeviceIdType.MESH


SHIFT1, SCALE1, GATE1, SHIFT2, SCALE2, GATE2, PROJ_B, FC2_B = range(8)
VMEM_BYTES = 67043328


def row_of(ref, sel, row, at=slice(None)):
    return ref[sel, pl.ds(row, 1), at]


def loop(count, body):
    lax.fori_loop(0, count, lambda i, carry: (body(i), carry)[-1], 0)


def normalize(x):
    centered = x - jnp.mean(x, axis=-1, keepdims=True)
    variance = jnp.mean(centered * centered, axis=-1, keepdims=True)
    return centered * lax.rsqrt(variance + NORM_EPS)


def modulated(x, vec_ref, sel, shift, scale):
    return ((1.0 + row_of(vec_ref, sel, scale)) * normalize(x) + row_of(vec_ref, sel, shift)).astype(BF16)


def mods_kernel(vec_ref, bt_ref, bi_ref, pt_ref, pi_ref, ft_ref, fi_ref, wt_hbm, wi_hbm, out_ref, wbuf, early, late, wsem, ssem, rsem):
    me = lax.axis_index('tp')
    batch, dim = vec_ref.shape
    width = wbuf.shape[3]
    n_dev = early.shape[0]
    barrier = pltpu.get_barrier_semaphore()
    for d in range(1, n_dev):
        pl.semaphore_signal(barrier, inc=1, device_id={'tp': (me + d) % n_dev}, device_id_type=MESH)

    def load(path, k):
        return pltpu.make_async_copy((wt_hbm, wi_hbm)[path].at[k], wbuf.at[path, k], wsem.at[path, k])

    for k in range(PROJ_B):
        for path in range(2):
            load(path, k).start()
    v = vec_ref[...].astype(F32)
    silu = (v * (1.0 / (1.0 + jnp.exp(-v)))).astype(BF16)
    pl.semaphore_wait(barrier, n_dev - 1)

    def compute(k, path):
        load(path, k).wait()
        acc = jnp.dot(silu, wbuf[path, k], preferred_element_type=F32)
        return (acc + (bt_ref, bi_ref)[path][k:k + 1, :].astype(F32)).astype(BF16)

    def send(part, buf, d):
        return pltpu.make_async_remote_copy(src_ref=buf.at[me], dst_ref=buf.at[me], send_sem=ssem.at[part, d], recv_sem=rsem.at[part, d], device_id={'tp': (me + d) % n_dev}, device_id_type=MESH)

    def receive(part, buf, d):
        ref = buf.at[(me + n_dev - d) % n_dev]
        return pltpu.make_async_remote_copy(src_ref=ref, dst_ref=ref, send_sem=ssem.at[part, d], recv_sem=rsem.at[part, d], device_id={'tp': (me + d) % n_dev}, device_id_type=MESH)

    early_kinds, late_kinds = (SHIFT1, SCALE1), (GATE1, SHIFT2, SCALE2, GATE2)
    early[me] = jnp.concatenate([compute(k, path) for k in early_kinds for path in range(2)], axis=0)
    for d in range(1, n_dev):
        send(0, early, d).start()
    late[me] = jnp.concatenate([compute(k, path) for k in late_kinds for path in range(2)], axis=0)
    for d in range(1, n_dev):
        send(1, late, d).start()

    def row(ref):
        return ref[...].astype(F32)

    for path, (pb, fb) in enumerate(((pt_ref, ft_ref), (pi_ref, fi_ref))):
        for b in range(batch):
            out_ref[path * batch + b, PROJ_B:FC2_B, :] = row(pb)
            out_ref[path * batch + b, FC2_B:, :] = row(fb)
    for part, buf, ks in ((0, early, early_kinds), (1, late, late_kinds)):
        for d in range(1, n_dev):
            send(part, buf, d).wait_send()
            receive(part, buf, d).wait_recv()
        for j in range(n_dev):
            for n, k in enumerate(ks):
                for path in range(2):
                    at = (n * 2 + path) * batch
                    block = buf[j, at:at + batch, :].astype(F32)
                    for b in range(batch):
                        out_ref[path * batch + b, k:k + 1, j * width:(j + 1) * width] = block[b:b + 1, :]


def mods_call(vec, wt, wi, bt, bi, pt, pi, ft, fi, n_dev):
    batch, dim = vec.shape
    width = wt.shape[2]
    vmem = pl.BlockSpec(memory_space=pltpu.VMEM)
    anywhere = pl.BlockSpec(memory_space=pl.ANY)
    return pl.pallas_call(
        mods_kernel,
        in_specs=[vmem] * 7 + [anywhere] * 2,
        out_specs=vmem,
        out_shape=jax.ShapeDtypeStruct((2 * batch, 8, dim), F32),
        scratch_shapes=[
            pltpu.VMEM((2, 6, dim, width), BF16),
            pltpu.VMEM((n_dev, 4 * batch, width), BF16),
            pltpu.VMEM((n_dev, 8 * batch, width), BF16),
            pltpu.SemaphoreType.DMA((2, 6)),
            pltpu.SemaphoreType.DMA((2, n_dev)),
            pltpu.SemaphoreType.DMA((2, n_dev)),
        ],
        compiler_params=pltpu.CompilerParams(collective_id=1, has_side_effects=True, vmem_limit_bytes=VMEM_BYTES),
        cost_estimate=pl.CostEstimate(flops=2 * batch * dim * 12 * width, bytes_accessed=24 * dim * width, transcendentals=0),
        name="mods",
    )(vec, bt, bi, pt[None, :], pi[None, :], ft[None, :], fi[None, :], wt, wi)

LOG2E = 1.4426950408889634
(W_FIRST, W_SECOND, W_RELAY, W_CORE, W_CORE_FIRST, W_CORE_SECOND, W_CORE_RELAY) = range(7)
(T_CORE, T_FIRST, T_SECOND, T_OUT_FIRST, T_OUT_SECOND, T_OUT_RELAY, T_CORE_OWN, T_CORE_FIRST, T_CORE_SECOND, T_CORE_RELAY) = range(10)
PIECES = 4
HEADS_HERE = 3


class Place:
    def __init__(self):
        me = lax.axis_index('tp')
        core = me % 2
        xi = (me // 2) % 2
        yi = me // 4
        x_next = me + 2 - 4 * xi
        y_next = me + 4 - 8 * yi
        self.me, self.core = me, core
        self.partner = me + 1 - 2 * core
        self.first = x_next * (1 - core) + y_next * core
        self.second = x_next * core + y_next * (1 - core)
        self.diagonal = x_next + y_next - me
        self.bit1 = xi * (1 - core) + yi * core
        self.bit2 = xi * core + yi * (1 - core)

    def enter(self):
        barrier = pltpu.get_barrier_semaphore()
        for dev in (self.partner, self.first, self.second):
            pl.semaphore_signal(barrier, inc=1, device_id={'tp': dev}, device_id_type=MESH)
        pl.semaphore_wait(barrier, 3)


def rows_at(start, size):
    return pl.ds(pl.multiple_of(start, size), size)


def front_kernel(cfg, txt_hbm, img_hbm, wt_hbm, wi_hbm, pw_hbm, tw_hbm, vec_ref, bias_ref, gain_ref, ids_ref, tab_ref,
                 o_hbm, wp_hbm, ut_hbm, x1_ref,
                 w, xs, ua, ub, qkv, s0, s1, s2, o_all, tw, t_send, t_recv, t_own, t_sum, t_rs1, t_rs2_out, t_rs2_in, t_keep, t_x, t_u,
                 wsem, xsem, osem, tsem, psend, precv, tsend, trecv):
    batch, txt_len, img_len, rows = cfg
    half, quarter, eighth = rows // 2, rows // 4, rows // 8
    total = txt_len + img_len
    per_img = img_len // rows
    blocks = batch * (per_img + 1)
    dim = w.shape[1]
    width = o_all.shape[1]
    heads = width // HEAD
    place = Place()
    me, core, partner, first, second, diagonal, bit1, bit2 = place.me, place.core, place.partner, place.first, place.second, place.diagonal, place.bit1, place.bit2
    piece = width // PIECES

    def position(n):
        n = jnp.int32(n)
        img = (n >= batch).astype(jnp.int32)
        m = n - batch
        b = (1 - img) * n + img * (m // per_img)
        r = img * (1 + m % per_img)
        return b, r * rows

    def x_copy(n, source):
        b, r0 = position(n)
        ref = txt_hbm.at[b] if source == 0 else img_hbm.at[b, rows_at(r0 - rows, rows), :]
        return pltpu.make_async_copy(ref, xs.at[n % 4], xsem.at[n % 4])

    def x_start(n):
        @pl.when(n < batch)
        def _():
            x_copy(n, 0).start()

        @pl.when((n >= batch) & (n < blocks))
        def _():
            x_copy(n, 1).start()

    def x_wait(n):
        @pl.when(n < blocks)
        def _():
            pltpu.make_async_copy(txt_hbm.at[0], xs.at[n % 4], xsem.at[n % 4]).wait()

    def w_load(path, j):
        return pltpu.make_async_copy((wt_hbm, wi_hbm)[path].at[j], w.at[path, :, j * width:(j + 1) * width], wsem.at[path, j])

    for path in range(2):
        for j in range(3):
            w_load(path, j).start()
            if path == 0 and j == 0:
                for n in range(3):
                    x_copy(n, 0 if n < batch else 1).start()
    tw_load = pltpu.make_async_copy(tw_hbm, tw, tsem.at[0])
    tw_load.start()
    place.enter()

    def piece_at(j):
        return rows_at(j * piece, piece)

    def remote(sends, recvs, kind, j, src, dst, dev):
        return pltpu.make_async_remote_copy(src_ref=src, dst_ref=dst, send_sem=sends.at[kind, j], recv_sem=recvs.at[kind, j], device_id={'tp': dev}, device_id_type=MESH)

    def p_copy(kind, j, owner, dev):
        dst = wp_hbm.at[owner, piece_at(j), :]
        src = pw_hbm.at[piece_at(j), :] if kind in (W_FIRST, W_SECOND, W_CORE) else dst
        return remote(psend, precv, kind, j, src, dst, dev)

    def w_relay(j):
        p_copy(W_FIRST, j, first, first).wait_recv()
        p_copy(W_RELAY, j, first, second).start()
        p_copy(W_CORE_FIRST, j, first, partner).start()

    def w_second(j):
        p_copy(W_SECOND, j, second, second).wait_recv()
        p_copy(W_CORE_SECOND, j, second, partner).start()

    def w_last(j):
        p_copy(W_RELAY, j, diagonal, second).wait_recv()
        p_copy(W_CORE_RELAY, j, diagonal, partner).start()

    for j in range(PIECES):
        p_copy(W_FIRST, j, me, first).start()
        p_copy(W_SECOND, j, me, second).start()
    for j in range(PIECES):
        p_copy(W_CORE, j, me, partner).start()

    even = lax.broadcasted_iota(jnp.int32, (rows, HEAD), 1) % 2 == 0
    code = lax.broadcasted_iota(jnp.int32, (N_IDS, rows), 0)

    def select(n):
        n = jnp.int32(n)
        img = (n >= batch).astype(jnp.int32)
        return (1 - img) * n + img * (batch + (n - batch) // per_img)

    def norm(n, u):
        u[...] = modulated(xs[n % 4].astype(F32), vec_ref, select(n), SHIFT1, SCALE1)

    def heads_of(n, u):
        b, r0 = position(n)
        path = (jnp.int32(n) >= batch).astype(jnp.int32)
        hot = jnp.concatenate([(ids_ref[b, axis:axis + 1, rows_at(r0, rows)] == code).astype(F32).astype(BF16) for axis in range(3)], axis=0)
        parts = lax.dot_general(hot, tab_ref[...], (((0,), (0,)), ((), ())), preferred_element_type=F32)
        cos_t, sin_t = (sum(parts[:, (3 * i + j) * HEAD:(3 * i + j + 1) * HEAD] for j in range(3)) for i in range(2))
        at = rows_at(b * total + r0, rows)
        for c0 in range(0, 3 * heads, 4):
            c1 = min(c0 + 4, 3 * heads)
            a = jnp.dot(u[...], w[path, :, c0 * HEAD:c1 * HEAD], preferred_element_type=F32) + bias_ref[path, 0:1, c0 * HEAD:c1 * HEAD]
            for c in range(c0, c1):
                t = a[:, (c - c0) * HEAD:(c - c0 + 1) * HEAD]
                kind = c // heads
                if kind < 2:
                    mean_sq = jnp.mean(t * t, axis=-1, keepdims=True)
                    t = t * lax.rsqrt(mean_sq + NORM_EPS) * gain_ref[path, kind:kind + 1, :]
                    swapped = jnp.where(even, pltpu.roll(t, HEAD - 1, 1), pltpu.roll(t, 1, 1))
                    t = t * cos_t + swapped * sin_t
                qkv[c, at, :] = t.astype(BF16)

    x_wait(0)
    norm(0, ua)
    for path in range(2):
        for j in range(3):
            w_load(path, j).wait()

    def qkv_step(t):
        x_start(2 * t + 3)
        x_start(2 * t + 4)
        x_wait(2 * t + 1)
        x_wait(2 * t + 2)
        for j, when in enumerate(QKV_RELAY):
            @pl.when(t == when)
            def _():
                w_relay(j)
        norm(2 * t + 1, ub)
        heads_of(2 * t, ua)
        norm(jnp.minimum(2 * t + 2, blocks - 1), ua)
        heads_of(2 * t + 1, ub)

    loop(blocks // 2, qkv_step)

    factor = HEAD ** -0.5 * LOG2E

    def scores(n, h, s):
        b, r0 = position(n)
        q = qkv[h, rows_at(b * total + r0, rows), :]
        k = qkv[heads + h, pl.ds(pl.multiple_of(b * total, rows), total), :]
        s[...] = lax.dot_general(q, k, (((1,), (1,)), ((), ())), preferred_element_type=F32)

    def weigh(n, h, s):
        b, r0 = position(n)
        v = qkv[2 * heads + h, pl.ds(pl.multiple_of(b * total, rows), total), :]
        top = jnp.max(s[...], axis=-1, keepdims=True)
        p = jnp.exp2((s[...] - top) * factor)
        denom = jnp.sum(p, axis=-1, keepdims=True)
        o = jnp.dot(p.astype(BF16), v, preferred_element_type=F32)
        o_all[rows_at(b * total + r0, rows), h * HEAD:(h + 1) * HEAD] = (o * (1.0 / denom)).astype(BF16)

    def t_copy(kind, src, dst, dev):
        return remote(tsend, trecv, kind, 0, src, dst, dev)

    def t_core():
        return t_copy(T_CORE, t_send, t_recv, partner)

    def t_first():
        return t_copy(T_FIRST, t_sum.at[:, rows_at((1 - bit1) * quarter, quarter), :], t_rs1, first)

    def t_second():
        return t_copy(T_SECOND, t_rs2_out, t_rs2_in, second)

    def own_rows(b1, b2):
        return rows_at(core * half + b1 * quarter + b2 * eighth, eighth)

    def t_out(kind, b1, b2, dev):
        ref = ut_hbm.at[:, own_rows(b1, b2), :]
        return t_copy(kind, t_u if kind in (T_OUT_FIRST, T_OUT_SECOND, T_CORE_OWN) else ref, ref, dev)

    def t_local():
        return pltpu.make_async_copy(t_u, ut_hbm.at[:, own_rows(bit1, bit2), :], tsem.at[1])

    def t_load(b):
        return pltpu.make_async_copy(txt_hbm.at[b, own_rows(bit1, bit2), :], t_x.at[b], tsem.at[2 + b])

    tile = min(512, dim)

    def text_partial():
        tw_load.wait()
        for b in range(batch):
            t_load(b).start()

            def theirs(n):
                at = rows_at(n * tile, tile)
                t_send[b, :, at] = jnp.dot(o_all[rows_at(b * total + (1 - core) * half, half), :], tw[:, at], preferred_element_type=F32).astype(BF16)

            loop(dim // tile, theirs)
        t_core().start()
        for b in range(batch):
            def mine(n):
                at = rows_at(n * tile, tile)
                t_own[b, :, at] = jnp.dot(o_all[rows_at(b * total + core * half, half), :], tw[:, at], preferred_element_type=F32)

            loop(dim // tile, mine)

    def text_sum():
        t_core().wait()
        for b in range(batch):
            def add(n):
                at = rows_at(n * 16, 16)
                t_sum[b, at, :] = (t_own[b, at, :] + t_recv[b, at, :].astype(F32)).astype(BF16)

            loop(half // 16, add)
        t_first().start()

    def text_quarter():
        t_first().wait()
        for b in range(batch):
            t_rs2_out[b] = (t_sum[b, rows_at(bit1 * quarter + (1 - bit2) * eighth, eighth), :].astype(F32) + t_rs1[b, rows_at((1 - bit2) * eighth, eighth), :].astype(F32)).astype(BF16)
            t_keep[b] = t_sum[b, rows_at(bit1 * quarter + bit2 * eighth, eighth), :].astype(F32) + t_rs1[b, rows_at(bit2 * eighth, eighth), :].astype(F32)
        t_second().start()

    def text_finish():
        t_second().wait()
        for b in range(batch):
            t_load(b).wait()
            branch = t_keep[b] + t_rs2_in[b].astype(F32) + row_of(vec_ref, b, PROJ_B)
            x1 = (t_x[b].astype(F32) + row_of(vec_ref, b, GATE1) * branch).astype(BF16)
            x1_ref[b] = x1
            t_u[b] = modulated(x1.astype(F32), vec_ref, b, SHIFT2, SCALE2)
        t_out(T_OUT_FIRST, bit1, bit2, first).start()
        t_out(T_OUT_SECOND, bit1, bit2, second).start()
        t_out(T_CORE_OWN, bit1, bit2, partner).start()
        t_local().start()

    def text_relay():
        t_out(T_OUT_FIRST, 1 - bit1, bit2, first).wait_recv()
        t_out(T_OUT_RELAY, 1 - bit1, bit2, second).start()
        t_out(T_CORE_FIRST, 1 - bit1, bit2, partner).start()
        t_out(T_OUT_SECOND, bit1, 1 - bit2, second).wait_recv()
        t_out(T_CORE_SECOND, bit1, 1 - bit2, partner).start()

    def text_last():
        t_out(T_OUT_RELAY, 1 - bit1, 1 - bit2, second).wait_recv()
        t_out(T_CORE_RELAY, 1 - bit1, 1 - bit2, partner).start()

    hooks = {
        1: [functools.partial(w_relay, 2)],
        2: [text_partial],
        3: [text_sum, functools.partial(w_relay, 3)],
        6: [text_quarter, functools.partial(w_second, 0), functools.partial(w_second, 1)],
        8: [text_finish, functools.partial(w_second, 2), functools.partial(w_second, 3)],
        11: [text_relay, functools.partial(w_last, 0)],
        14: [text_last, functools.partial(w_last, 1)],
        15: [functools.partial(w_last, 2)],
    }

    def o_store(n):
        b, r0 = position(n)
        return pltpu.make_async_copy(o_all.at[rows_at(b * total + r0, rows), :], o_hbm.at[b, rows_at(r0, rows), :], osem.at[n % 4])

    scores(0, 0, s0)

    def attention_step(n):
        for when, calls in hooks.items():
            @pl.when(n == min(when, blocks - 1))
            def _():
                for call in calls:
                    call()

        @pl.when(n >= 4)
        def _():
            o_store(n - 4).wait()

        scores(n, 1, s1)
        weigh(n, 0, s0)
        scores(n, 2, s2)
        weigh(n, 1, s1)
        scores(jnp.minimum(n + 1, blocks - 1), 0, s0)
        weigh(n, 2, s2)
        o_store(n).start()

    loop(blocks, attention_step)

    w_last(3)
    for n in range(blocks - 4, blocks):
        o_store(n).wait()
    t_local().wait()
    for kind, b1, b2, dev in ((T_OUT_FIRST, bit1, bit2, first), (T_OUT_SECOND, bit1, bit2, second), (T_OUT_RELAY, 1 - bit1, bit2, second)):
        t_out(kind, b1, b2, dev).wait_send()
    for kind, b1, b2 in ((T_CORE_OWN, bit1, bit2), (T_CORE_FIRST, 1 - bit1, bit2), (T_CORE_SECOND, bit1, 1 - bit2), (T_CORE_RELAY, 1 - bit1, 1 - bit2)):
        t_out(kind, b1, b2, partner).wait()
    for j in range(PIECES):
        for kind, owner, dev in ((W_FIRST, me, first), (W_SECOND, me, second), (W_RELAY, first, second)):
            p_copy(kind, j, owner, dev).wait_send()
        for kind, owner in ((W_CORE, me), (W_CORE_FIRST, first), (W_CORE_SECOND, second), (W_CORE_RELAY, diagonal)):
            p_copy(kind, j, owner, partner).wait()


QKV_RELAY = (4, 7)


def front_call(txt, img, wt, wi, pw, tw, vecs, bias, gains, ids_t, table, n_dev, rows):
    batch, txt_len, dim = txt.shape
    img_len = img.shape[1]
    total = txt_len + img_len
    width = pw.shape[0]
    heads = width // HEAD
    half, quarter, eighth = rows // 2, rows // 4, rows // 8
    assert heads == HEADS_HERE or heads == 1
    cfg = (batch, txt_len, img_len, rows)
    vmem = pl.BlockSpec(memory_space=pltpu.VMEM)
    anywhere = pl.BlockSpec(memory_space=pl.ANY)
    flops = 2 * batch * total * dim * 3 * width + 8 * batch * heads * total * total * HEAD
    return pl.pallas_call(
        functools.partial(front_kernel, cfg),
        in_specs=[anywhere] * 6 + [vmem] * 5,
        out_specs=[anywhere, anywhere, anywhere, vmem],
        out_shape=[
            jax.ShapeDtypeStruct((batch, total, width), BF16),
            jax.ShapeDtypeStruct((n_dev, width, dim), BF16),
            jax.ShapeDtypeStruct((batch, txt_len, dim), BF16),
            jax.ShapeDtypeStruct((batch, eighth, dim), BF16),
        ],
        scratch_shapes=[
            pltpu.VMEM((2, dim, 3 * width), BF16),
            pltpu.VMEM((4, rows, dim), BF16),
            pltpu.VMEM((rows, dim), BF16),
            pltpu.VMEM((rows, dim), BF16),
            pltpu.VMEM((3 * heads, batch * total, HEAD), BF16),
            pltpu.VMEM((rows, total), F32),
            pltpu.VMEM((rows, total), F32),
            pltpu.VMEM((rows, total), F32),
            pltpu.VMEM((batch * total, width), BF16),
            pltpu.VMEM((width, dim), BF16),
            pltpu.VMEM((batch, half, dim), BF16),
            pltpu.VMEM((batch, half, dim), BF16),
            pltpu.VMEM((batch, half, dim), F32),
            pltpu.VMEM((batch, half, dim), BF16),
            pltpu.VMEM((batch, quarter, dim), BF16),
            pltpu.VMEM((batch, eighth, dim), BF16),
            pltpu.VMEM((batch, eighth, dim), BF16),
            pltpu.VMEM((batch, eighth, dim), F32),
            pltpu.VMEM((batch, eighth, dim), BF16),
            pltpu.VMEM((batch, eighth, dim), BF16),
            pltpu.SemaphoreType.DMA((2, 3)),
            pltpu.SemaphoreType.DMA((4,)),
            pltpu.SemaphoreType.DMA((4,)),
            pltpu.SemaphoreType.DMA((4,)),
            pltpu.SemaphoreType.DMA((7, PIECES)),
            pltpu.SemaphoreType.DMA((7, PIECES)),
            pltpu.SemaphoreType.DMA((10, 1)),
            pltpu.SemaphoreType.DMA((10, 1)),
        ],
        compiler_params=pltpu.CompilerParams(collective_id=2, has_side_effects=True, vmem_limit_bytes=VMEM_BYTES),
        cost_estimate=pl.CostEstimate(flops=flops, bytes_accessed=2 * batch * total * (dim + width), transcendentals=batch * heads * total * total),
        name="front",
    )(txt, img, wt, wi, pw, tw, vecs, bias, gains, ids_t, table)


(O_CORE, O_FIRST, O_SECOND, O_RELAY, U_CORE, PART_CORE, RS_FIRST, RS_SECOND, OUT_FIRST, OUT_SECOND, OUT_RELAY, CORE_OWN, CORE_FIRST, CORE_SECOND, CORE_RELAY) = range(15)
(L_O, L_X, L_OUT) = range(3)
SLOTS = 4
SEMS = 8


def block_kernel(cfg, o_hbm, x_hbm, ut_hbm, x1t_hbm, wp_hbm, pw_hbm, w1t_hbm, w2t_hbm, w1i_hbm, w2i_hbm, vec_ref, fb_ref, out_hbm,
                 wp, w1, w2, obuf, xbuf, x1buf, x1keep, u2, hid, psend, precv, own, chip_sum, rs1, keep2, rs2_out, rs2_in, outb,
                 wsem, lsem, tsem, ssem, rsem):
    batch, txt_chunks, img_chunks, per_img, rows, tile = cfg
    half, quarter, eighth = rows // 2, rows // 4, rows // 8
    dim = wp.shape[0]
    ff = w1.shape[1]
    cols = o_hbm.shape[2]
    total = txt_chunks + img_chunks
    per_txt = txt_chunks // batch

    place = Place()
    me, core, partner, first, second, bit1, bit2 = place.me, place.core, place.partner, place.first, place.second, place.bit1, place.bit2
    txt_len = ut_hbm.shape[1]
    place.enter()

    def remote(kind, g, src, dst, dev):
        return pltpu.make_async_remote_copy(src_ref=src, dst_ref=dst, send_sem=ssem.at[kind, g % SEMS], recv_sem=rsem.at[kind, g % SEMS], device_id={'tp': dev}, device_id_type=MESH)

    def img_pos(g):
        k = g - txt_chunks
        return k // per_img, (k % per_img) * rows

    def chip_cols(dev):
        return rows_at((dev // 2) * (2 * cols), 2 * cols)

    def own_rows(b1, b2):
        return core * half + b1 * quarter + b2 * eighth

    def o_local(g):
        b, r0 = img_pos(g)
        return pltpu.make_async_copy(o_hbm.at[b, rows_at(txt_len + r0 + core * half, half), :], obuf.at[g % SLOTS, :, rows_at(me * cols, cols)], lsem.at[L_O, g % SEMS])

    def o_core(g):
        b, r0 = img_pos(g)
        return remote(O_CORE, g, o_hbm.at[b, rows_at(txt_len + r0 + (1 - core) * half, half), :], obuf.at[g % SLOTS, :, rows_at(me * cols, cols)], partner)

    def o_send(kind, g, owner, dev):
        ref = obuf.at[g % SLOTS, :, chip_cols(owner)]
        return remote(kind, g, ref, ref, dev)

    def x_load(g):
        b, r0 = img_pos(g)
        return pltpu.make_async_copy(x_hbm.at[b, rows_at(r0 + core * half, half), :], xbuf.at[g % 2], lsem.at[L_X, g % SEMS])

    def u_core(g):
        ref = u2.at[g % 2, rows_at(core * half, half), :]
        return remote(U_CORE, g, ref, ref, partner)

    def part_core(g):
        return remote(PART_CORE, g, psend, precv.at[g % 2], partner)

    def rs_first(g):
        return remote(RS_FIRST, g, chip_sum.at[rows_at((1 - bit1) * quarter, quarter), :], rs1.at[g % 2], first)

    def rs_second(g):
        return remote(RS_SECOND, g, rs2_out.at[g % 2], rs2_in.at[g % SLOTS], second)

    def out_ref(g, b1, b2):
        return out_hbm.at[rows_at(g * rows + own_rows(b1, b2), eighth), :]

    def out_send(kind, g, b1, b2, dev):
        ref = out_ref(g, b1, b2)
        mine = kind in (OUT_FIRST, OUT_SECOND, CORE_OWN)
        return remote(kind, g, outb.at[g % SLOTS] if mine else ref, ref, dev)

    def out_local(g):
        return pltpu.make_async_copy(outb.at[g % SLOTS], out_ref(g, bit1, bit2), lsem.at[L_OUT, g % SEMS])

    def txt_load(g):
        b, r0 = g // per_txt, (g % per_txt) * rows
        return (pltpu.make_async_copy(ut_hbm.at[b, rows_at(r0, rows), :], u2.at[g % 2], tsem.at[0, g % 2]),
                pltpu.make_async_copy(x1t_hbm.at[g], x1keep.at[g % SLOTS], tsem.at[1, g % 2]))

    def w_load(k, src, dst):
        return pltpu.make_async_copy(src, dst, wsem.at[k])

    def wp_load(j, src):
        return pltpu.make_async_copy(src, wp.at[j * cols:(j + 1) * cols, :], wsem.at[2 + j])

    def select(g):
        txt = (g < txt_chunks).astype(jnp.int32)
        return txt * (g // per_txt) + (1 - txt) * (batch + (g - txt_chunks) // per_img)

    def start_o(g):
        o_local(g).start()
        o_core(g).start()

    def send_o(g):
        o_local(g).wait()
        o_core(g).wait()
        o_send(O_FIRST, g, me, first).start()
        o_send(O_SECOND, g, me, second).start()

    def relay_o(g):
        o_send(O_FIRST, g, first, first).wait_recv()
        o_send(O_RELAY, g, first, second).start()
        x_load(g).start()

    def project(g):
        o_send(O_FIRST, g, me, first).wait_send()
        o_send(O_SECOND, g, me, second).wait_send()
        o_send(O_RELAY, g, first, second).wait_send()
        o_send(O_SECOND, g, second, second).wait_recv()
        o_send(O_RELAY, g, second, second).wait_recv()
        x_load(g).wait()

        @pl.when(g == txt_chunks)
        def _():
            for j in range(wp_hbm.shape[0]):
                wp_load(j, wp_hbm.at[j]).wait()

        sel = select(g)
        slot = g % SLOTS

        def columns(n):
            at = rows_at(n * tile, tile)
            acc = jnp.dot(obuf[slot], wp[:, at], preferred_element_type=F32)
            branch = acc + row_of(vec_ref, sel, PROJ_B, at)
            x1buf[:, at] = (xbuf[g % 2, :, at].astype(F32) + row_of(vec_ref, sel, GATE1, at) * branch).astype(BF16)

        loop(dim // tile, columns)

        def norm(n):
            at = rows_at(n * 16, 16)
            u2[g % 2, rows_at(core * half + n * 16, 16), :] = modulated(x1buf[at, :].astype(F32), vec_ref, sel, SHIFT2, SCALE2)

        loop(half // 16, norm)
        u_core(g).start()
        x1keep[slot] = x1buf[rows_at(bit1 * quarter + bit2 * eighth, eighth), :]

    def mlp(g):
        @pl.when(g < txt_chunks)
        def _():
            for copy in txt_load(g):
                copy.wait()

        @pl.when(g >= txt_chunks)
        def _():
            u_core(g).wait()

        @pl.when(g == 0)
        def _():
            w_load(0, w1t_hbm, w1).wait()
            w_load(1, w2t_hbm, w2).wait()

        @pl.when(g == txt_chunks)
        def _():
            w_load(0, w1i_hbm, w1).wait()
            w_load(1, w2i_hbm, w2).wait()

        path = (g >= txt_chunks).astype(jnp.int32)

        def hidden(n):
            at = rows_at(n * tile, tile)
            acc = jnp.dot(u2[g % 2], w1[:, at], preferred_element_type=F32)
            pre = acc + fb_ref[path, 0:1, at]
            hid[:, at] = jax.nn.gelu(pre, approximate=True).astype(BF16)

        loop(ff // tile, hidden)

        def theirs(n):
            at = rows_at(n * tile, tile)
            psend[:, at] = jnp.dot(hid[rows_at((1 - core) * half, half), :], w2[:, at], preferred_element_type=F32).astype(BF16)

        loop(dim // tile, theirs)
        part_core(g).start()

        def mine(n):
            at = rows_at(n * tile, tile)
            own[:, at] = jnp.dot(hid[rows_at(core * half, half), :], w2[:, at], preferred_element_type=F32)

        loop(dim // tile, mine)

        @pl.when(g == txt_chunks - 1)
        def _():
            w_load(0, w1i_hbm, w1).start()
            w_load(1, w2i_hbm, w2).start()

        part_core(g).wait()

        def add(n):
            at = rows_at(n * 16, 16)
            chip_sum[at, :] = (own[at, :] + precv[g % 2, at, :].astype(F32)).astype(BF16)

        loop(half // 16, add)
        rs_first(g).start()

    def add_first(g):
        rs_first(g).wait()
        rs2_out[g % 2] = (chip_sum[rows_at(bit1 * quarter + (1 - bit2) * eighth, eighth), :].astype(F32) + rs1[g % 2, rows_at((1 - bit2) * eighth, eighth), :].astype(F32)).astype(BF16)
        rs_second(g).start()
        keep2[g % 2] = chip_sum[rows_at(bit1 * quarter + bit2 * eighth, eighth), :].astype(F32) + rs1[g % 2, rows_at(bit2 * eighth, eighth), :].astype(F32)

    def finish(g):
        rs_second(g).wait()
        sel = select(g)
        branch = keep2[g % 2] + rs2_in[g % SLOTS].astype(F32) + row_of(vec_ref, sel, FC2_B)
        outb[g % SLOTS] = (x1keep[g % SLOTS].astype(F32) + row_of(vec_ref, sel, GATE2) * branch).astype(BF16)
        out_send(OUT_FIRST, g, bit1, bit2, first).start()
        out_send(OUT_SECOND, g, bit1, bit2, second).start()
        out_send(CORE_OWN, g, bit1, bit2, partner).start()
        out_local(g).start()

    def relay_out(g):
        out_send(OUT_FIRST, g, 1 - bit1, bit2, first).wait_recv()
        out_send(OUT_RELAY, g, 1 - bit1, bit2, second).start()
        out_send(CORE_FIRST, g, 1 - bit1, bit2, partner).start()
        out_send(OUT_SECOND, g, bit1, 1 - bit2, second).wait_recv()
        out_send(CORE_SECOND, g, bit1, 1 - bit2, partner).start()

    def relay_core(g):
        out_send(OUT_RELAY, g, 1 - bit1, 1 - bit2, second).wait_recv()
        out_send(CORE_RELAY, g, 1 - bit1, 1 - bit2, partner).start()

    def drain(g):
        out_local(g).wait()
        out_send(OUT_FIRST, g, bit1, bit2, first).wait_send()
        out_send(OUT_SECOND, g, bit1, bit2, second).wait_send()
        out_send(OUT_RELAY, g, 1 - bit1, bit2, second).wait_send()
        out_send(CORE_OWN, g, bit1, bit2, partner).wait()
        out_send(CORE_FIRST, g, 1 - bit1, bit2, partner).wait()
        out_send(CORE_SECOND, g, bit1, 1 - bit2, partner).wait()
        out_send(CORE_RELAY, g, 1 - bit1, 1 - bit2, partner).wait()

    w_load(0, w1t_hbm, w1).start()
    w_load(1, w2t_hbm, w2).start()
    for g in range(txt_chunks):
        for copy in txt_load(g):
            copy.start()
    for j in range(wp_hbm.shape[0]):
        @pl.when(j != me)
        def _():
            wp_load(j, wp_hbm.at[j]).start()

        @pl.when(j == me)
        def _():
            wp_load(j, pw_hbm).start()

    stages = ((start_o, 4, txt_chunks), (send_o, 3, txt_chunks), (relay_o, 2, txt_chunks), (relay_out, -3, 0), (relay_core, -4, 0), (drain, -5, 0),
              (project, 1, txt_chunks), (add_first, -1, 0), (finish, -2, 0), (mlp, 0, 0))
    lead = 4 - txt_chunks

    def step(i):
        for stage, ahead, lowest in stages:
            g = i - lead + ahead

            @pl.when((g >= lowest) & (g < total))
            def _():
                stage(g)

    loop(total + lead + 5, step)


def block_call(img_o, x, u_txt, x1_txt, wp, pw, w1t, w2t, w1i, w2i, vecs, fb, rows):
    batch, img_len, dim = x.shape
    txt_len = u_txt.shape[1]
    ff = w1t.shape[1]
    txt_chunks = batch * (txt_len // rows)
    per_img = img_len // rows
    img_chunks = batch * per_img
    assert txt_chunks == 2
    half, quarter, eighth = rows // 2, rows // 4, rows // 8
    cfg = (batch, txt_chunks, img_chunks, per_img, rows, 512)
    total = txt_chunks + img_chunks
    anywhere = pl.BlockSpec(memory_space=pl.ANY)
    flops = 2 * total * rows * 2 * dim * ff + 2 * img_chunks * half * dim * dim
    return pl.pallas_call(
        functools.partial(block_kernel, cfg),
        in_specs=[anywhere] * 10 + [pl.BlockSpec(memory_space=pltpu.VMEM)] * 2,
        out_specs=anywhere,
        out_shape=jax.ShapeDtypeStruct((total * rows, dim), BF16),
        scratch_shapes=[
            pltpu.VMEM((dim, dim), BF16),
            pltpu.VMEM((dim, ff), BF16),
            pltpu.VMEM((ff, dim), BF16),
            pltpu.VMEM((SLOTS, half, dim), BF16),
            pltpu.VMEM((2, half, dim), BF16),
            pltpu.VMEM((half, dim), BF16),
            pltpu.VMEM((SLOTS, eighth, dim), BF16),
            pltpu.VMEM((2, rows, dim), BF16),
            pltpu.VMEM((rows, ff), BF16),
            pltpu.VMEM((half, dim), BF16),
            pltpu.VMEM((2, half, dim), BF16),
            pltpu.VMEM((half, dim), F32),
            pltpu.VMEM((half, dim), BF16),
            pltpu.VMEM((2, quarter, dim), BF16),
            pltpu.VMEM((2, eighth, dim), F32),
            pltpu.VMEM((2, eighth, dim), BF16),
            pltpu.VMEM((SLOTS, eighth, dim), BF16),
            pltpu.VMEM((SLOTS, eighth, dim), BF16),
            pltpu.SemaphoreType.DMA((10,)),
            pltpu.SemaphoreType.DMA((3, SEMS)),
            pltpu.SemaphoreType.DMA((2, 2)),
            pltpu.SemaphoreType.DMA((15, SEMS)),
            pltpu.SemaphoreType.DMA((15, SEMS)),
        ],
        compiler_params=pltpu.CompilerParams(collective_id=0, has_side_effects=True, vmem_limit_bytes=VMEM_BYTES),
        cost_estimate=pl.CostEstimate(flops=flops, bytes_accessed=4 * dim * dim + 8 * dim * ff + 4 * total * rows * dim, transcendentals=0),
        name="block",
    )(img_o, x, u_txt, x1_txt, wp, pw, w1t, w2t, w1i, w2i, vecs, fb)


def copy_kernel(pieces, flat_hbm, *rest):
    outs, (buf, isem, osem) = rest[:-3], rest[-3:]
    rows = buf.shape[1]
    loads = []
    for n, (which, b, r) in enumerate(pieces):
        load = pltpu.make_async_copy(flat_hbm.at[n * rows:(n + 1) * rows, :], buf.at[n], isem.at[n])
        load.start()
        loads.append(load)
    stores = []
    for n, (which, b, r) in enumerate(pieces):
        loads[n].wait()
        store = pltpu.make_async_copy(buf.at[n], outs[which].at[b, r:r + rows, :], osem.at[n])
        store.start()
        stores.append(store)
    for store in stores:
        store.wait()


def copy_call(flat, shapes, rows):
    pieces = [(which, b, r) for which, shape in enumerate(shapes) for b in range(shape[0]) for r in range(0, shape[1], rows)]
    anywhere = pl.BlockSpec(memory_space=pl.ANY)
    dim = flat.shape[1]
    return pl.pallas_call(
        functools.partial(copy_kernel, pieces),
        in_specs=[anywhere],
        out_specs=[anywhere] * len(shapes),
        out_shape=[jax.ShapeDtypeStruct(shape, flat.dtype) for shape in shapes],
        scratch_shapes=[
            pltpu.VMEM((len(pieces), rows, dim), flat.dtype),
            pltpu.SemaphoreType.DMA((len(pieces),)),
            pltpu.SemaphoreType.DMA((len(pieces),)),
        ],
        compiler_params=pltpu.CompilerParams(vmem_limit_bytes=VMEM_BYTES),
        cost_estimate=pl.CostEstimate(flops=0, bytes_accessed=4 * flat.shape[0] * dim, transcendentals=0),
        name="copy_out",
    )(flat)


def local_block(img, txt, vec, ids, img_w, txt_w):
    n_dev = 8
    batch, txt_len = txt.shape[:2]
    rows = txt_len

    def by_kind(weight):
        return jnp.transpose(weight, (1, 0, 2))

    def both(pick):
        return jnp.stack([pick(txt_w), pick(img_w)]).astype(F32)

    vecs = mods_call(vec, by_kind(txt_w[0]), by_kind(img_w[0]), txt_w[1], img_w[1], txt_w[7], img_w[7], txt_w[11], img_w[11], n_dev)
    bias = both(lambda w: w[3].reshape(1, -1))
    gains = both(lambda w: jnp.stack([w[4], w[5]]))
    fb = both(lambda w: w[9][None, :])
    table = jnp.asarray(rope_table())
    ids_t = jnp.swapaxes(ids, 1, 2)
    o, proj_w, txt_u, txt_x1 = front_call(txt, img, by_kind(txt_w[2]), by_kind(img_w[2]), img_w[6], txt_w[6], vecs, bias, gains, ids_t, table, n_dev, rows)
    flat = block_call(o, img, txt_u, txt_x1, proj_w, img_w[6], txt_w[8], txt_w[10], img_w[8], img_w[10], vecs, fb, rows)
    txt_out, img_out = copy_call(flat, (txt.shape, img.shape), rows)
    return img_out, txt_out


def solution(mesh):
    act_spec = P('dp', WHOLE, WHOLE)
    mapped = jax.shard_map(local_block, mesh=mesh, in_specs=(act_spec, act_spec, P('dp', WHOLE), act_spec, PATH_SPECS, PATH_SPECS), out_specs=(act_spec, act_spec), check_vma=False)

    def forward(img, txt, vec, ids, *weights):
        return mapped(img, txt, vec, ids, weights[:12], weights[12:])

    return forward
```

time: 703 us -> 560 us (0.80)
  waiting for transfers between devices: 90.2 us -> 0 us
  local copies, waits for them, and re-layouts: 28.5 us -> 9.43 us
  Pallas kernels: 532 us -> 546 us
  matrix products: 13.6 us -> 0 us
  between operations: 14.3 us -> 0.84 us
  blocking collectives: 11 us -> 0 us
  other arithmetic: 12.9 us -> 2.51 us
    all_gather x1 -> x0, waiting for transfers between devices: 89.7 us -> none  [local_block(): proj_w = lax.all_gather(img_w[6], 'tp', axis=0, tiled=True)]
    slice x4 -> x0, local copies, waits for them, and re-layouts: 24.6 us -> none  [the longest x2 24.4 us: local_block(): return (flat[split:].reshape(img.shape), flat[:split].reshape(txt.shape))]
    pallas_call x4 -> x3, Pallas kernels: 150 us -> 165 us  [the longest x1 129 us: front_call(): pl.pallas_call(functools.partial(front_kernel, cfg), in_specs=[anywhere]...]
    dot_general x3 -> x0, matrix products: 13.6 us -> none  [the longest x2 9.05 us: modulation(): jnp.einsum('bd,dke->bke', silu_vec, weights[0], preferred_element_type=F32)]
    all_gather x1 -> x0, blocking collectives: 11 us -> none  [local_block(): full_mods = lax.all_gather(own_mods, 'tp', axis=3, tiled=True)]
  transfers between devices with their start and end apart: 2 -> 0, of which waited for: 1 -> 0; matrix products, arithmetic and copies ran while one was open for 1% -> 0% of each run, Pallas kernels for 10% -> 0%
where the time goes in v2:
time: 560 us; the launch traced here: 559 us
  Pallas kernels  546 us (98%)
  local copies, waits for them, and re-layouts  9.43 us (2%)
    pallas_call x1, Pallas kernels, block_call(): pl.pallas_call(functools.partial(block_kernel, cfg), in_specs=[anywhere]...  381 us
    pallas_call x1, Pallas kernels, front_call(): pl.pallas_call(functools.partial(front_kernel, cfg), in_specs=[anywhere]...  129 us
    pallas_call x1, Pallas kernels, copy_call(): pl.pallas_call(functools.partial(copy_kernel, pieces), in_specs=[anywhere...  19.3 us
    pallas_call x1, Pallas kernels, mods_call(): pl.pallas_call(mods_kernel, in_specs=[vmem] * 7 + [anywhere] * 2, out_spe...  17.4 us

profile of v2, /device:TPU:0, one launch (start us, length us, event | category | flops | bytes accessed | tf_op | source)
XLA Modules:
  0.0 559.2 jit_solution(7091344873181154490)
XLA Ops:
  0.6 0.7 maximum_bitcast_fusion
  1.3 0.6 maximum_convert_fusion.2.gain_ref
  1.9 0.7 stack.42
  2.6 0.7 stack.41
  3.3 0.6 maximum_convert_fusion.1.bias_ref
  3.9 0.7 stack.54
  4.6 0.7 stack.53
  5.3 0.6 maximum_convert_fusion.fb_ref
  5.9 1.3 broadcast_in_dim.13.pi_ref
  7.2 1.3 broadcast_in_dim.15.fi_ref
  8.5 1.3 broadcast_in_dim.12.pt_ref
  9.8 1.3 broadcast_in_dim.14.ft_ref
  11.1 1.5 copy.33
  12.6 17.4 %mods.1.vec_ref = f32[4,8,3072]{2,1,0:T(8,128)} custom-call(bf16[2,3072]{1,0:T(2,128)(2,1)} %vec_ref.1, bf16[6,384]{1,0:T(8,128)(2,1)} %bt_ref.1, bf16[6,384]{1,0:T(8,128)(2,1)} %bi_ref.1, bf16[1,3072]{1,0:T(2,128)(2,1)} %broadcast_in_dim.12.pt_ref, bf16[1,3072]{1,0:T(2,128)(2,1)} %broadcast_in_dim.13.pi_ref, bf16[1,3072]{1,0:T(2,128)(2,1)} %broadcast_in_dim.14.ft_ref, ...), custom_call_target="tpu_custom_call" | custom-call | flops 56623104 | bytes 28311552 | tf_op jit(solution)/shard_map/mods/pallas_call | solution.py:136
  30.0 128.8 %front.1 = (bf16[2,2304,384]{2,1,0:T(8,128)(2,1)}, bf16[8,384,3072]{2,1,0:T(8,128)(2,1)}, bf16[2,256,3072]{2,1,0:T(8,128)(2,1)}, bf16[2,32,3072]{2,1,0:T(8,128)(2,1)}) custom-call(bf16[2,256,3072]{2,1,0:T(8,128)(2,1)} %txt_hbm.1, bf16[2,2048,3072]{2,1,0:T(8,128)(2,1)} %x_hbm.1, bf16[3,3072,384]{2,1,0:T(8,128)(2,1)} %bitcast.22, ...), custom_call_target="tpu_custom_call" | custom-call | flops 65229815808 | bytes 31850496 | tf_op jit(solution)/shard_map/front/pallas_call | solution.py:498
  158.7 381.0 %block.1.flat_hbm = bf16[4608,3072]{1,0:T(8,128)(2,1)} custom-call(bf16[2,2304,384]{2,1,0:T(8,128)(2,1)} %get-tuple-element.8.o_hbm, bf16[2,2048,3072]{2,1,0:T(8,128)(2,1)} %x_hbm.1, bf16[2,256,3072]{2,1,0:T(8,128)(2,1)} %get-tuple-element.9.ut_hbm, bf16[2,32,3072]{2,1,0:T(8,128)(2,1)} %get-tuple-element.10.x1t_hbm, ...), custom_call_target="tpu_custom_call" | custom-call | flops 125627793408 | bytes 132120576 | tf_op jit(solution)/shard_map/block/pallas_call | solution.py:817
  539.8 19.3 %copy_out.1 = (bf16[2,256,3072]{2,1,0:T(8,128)(2,1)}, bf16[2,2048,3072]{2,1,0:T(8,128)(2,1)}) custom-call(bf16[4608,3072]{1,0:T(8,128)(2,1)} %block.1.flat_hbm), custom_call_target="tpu_custom_call" | custom-call | bytes 56623104 | tf_op jit(solution)/shard_map/copy_out/pallas_call | solution.py:875

commit v3 on v2

--- a/solution.py
+++ b/solution.py
@@ -48,6 +48,7 @@
 
 
 SHIFT1, SCALE1, GATE1, SHIFT2, SCALE2, GATE2, PROJ_B, FC2_B = range(8)
+QKV_B, Q_GAIN, K_GAIN, FC1_B = range(4)
 VMEM_BYTES = 67043328
 
 
@@ -69,10 +70,10 @@
     return ((1.0 + row_of(vec_ref, sel, scale)) * normalize(x) + row_of(vec_ref, sel, shift)).astype(BF16)
 
 
-def mods_kernel(vec_ref, bt_ref, bi_ref, pt_ref, pi_ref, ft_ref, fi_ref, wt_hbm, wi_hbm, out_ref, wbuf, early, late, wsem, ssem, rsem):
+def mods_kernel(vec_ref, small_t, small_i, wt_hbm, wi_hbm, vecs_ref, small_ref, wbuf, early, late, wsem, ssem, rsem):
     me = lax.axis_index('tp')
-    batch, dim = vec_ref.shape
-    width = wbuf.shape[3]
+    batch = vec_ref.shape[0]
+    width = wbuf.shape[-1]
     n_dev = early.shape[0]
     barrier = pltpu.get_barrier_semaphore()
     for d in range(1, n_dev):
@@ -86,12 +87,22 @@
             load(path, k).start()
     v = vec_ref[...].astype(F32)
     silu = (v * (1.0 / (1.0 + jnp.exp(-v)))).astype(BF16)
+    for path, (mod_b, qkv_b, q_gain, k_gain, proj_b, fc1_b, fc2_b) in enumerate((small_t, small_i)):
+        for row, ref in ((PROJ_B, proj_b), (FC2_B, fc2_b)):
+            vector = ref[...].astype(F32)[None, :]
+            for b in range(batch):
+                vecs_ref[path * batch + b, row:row + 1, :] = vector
+        for row, ref in ((Q_GAIN, q_gain), (K_GAIN, k_gain), (FC1_B, fc1_b)):
+            vector = ref[...].astype(F32)[None, :]
+            small_ref[path, row:row + 1, :vector.shape[1]] = vector
+        for j in range(qkv_b.shape[0]):
+            small_ref[path, QKV_B:Q_GAIN, j * width:(j + 1) * width] = qkv_b[j:j + 1, :].astype(F32)
     pl.semaphore_wait(barrier, n_dev - 1)
 
     def compute(k, path):
         load(path, k).wait()
         acc = jnp.dot(silu, wbuf[path, k], preferred_element_type=F32)
-        return (acc + (bt_ref, bi_ref)[path][k:k + 1, :].astype(F32)).astype(BF16)
+        return (acc + (small_t, small_i)[path][0][k:k + 1, :].astype(F32)).astype(BF16)
 
     def send(part, buf, d):
         return pltpu.make_async_remote_copy(src_ref=buf.at[me], dst_ref=buf.at[me], send_sem=ssem.at[part, d], recv_sem=rsem.at[part, d], device_id={'tp': (me + d) % n_dev}, device_id_type=MESH)
@@ -100,56 +111,47 @@
         ref = buf.at[(me + n_dev - d) % n_dev]
         return pltpu.make_async_remote_copy(src_ref=ref, dst_ref=ref, send_sem=ssem.at[part, d], recv_sem=rsem.at[part, d], device_id={'tp': (me + d) % n_dev}, device_id_type=MESH)
 
-    early_kinds, late_kinds = (SHIFT1, SCALE1), (GATE1, SHIFT2, SCALE2, GATE2)
-    early[me] = jnp.concatenate([compute(k, path) for k in early_kinds for path in range(2)], axis=0)
-    for d in range(1, n_dev):
-        send(0, early, d).start()
-    late[me] = jnp.concatenate([compute(k, path) for k in late_kinds for path in range(2)], axis=0)
-    for d in range(1, n_dev):
-        send(1, late, d).start()
-
-    def row(ref):
-        return ref[...].astype(F32)
-
-    for path, (pb, fb) in enumerate(((pt_ref, ft_ref), (pi_ref, fi_ref))):
-        for b in range(batch):
-            out_ref[path * batch + b, PROJ_B:FC2_B, :] = row(pb)
-            out_ref[path * batch + b, FC2_B:, :] = row(fb)
-    for part, buf, ks in ((0, early, early_kinds), (1, late, late_kinds)):
+    parts = ((early, (SHIFT1, SCALE1)), (late, (GATE1, SHIFT2, SCALE2, GATE2)))
+    for part, (buf, kinds) in enumerate(parts):
+        buf[me] = jnp.concatenate([compute(k, path) for k in kinds for path in range(2)], axis=0)
+        for d in range(1, n_dev):
+            send(part, buf, d).start()
+    for part, (buf, kinds) in enumerate(parts):
         for d in range(1, n_dev):
             send(part, buf, d).wait_send()
             receive(part, buf, d).wait_recv()
         for j in range(n_dev):
-            for n, k in enumerate(ks):
+            for n, k in enumerate(kinds):
                 for path in range(2):
                     at = (n * 2 + path) * batch
                     block = buf[j, at:at + batch, :].astype(F32)
                     for b in range(batch):
-                        out_ref[path * batch + b, k:k + 1, j * width:(j + 1) * width] = block[b:b + 1, :]
-
-
-def mods_call(vec, wt, wi, bt, bi, pt, pi, ft, fi, n_dev):
+                        vecs_ref[path * batch + b, k:k + 1, j * width:(j + 1) * width] = block[b:b + 1, :]
+
+
+def mods_call(vec, small_t, small_i, wt, wi, n_dev):
     batch, dim = vec.shape
-    width = wt.shape[2]
+    width = wt.shape[-1]
     vmem = pl.BlockSpec(memory_space=pltpu.VMEM)
     anywhere = pl.BlockSpec(memory_space=pl.ANY)
     return pl.pallas_call(
         mods_kernel,
-        in_specs=[vmem] * 7 + [anywhere] * 2,
-        out_specs=vmem,
-        out_shape=jax.ShapeDtypeStruct((2 * batch, 8, dim), F32),
+        in_specs=[vmem, (vmem,) * len(small_t), (vmem,) * len(small_i), anywhere, anywhere],
+        out_specs=[vmem, vmem],
+        out_shape=[jax.ShapeDtypeStruct((2 * batch, FC2_B + 1, dim), F32), jax.ShapeDtypeStruct((2, FC1_B + 1, dim), F32)],
         scratch_shapes=[
-            pltpu.VMEM((2, 6, dim, width), BF16),
+            pltpu.VMEM((2, PROJ_B, dim, width), BF16),
             pltpu.VMEM((n_dev, 4 * batch, width), BF16),
             pltpu.VMEM((n_dev, 8 * batch, width), BF16),
-            pltpu.SemaphoreType.DMA((2, 6)),
+            pltpu.SemaphoreType.DMA((2, PROJ_B)),
             pltpu.SemaphoreType.DMA((2, n_dev)),
             pltpu.SemaphoreType.DMA((2, n_dev)),
         ],
         compiler_params=pltpu.CompilerParams(collective_id=1, has_side_effects=True, vmem_limit_bytes=VMEM_BYTES),
         cost_estimate=pl.CostEstimate(flops=2 * batch * dim * 12 * width, bytes_accessed=24 * dim * width, transcendentals=0),
         name="mods",
-    )(vec, bt, bi, pt[None, :], pi[None, :], ft[None, :], fi[None, :], wt, wi)
+    )(vec, small_t, small_i, wt, wi)
+
 
 LOG2E = 1.4426950408889634
 (W_FIRST, W_SECOND, W_RELAY, W_CORE, W_CORE_FIRST, W_CORE_SECOND, W_CORE_RELAY) = range(7)
@@ -185,7 +187,7 @@
     return pl.ds(pl.multiple_of(start, size), size)
 
 
-def front_kernel(cfg, txt_hbm, img_hbm, wt_hbm, wi_hbm, pw_hbm, tw_hbm, vec_ref, bias_ref, gain_ref, ids_ref, tab_ref,
+def front_kernel(cfg, txt_hbm, img_hbm, wt_hbm, wi_hbm, pw_hbm, tw_hbm, vec_ref, small_ref, ids_ref, tab_ref,
                  o_hbm, wp_hbm, ut_hbm, x1_ref,
                  w, xs, ua, ub, qkv, s0, s1, s2, o_all, tw, t_send, t_recv, t_own, t_sum, t_rs1, t_rs2_out, t_rs2_in, t_keep, t_x, t_u,
                  wsem, xsem, osem, tsem, psend, precv, tsend, trecv):
@@ -285,19 +287,19 @@
     def heads_of(n, u):
         b, r0 = position(n)
         path = (jnp.int32(n) >= batch).astype(jnp.int32)
-        hot = jnp.concatenate([(ids_ref[b, axis:axis + 1, rows_at(r0, rows)] == code).astype(F32).astype(BF16) for axis in range(3)], axis=0)
+        hot = jnp.concatenate([(ids_ref[axis, pl.ds(b, 1), rows_at(r0, rows)] == code).astype(F32).astype(BF16) for axis in range(3)], axis=0)
         parts = lax.dot_general(hot, tab_ref[...], (((0,), (0,)), ((), ())), preferred_element_type=F32)
         cos_t, sin_t = (sum(parts[:, (3 * i + j) * HEAD:(3 * i + j + 1) * HEAD] for j in range(3)) for i in range(2))
         at = rows_at(b * total + r0, rows)
         for c0 in range(0, 3 * heads, 4):
             c1 = min(c0 + 4, 3 * heads)
-            a = jnp.dot(u[...], w[path, :, c0 * HEAD:c1 * HEAD], preferred_element_type=F32) + bias_ref[path, 0:1, c0 * HEAD:c1 * HEAD]
+            a = jnp.dot(u[...], w[path, :, c0 * HEAD:c1 * HEAD], preferred_element_type=F32) + row_of(small_ref, path, QKV_B, slice(c0 * HEAD, c1 * HEAD))
             for c in range(c0, c1):
                 t = a[:, (c - c0) * HEAD:(c - c0 + 1) * HEAD]
                 kind = c // heads
                 if kind < 2:
                     mean_sq = jnp.mean(t * t, axis=-1, keepdims=True)
-                    t = t * lax.rsqrt(mean_sq + NORM_EPS) * gain_ref[path, kind:kind + 1, :]
+                    t = t * lax.rsqrt(mean_sq + NORM_EPS) * row_of(small_ref, path, Q_GAIN + kind, slice(HEAD))
                     swapped = jnp.where(even, pltpu.roll(t, HEAD - 1, 1), pltpu.roll(t, 1, 1))
                     t = t * cos_t + swapped * sin_t
                 qkv[c, at, :] = t.astype(BF16)
@@ -313,10 +315,6 @@
         x_start(2 * t + 4)
         x_wait(2 * t + 1)
         x_wait(2 * t + 2)
-        for j, when in enumerate(QKV_RELAY):
-            @pl.when(t == when)
-            def _():
-                w_relay(j)
         norm(2 * t + 1, ub)
         heads_of(2 * t, ua)
         norm(jnp.minimum(2 * t + 2, blocks - 1), ua)
@@ -428,14 +426,14 @@
         t_out(T_CORE_RELAY, 1 - bit1, 1 - bit2, partner).start()
 
     hooks = {
-        1: [functools.partial(w_relay, 2)],
+        0: [functools.partial(w_relay, j) for j in range(PIECES)],
         2: [text_partial],
-        3: [text_sum, functools.partial(w_relay, 3)],
-        6: [text_quarter, functools.partial(w_second, 0), functools.partial(w_second, 1)],
-        8: [text_finish, functools.partial(w_second, 2), functools.partial(w_second, 3)],
-        11: [text_relay, functools.partial(w_last, 0)],
-        14: [text_last, functools.partial(w_last, 1)],
-        15: [functools.partial(w_last, 2)],
+        3: [text_sum],
+        4: [functools.partial(w_second, j) for j in range(PIECES)],
+        10: [text_quarter],
+        12: [text_finish],
+        15: [text_relay, functools.partial(w_last, 0), functools.partial(w_last, 1)],
+        17: [text_last, functools.partial(w_last, 2)],
     }
 
     def o_store(n):
@@ -480,10 +478,7 @@
             p_copy(kind, j, owner, partner).wait()
 
 
-QKV_RELAY = (4, 7)
-
-
-def front_call(txt, img, wt, wi, pw, tw, vecs, bias, gains, ids_t, table, n_dev, rows):
+def front_call(txt, img, wt, wi, pw, tw, vecs, small, ids_t, table, n_dev, rows):
     batch, txt_len, dim = txt.shape
     img_len = img.shape[1]
     total = txt_len + img_len
@@ -497,7 +492,7 @@
     flops = 2 * batch * total * dim * 3 * width + 8 * batch * heads * total * total * HEAD
     return pl.pallas_call(
         functools.partial(front_kernel, cfg),
-        in_specs=[anywhere] * 6 + [vmem] * 5,
+        in_specs=[anywhere] * 6 + [vmem] * 4,
         out_specs=[anywhere, anywhere, anywhere, vmem],
         out_shape=[
             jax.ShapeDtypeStruct((batch, total, width), BF16),
@@ -538,12 +533,13 @@
         compiler_params=pltpu.CompilerParams(collective_id=2, has_side_effects=True, vmem_limit_bytes=VMEM_BYTES),
         cost_estimate=pl.CostEstimate(flops=flops, bytes_accessed=2 * batch * total * (dim + width), transcendentals=batch * heads * total * total),
         name="front",
-    )(txt, img, wt, wi, pw, tw, vecs, bias, gains, ids_t, table)
+    )(txt, img, wt, wi, pw, tw, vecs, small, ids_t, table)
 
 
 (O_CORE, O_FIRST, O_SECOND, O_RELAY, U_CORE, PART_CORE, RS_FIRST, RS_SECOND, OUT_FIRST, OUT_SECOND, OUT_RELAY, CORE_OWN, CORE_FIRST, CORE_SECOND, CORE_RELAY) = range(15)
 (L_O, L_X, L_OUT) = range(3)
 SLOTS = 4
+O_SLOTS = 6
 SEMS = 8
 
 
@@ -578,14 +574,14 @@
 
     def o_local(g):
         b, r0 = img_pos(g)
-        return pltpu.make_async_copy(o_hbm.at[b, rows_at(txt_len + r0 + core * half, half), :], obuf.at[g % SLOTS, :, rows_at(me * cols, cols)], lsem.at[L_O, g % SEMS])
+        return pltpu.make_async_copy(o_hbm.at[b, rows_at(txt_len + r0 + core * half, half), :], obuf.at[g % O_SLOTS, :, rows_at(me * cols, cols)], lsem.at[L_O, g % SEMS])
 
     def o_core(g):
         b, r0 = img_pos(g)
-        return remote(O_CORE, g, o_hbm.at[b, rows_at(txt_len + r0 + (1 - core) * half, half), :], obuf.at[g % SLOTS, :, rows_at(me * cols, cols)], partner)
+        return remote(O_CORE, g, o_hbm.at[b, rows_at(txt_len + r0 + (1 - core) * half, half), :], obuf.at[g % O_SLOTS, :, rows_at(me * cols, cols)], partner)
 
     def o_send(kind, g, owner, dev):
-        ref = obuf.at[g % SLOTS, :, chip_cols(owner)]
+        ref = obuf.at[g % O_SLOTS, :, chip_cols(owner)]
         return remote(kind, g, ref, ref, dev)
 
     def x_load(g):
@@ -664,7 +660,7 @@
 
         def columns(n):
             at = rows_at(n * tile, tile)
-            acc = jnp.dot(obuf[slot], wp[:, at], preferred_element_type=F32)
+            acc = jnp.dot(obuf[g % O_SLOTS], wp[:, at], preferred_element_type=F32)
             branch = acc + row_of(vec_ref, sel, PROJ_B, at)
             x1buf[:, at] = (xbuf[g % 2, :, at].astype(F32) + row_of(vec_ref, sel, GATE1, at) * branch).astype(BF16)
 
@@ -678,7 +674,7 @@
         u_core(g).start()
         x1keep[slot] = x1buf[rows_at(bit1 * quarter + bit2 * eighth, eighth), :]
 
-    def mlp(g):
+    def mlp_hidden(g):
         @pl.when(g < txt_chunks)
         def _():
             for copy in txt_load(g):
@@ -692,6 +688,14 @@
         def _():
             w_load(0, w1t_hbm, w1).wait()
             w_load(1, w2t_hbm, w2).wait()
+            for j in range(wp_hbm.shape[0]):
+                @pl.when(j != me)
+                def _():
+                    wp_load(j, wp_hbm.at[j]).start()
+
+                @pl.when(j == me)
+                def _():
+                    wp_load(j, pw_hbm).start()
 
         @pl.when(g == txt_chunks)
         def _():
@@ -703,11 +707,12 @@
         def hidden(n):
             at = rows_at(n * tile, tile)
             acc = jnp.dot(u2[g % 2], w1[:, at], preferred_element_type=F32)
-            pre = acc + fb_ref[path, 0:1, at]
+            pre = acc + row_of(fb_ref, path, FC1_B, at)
             hid[:, at] = jax.nn.gelu(pre, approximate=True).astype(BF16)
 
         loop(ff // tile, hidden)
 
+    def mlp_theirs(g):
         def theirs(n):
             at = rows_at(n * tile, tile)
             psend[:, at] = jnp.dot(hid[rows_at((1 - core) * half, half), :], w2[:, at], preferred_element_type=F32).astype(BF16)
@@ -715,6 +720,7 @@
         loop(dim // tile, theirs)
         part_core(g).start()
 
+    def mlp_mine(g):
         def mine(n):
             at = rows_at(n * tile, tile)
             own[:, at] = jnp.dot(hid[rows_at(core * half, half), :], w2[:, at], preferred_element_type=F32)
@@ -755,6 +761,8 @@
         out_send(OUT_FIRST, g, 1 - bit1, bit2, first).wait_recv()
         out_send(OUT_RELAY, g, 1 - bit1, bit2, second).start()
         out_send(CORE_FIRST, g, 1 - bit1, bit2, partner).start()
+
+    def second_out(g):
         out_send(OUT_SECOND, g, bit1, 1 - bit2, second).wait_recv()
         out_send(CORE_SECOND, g, bit1, 1 - bit2, partner).start()
 
@@ -777,28 +785,21 @@
     for g in range(txt_chunks):
         for copy in txt_load(g):
             copy.start()
-    for j in range(wp_hbm.shape[0]):
-        @pl.when(j != me)
-        def _():
-            wp_load(j, wp_hbm.at[j]).start()
-
-        @pl.when(j == me)
-        def _():
-            wp_load(j, pw_hbm).start()
-
-    stages = ((start_o, 4, txt_chunks), (send_o, 3, txt_chunks), (relay_o, 2, txt_chunks), (relay_out, -3, 0), (relay_core, -4, 0), (drain, -5, 0),
-              (project, 1, txt_chunks), (add_first, -1, 0), (finish, -2, 0), (mlp, 0, 0))
-    lead = 4 - txt_chunks
+
+    stages = ((mlp_hidden, 0, 0), (relay_o, 2, 1), (finish, -3, 0), (start_o, 5, 1), (relay_out, -4, 0), (mlp_theirs, 0, 0), (second_out, -5, 0),
+              (send_o, 5, 1), (relay_core, -6, 0), (project, 1, 1), (add_first, -1, 0), (mlp_mine, 0, 0), (drain, -6, 0))
+    most = max(ahead for _, ahead, _ in stages)
+    least = min(ahead for _, ahead, _ in stages)
 
     def step(i):
-        for stage, ahead, lowest in stages:
-            g = i - lead + ahead
-
-            @pl.when((g >= lowest) & (g < total))
+        for stage, ahead, img_only in stages:
+            g = i + txt_chunks - most + ahead
+
+            @pl.when((g >= img_only * txt_chunks) & (g < total))
             def _():
                 stage(g)
 
-    loop(total + lead + 5, step)
+    loop(total - txt_chunks + most - least, step)
 
 
 def block_call(img_o, x, u_txt, x1_txt, wp, pw, w1t, w2t, w1i, w2i, vecs, fb, rows):
@@ -823,7 +824,7 @@
             pltpu.VMEM((dim, dim), BF16),
             pltpu.VMEM((dim, ff), BF16),
             pltpu.VMEM((ff, dim), BF16),
-            pltpu.VMEM((SLOTS, half, dim), BF16),
+            pltpu.VMEM((O_SLOTS, half, dim), BF16),
             pltpu.VMEM((2, half, dim), BF16),
             pltpu.VMEM((half, dim), BF16),
             pltpu.VMEM((SLOTS, eighth, dim), BF16),
@@ -896,17 +897,14 @@
     def by_kind(weight):
         return jnp.transpose(weight, (1, 0, 2))
 
-    def both(pick):
-        return jnp.stack([pick(txt_w), pick(img_w)]).astype(F32)
-
-    vecs = mods_call(vec, by_kind(txt_w[0]), by_kind(img_w[0]), txt_w[1], img_w[1], txt_w[7], img_w[7], txt_w[11], img_w[11], n_dev)
-    bias = both(lambda w: w[3].reshape(1, -1))
-    gains = both(lambda w: jnp.stack([w[4], w[5]]))
-    fb = both(lambda w: w[9][None, :])
+    def small_of(w):
+        return w[1], w[3], w[4], w[5], w[7], w[9], w[11]
+
+    vecs, small = mods_call(vec, small_of(txt_w), small_of(img_w), by_kind(txt_w[0]), by_kind(img_w[0]), n_dev)
     table = jnp.asarray(rope_table())
-    ids_t = jnp.swapaxes(ids, 1, 2)
-    o, proj_w, txt_u, txt_x1 = front_call(txt, img, by_kind(txt_w[2]), by_kind(img_w[2]), img_w[6], txt_w[6], vecs, bias, gains, ids_t, table, n_dev, rows)
-    flat = block_call(o, img, txt_u, txt_x1, proj_w, img_w[6], txt_w[8], txt_w[10], img_w[8], img_w[10], vecs, fb, rows)
+    ids_t = jnp.transpose(ids, (2, 0, 1))
+    o, proj_w, txt_u, txt_x1 = front_call(txt, img, by_kind(txt_w[2]), by_kind(img_w[2]), img_w[6], txt_w[6], vecs, small, ids_t, table, n_dev, rows)
+    flat = block_call(o, img, txt_u, txt_x1, proj_w, img_w[6], txt_w[8], txt_w[10], img_w[8], img_w[10], vecs, small, rows)
     txt_out, img_out = copy_call(flat, (txt.shape, img.shape), rows)
     return img_out, txt_out
 

time: 560 us -> 511 us (0.912)
  Pallas kernels: 546 us -> 510 us
  local copies, waits for them, and re-layouts: 9.43 us -> 0 us
    pallas_call x1, Pallas kernels: 381 us -> 350 us  [block_call(): pl.pallas_call(functools.partial(block_kernel, cfg), in_specs=[anywhere]...]
    pallas_call x1, Pallas kernels: 129 us -> 123 us  [front_call(): pl.pallas_call(functools.partial(front_kernel, cfg), in_specs=[anywhere]...]
where the time goes in v3:
time: 511 us; the launch traced here: 510 us
  Pallas kernels  510 us (100%)
    pallas_call x1, Pallas kernels, block_call(): pl.pallas_call(functools.partial(block_kernel, cfg), in_specs=[anywhere]...  350 us
    pallas_call x1, Pallas kernels, front_call(): pl.pallas_call(functools.partial(front_kernel, cfg), in_specs=[anywhere]...  123 us
    pallas_call x1, Pallas kernels, copy_call(): pl.pallas_call(functools.partial(copy_kernel, pieces), in_specs=[anywhere...  19.3 us
    pallas_call x1, Pallas kernels, mods_call(): pl.pallas_call(mods_kernel, in_specs=[vmem, (vmem,) * len(small_t), (vmem...  17.4 us

profile of v3, /device:TPU:0, one launch (start us, length us, event | category | flops | bytes accessed | tf_op | source)
XLA Modules:
  0.0 510.4 jit_solution(2837345363152865264)
XLA Ops:
  0.6 17.4 %mods.1 = (f32[4,8,3072]{2,1,0:T(8,128)}, f32[2,4,3072]{2,1,0:T(4,128)}) custom-call(bf16[2,3072]{1,0:T(2,128)(2,1)} %vec_ref.1, bf16[6,384]{1,0:T(8,128)(2,1)} %small_t_0_.1, bf16[3,384]{1,0:T(4,128)(2,1)} %small_t_1_.1, bf16[128]{0:T(256)(128)(2,1)} %small_t_2_.1, bf16[128]{0:T(256)(128)(2,1)} %small_t_3_.1, bf16[3072]{0:T(1024)(128)(2,1)} %small_t_4_.1, ...), custom_call_target="tpu_custom_call" | custom-call | flops 56623104 | bytes 28311552 | tf_op jit(solution)/shard_map/mods/pallas_call | solution.py:137
  18.1 122.8 %front.1 = (bf16[2,2304,384]{2,1,0:T(8,128)(2,1)}, bf16[8,384,3072]{2,1,0:T(8,128)(2,1)}, bf16[2,256,3072]{2,1,0:T(8,128)(2,1)}, bf16[2,32,3072]{2,1,0:T(8,128)(2,1)}) custom-call(bf16[2,256,3072]{2,1,0:T(8,128)(2,1)} %txt_hbm.1, bf16[2,2048,3072]{2,1,0:T(8,128)(2,1)} %x_hbm.1, bf16[3,3072,384]{2,1,0:T(8,128)(2,1)} %bitcast.7, ...), custom_call_target="tpu_custom_call" | custom-call | flops 65229815808 | bytes 31850496 | tf_op jit(solution)/shard_map/front/pallas_call | solution.py:493
  140.9 350.1 %block.1.flat_hbm = bf16[4608,3072]{1,0:T(8,128)(2,1)} custom-call(bf16[2,2304,384]{2,1,0:T(8,128)(2,1)} %get-tuple-element.12.o_hbm, bf16[2,2048,3072]{2,1,0:T(8,128)(2,1)} %x_hbm.1, bf16[2,256,3072]{2,1,0:T(8,128)(2,1)} %get-tuple-element.13.ut_hbm, bf16[2,32,3072]{2,1,0:T(8,128)(2,1)} %get-tuple-element.14.x1t_hbm, ...), custom_call_target="tpu_custom_call" | custom-call | flops 125627793408 | bytes 132120576 | tf_op jit(solution)/shard_map/block/pallas_call | solution.py:818
  491.0 19.3 %copy_out.1 = (bf16[2,256,3072]{2,1,0:T(8,128)(2,1)}, bf16[2,2048,3072]{2,1,0:T(8,128)(2,1)}) custom-call(bf16[4608,3072]{1,0:T(8,128)(2,1)} %block.1.flat_hbm), custom_call_target="tpu_custom_call" | custom-call | bytes 56623104 | tf_op jit(solution)/shard_map/copy_out/pallas_call | solution.py:876

commit v4 on v3

v4 whole, which is shorter than its diff:
```python
import functools

import jax
import jax.numpy as jnp
import numpy as np
from jax import lax
from jax.experimental import pallas as pl
from jax.experimental.pallas import tpu as pltpu
from jax.sharding import PartitionSpec as P

HEAD = 128
NORM_EPS = 1e-6
ROPE_THETA = 10000.0
AXES_DIM = (16, 56, 56)
N_IDS = 64
WHOLE = None
PATH_SPECS = (P(WHOLE, WHOLE, 'tp'), P(WHOLE, 'tp'), P(WHOLE, WHOLE, 'tp'), P(WHOLE, 'tp'), P(WHOLE), P(WHOLE), P('tp', WHOLE), P(WHOLE), P(WHOLE, 'tp'), P('tp'), P('tp', WHOLE), P(WHOLE))
F32 = jnp.float32
BF16 = jnp.bfloat16


def rope_table():
    cos = np.zeros((3 * N_IDS, HEAD), np.float32)
    sin = np.zeros((3 * N_IDS, HEAD), np.float32)
    lane = 0
    for axis, dim in enumerate(AXES_DIM):
        inv_freq = np.float32(ROPE_THETA) ** (-np.arange(0, dim, 2, dtype=np.float32) / np.float32(dim))
        angles = np.arange(N_IDS, dtype=np.float32)[:, None] * inv_freq.astype(np.float32)
        rows = slice(axis * N_IDS, (axis + 1) * N_IDS)
        c = np.cos(angles.astype(np.float64)).astype(np.float32)
        s = np.sin(angles.astype(np.float64)).astype(np.float32)
        cos[rows, lane:lane + dim:2] = c
        cos[rows, lane + 1:lane + dim:2] = c
        sin[rows, lane:lane + dim:2] = -s
        sin[rows, lane + 1:lane + dim:2] = s
        lane += dim
    parts = []
    for table in (cos, sin):
        rest = table
        for _ in range(3):
            part = rest.astype(jnp.bfloat16)
            parts.append(np.asarray(part))
            rest = rest - np.asarray(part).astype(np.float32)
    return np.concatenate(parts, axis=1)


MESH = pl.DeviceIdType.MESH


SHIFT1, SCALE1, GATE1, SHIFT2, SCALE2, GATE2, PROJ_B, FC2_B = range(8)
QKV_B, Q_GAIN, K_GAIN, FC1_B = range(4)
VMEM_BYTES = 67043328


def row_of(ref, sel, row, at=slice(None)):
    return ref[sel, pl.ds(row, 1), at]


STRIP = 16
PATHS = range(2)


def loop(count, body):
    lax.fori_loop(0, count, lambda i, carry: (body(i), carry)[-1], 0)


def row_mean(x):
    return jnp.mean(x, axis=-1, keepdims=True)


def normalize(x):
    centered = x - row_mean(x)
    return centered * lax.rsqrt(row_mean(centered * centered) + NORM_EPS)


def weighted(s, v):
    top = jnp.max(s, axis=-1, keepdims=True)
    p = jnp.exp2((s - top) * (HEAD ** -0.5 * LOG2E))
    total = jnp.sum(p, axis=-1, keepdims=True)
    o = jnp.dot(p.astype(BF16), v, preferred_element_type=F32)
    return (o * (1.0 / total)).astype(BF16)


def scores_of(q, k):
    return lax.dot_general(q, k, (((1,), (1,)), ((), ())), preferred_element_type=F32)


def modulated(x, vec_ref, sel, shift, scale):
    return ((1.0 + row_of(vec_ref, sel, scale)) * normalize(x) + row_of(vec_ref, sel, shift)).astype(BF16)


LOG2E = 1.4426950408889634
(W_FIRST, W_SECOND, W_RELAY, W_CORE, W_CORE_FIRST, W_CORE_SECOND, W_CORE_RELAY, Z_FIRST, Z_SECOND, Z_RELAY) = range(10)
(G_CORE, G_FIRST, G_SECOND, G_RELAY) = range(4)
(T_CORE, T_FIRST, T_SECOND, T_OUT_FIRST, T_OUT_SECOND, T_OUT_RELAY, T_CORE_OWN, T_CORE_FIRST, T_CORE_SECOND, T_CORE_RELAY) = range(10)
SHARED, COMMON, MISSING = range(3)
PIECES = 3
READY = 3
EARLY = 2
HEADS_HERE = 3


def ident(dev):
    return dev if isinstance(dev, dict) else {'tp': dev}


class Place:
    def __init__(self):
        me = lax.axis_index('tp')
        core = me % 2
        xi = (me // 2) % 2
        yi = me // 4
        x_next = me + 2 - 4 * xi
        y_next = me + 4 - 8 * yi
        self.me, self.core = me, core
        self.partner = me + 1 - 2 * core
        self.first = x_next * (1 - core) + y_next * core
        self.second = x_next * core + y_next * (1 - core)
        self.diagonal = x_next + y_next - me
        self.bit1 = xi * (1 - core) + yi * core
        self.bit2 = xi * core + yi * (1 - core)
        self.not1, self.not2, self.far = 1 - self.bit1, 1 - self.bit2, 1 - core

    def enter(self, others):
        barrier = pltpu.get_barrier_semaphore()
        for dev in others:
            pl.semaphore_signal(barrier, inc=1, device_id=ident(dev), device_id_type=MESH)
        pl.semaphore_wait(barrier, len(others))


def rows_at(start, size):
    return pl.ds(pl.multiple_of(start, size), size)


def front_kernel(cfg, txt_hbm, img_hbm, wt_hbm, wi_hbm, mt_hbm, mi_hbm, pw_hbm, tw_hbm, cond_ref, small_t, small_i, ids_ref, tab_ref,
                 o_hbm, kv_hbm, wp_hbm, ut_hbm, og_hbm, x1_ref, vec_ref, small_ref,
                 w, m_w, m_b, m_early, m_late, xs, ua, ub, qkv, s0, s1, s2, o_all, tw, t_send, t_recv, t_own, t_sum, t_rs1, t_rs2_out, t_rs2_in, t_keep, t_x, t_u,
                 wsem, msem, xsem, osem, tsem, gsem, psend, precv, tsend, trecv, gsend, grecv, msend, mrecv):
    batch, txt_len, img_len, rows = cfg
    half, quarter, eighth = rows // 2, rows // 4, rows // 8
    total = txt_len + img_len
    per_img = img_len // rows
    blocks = batch * (per_img + 1)
    n_dev = m_early.shape[0]
    others = range(1, n_dev)
    dim = w.shape[1]
    width = o_all.shape[1]
    heads = width // HEAD
    place = Place()
    me, core, partner, first, second, diagonal, bit1, bit2 = place.me, place.core, place.partner, place.first, place.second, place.diagonal, place.bit1, place.bit2
    not1, not2, far = place.not1, place.not2, place.far
    piece = width // PIECES
    plane = lax.axis_index('dp')
    odd = plane % 2
    beside = {'dp': plane + 1 - 2 * odd}

    def position(n):
        n = jnp.int32(n)
        img = (n >= batch).astype(jnp.int32)
        m = n - batch
        b = (1 - img) * n + img * (m // per_img)
        r = img * (1 + m % per_img)
        return b, r * rows

    def x_copy(n, source):
        b, r0 = position(n)
        ref = txt_hbm.at[b] if source == 0 else img_hbm.at[b, rows_at(r0 - rows, rows), :]
        return pltpu.make_async_copy(ref, xs.at[n % 4], xsem.at[n % 4])

    def x_start(n):
        @pl.when(n < batch)
        def _():
            x_copy(n, 0).start()

        @pl.when((n >= batch) & (n < blocks))
        def _():
            x_copy(n, 1).start()

    def x_wait(n):
        @pl.when(n < blocks)
        def _():
            pltpu.make_async_copy(txt_hbm.at[0], xs.at[n % 4], xsem.at[n % 4]).wait()

    def w_columns(path, j):
        return w.at[path, :, j * width:(j + 1) * width]

    def w_load(path, j):
        return pltpu.make_async_copy((wt_hbm, wi_hbm)[path].at[j], w_columns(path, j), wsem.at[path, j])

    def early_load(path, k):
        return pltpu.make_async_copy((mt_hbm, mi_hbm)[path].at[k], w_columns(path, k), wsem.at[path, k])

    def late_load(c, path):
        return pltpu.make_async_copy((mt_hbm, mi_hbm)[path].at[GATE1 + c // 2], m_w.at[c % 2], msem.at[c % 2])

    def late_start(c):
        for path in PATHS:
            @pl.when(c % 2 == path)
            def _():
                late_load(c, path).start()

    def m_copy(part, d, send):
        buf = (m_early, m_late)[part]
        ref = buf.at[me if send else (me + n_dev - d) % n_dev, :8]
        return pltpu.make_async_remote_copy(src_ref=ref, dst_ref=ref, send_sem=msend.at[part, d], recv_sem=mrecv.at[part, d], device_id={'tp': (me + d) % n_dev}, device_id_type=MESH)

    def m_send(part):
        for d in others:
            m_copy(part, d, True).start()

    def m_wait(part):
        for d in others:
            m_copy(part, d, True).wait_send()
            m_copy(part, d, False).wait_recv()

    for k in (SHIFT1, SCALE1):
        for path in PATHS:
            early_load(path, k).start()
    for n in range(3):
        x_copy(n, 0 if n < batch else 1).start()
    v = cond_ref[...].astype(F32)
    silu = (v * (1.0 / (1.0 + jnp.exp(-v)))).astype(BF16)
    for path, (mod_b, qkv_b, q_gain, k_gain, proj_b, fc1_b, fc2_b) in enumerate((small_t, small_i)):
        m_b[path] = mod_b[...].astype(F32)
        for row, ref in ((PROJ_B, proj_b), (FC2_B, fc2_b)):
            vector = ref[...].astype(F32)[None, :]
            for b in range(batch):
                vec_ref[path * batch + b, row:row + 1, :] = vector
        for row, ref in ((Q_GAIN, q_gain), (K_GAIN, k_gain), (FC1_B, fc1_b)):
            vector = ref[...].astype(F32)[None, :]
            small_ref[path, row:row + 1, :vector.shape[1]] = vector
        for j in range(qkv_b.shape[0]):
            small_ref[path, QKV_B:Q_GAIN, j * width:(j + 1) * width] = qkv_b[j:j + 1, :].astype(F32)
    place.enter([(me + d) % n_dev for d in others] + [beside])

    def early_chunk(k, path):
        early_load(path, k).wait()
        acc = jnp.dot(silu, w_columns(path, k)[...], preferred_element_type=F32)
        return (acc + m_b[path, k:k + 1, :]).astype(BF16)

    m_early[me] = jnp.concatenate([early_chunk(k, path) for k in (SHIFT1, SCALE1) for path in PATHS], axis=0)
    m_send(0)
    for path in PATHS:
        for j in range(3):
            w_load(path, j).start()
    for c in range(2):
        late_load(c, c).start()
    tw_load = pltpu.make_async_copy(tw_hbm, tw, tsem.at[1])
    tw_load.start()

    def late_chunk(t):
        c = jnp.minimum(t, 7)
        path, k = c % 2, GATE1 + c // 2
        acc = jnp.dot(silu, m_w[c % 2], preferred_element_type=F32) + m_b[path, pl.ds(k, 1), :]
        m_late[me, t] = acc.astype(BF16).astype(F32)

    def late_rows():
        m_wait(1)
        for j in range(n_dev):
            for c in range(8):
                for b in range(batch):
                    vec_ref[c % 2 * batch + b, pl.ds(GATE1 + c // 2, 1), j * width:(j + 1) * width] = m_late[j, c, b:b + 1, :]

    def piece_at(j):
        return rows_at(((1 - j) * (2 * odd - 1) + 1) * piece, piece)

    def remote(sends, recvs, kind, j, src, dst, dev):
        return pltpu.make_async_remote_copy(src_ref=src, dst_ref=dst, send_sem=sends.at[kind, j], recv_sem=recvs.at[kind, j], device_id=ident(dev), device_id_type=MESH)

    def p_copy(kind, j, owner, dev):
        dst = wp_hbm.at[owner, piece_at(j), :]
        src = pw_hbm.at[piece_at(j), :] if kind in (W_FIRST, W_SECOND) else dst
        return remote(psend, precv, kind, j, src, dst, dev)

    def w_own():
        return remote(psend, precv, W_CORE, SHARED, pw_hbm, wp_hbm.at[me], partner)

    def z_copy(kind, owner, j=SHARED):
        ref = wp_hbm.at[owner, piece_at(j), :]
        return remote(psend, precv, kind, SHARED, ref, ref, beside)

    def w_relay(j):
        p_copy(W_FIRST, j, first, first).wait_recv()
        p_copy(W_RELAY, j, first, second).start()
        p_copy(W_CORE_FIRST, j, first, partner).start()
        if j == SHARED:
            p_copy(W_SECOND, COMMON, me, second).start()
            z_copy(Z_FIRST, first).start()

    def w_second(j):
        p_copy(W_SECOND, j, second, second).wait_recv()
        p_copy(W_CORE_SECOND, j, second, partner).start()
        if j == SHARED:
            z_copy(Z_SECOND, second).start()

    def w_last(j):
        p_copy(W_RELAY, j, diagonal, second).wait_recv()
        p_copy(W_CORE_RELAY, j, diagonal, partner).start()
        if j == SHARED:
            z_copy(Z_RELAY, diagonal).start()

    from_beside = ((Z_FIRST, first, W_CORE_FIRST), (Z_SECOND, second, W_CORE_SECOND), (Z_RELAY, diagonal, W_CORE_RELAY))

    def w_beside(n):
        kind, owner, core_kind = from_beside[n]
        z_copy(kind, owner, MISSING).wait_recv()
        p_copy(core_kind, MISSING, owner, partner).start()

    p_copy(W_FIRST, SHARED, me, first).start()
    p_copy(W_SECOND, SHARED, me, second).start()
    p_copy(W_FIRST, COMMON, me, first).start()
    w_own().start()

    even = lax.broadcasted_iota(jnp.int32, (rows, HEAD), 1) % 2 == 0
    code = lax.broadcasted_iota(jnp.int32, (N_IDS, rows), 0)

    def select(n):
        n = jnp.int32(n)
        img = (n >= batch).astype(jnp.int32)
        return (1 - img) * n + img * (batch + (n - batch) // per_img)

    def norm(n, u):
        u[...] = modulated(xs[n % 4].astype(F32), vec_ref, select(n), SHIFT1, SCALE1).reshape(u.shape)

    def heads_of(n, u):
        b, r0 = position(n)
        path = (jnp.int32(n) >= batch).astype(jnp.int32)
        hot = jnp.concatenate([(ids_ref[axis, pl.ds(b, 1), rows_at(r0, rows)] == code).astype(F32).astype(BF16) for axis in range(3)], axis=0)
        parts = lax.dot_general(hot, tab_ref[...], (((0,), (0,)), ((), ())), preferred_element_type=F32)
        cos_t, sin_t = (sum(parts[:, (3 * i + j) * HEAD:(3 * i + j + 1) * HEAD] for j in range(3)) for i in range(2))
        at = rows_at(b * total + r0, rows)
        for c0 in range(0, 3 * heads, 4):
            c1 = min(c0 + 4, 3 * heads)
            a = jnp.dot(u[...].reshape(rows, dim), w[path, :, c0 * HEAD:c1 * HEAD], preferred_element_type=F32) + row_of(small_ref, path, QKV_B, slice(c0 * HEAD, c1 * HEAD))
            for c in range(c0, c1):
                t = a[:, (c - c0) * HEAD:(c - c0 + 1) * HEAD]
                kind = c // heads
                if kind < 2:
                    t = t * lax.rsqrt(row_mean(t * t) + NORM_EPS) * row_of(small_ref, path, Q_GAIN + kind, slice(HEAD))
                    swapped = jnp.where(even, pltpu.roll(t, HEAD - 1, 1), pltpu.roll(t, 1, 1))
                    t = t * cos_t + swapped * sin_t
                qkv[c, at, :] = t.astype(BF16)

    m_wait(0)
    for j in range(n_dev):
        rows_here = m_early[j].astype(F32)
        for n in range(2 * 2 * batch):
            k, sel = n // (2 * batch), n % (2 * batch)
            vec_ref[sel, k:k + 1, j * width:(j + 1) * width] = rows_here[n:n + 1, :]
    x_wait(0)
    norm(0, ua)
    for path in PATHS:
        for j in range(3):
            w_load(path, j).wait()

    def qkv_step(t):
        x_start(2 * t + 3)
        x_start(2 * t + 4)
        x_wait(2 * t + 1)
        x_wait(2 * t + 2)
        @pl.when(t < 8)
        def _():
            late_load(t, 0).wait()

        late_chunk(t)
        norm(2 * t + 1, ub)
        heads_of(2 * t, ua)
        norm(jnp.minimum(2 * t + 2, blocks - 1), ua)
        heads_of(2 * t + 1, ub)

        @pl.when(t < 6)
        def _():
            late_start(t + 2)

    kv_store = pltpu.make_async_copy(qkv.at[:, total:, :], kv_hbm, tsem.at[0])

    def late_send():
        m_send(1)

    def kv_send():
        kv_store.start()

    done_here = batch + per_img

    def rows_of(n, c, size, r0):
        return qkv[c, rows_at(position(n)[0] * total + r0, size), :]

    def scores(n, h, s):
        s[...] = scores_of(rows_of(n, h, rows, position(n)[1]), rows_of(n, heads + h, total, 0))

    def weigh(n, h, s):
        o_all[rows_at(n * rows, rows), h * HEAD:(h + 1) * HEAD] = weighted(s[...], rows_of(n, 2 * heads + h, total, 0))

    def t_copy(kind, b, src, dst, dev):
        return remote(tsend, trecv, kind, b, src, dst, dev)

    def t_core(b):
        return t_copy(T_CORE, b, t_send, t_recv.at[b], partner)

    def t_first(b):
        return t_copy(T_FIRST, b, t_sum.at[b, rows_at(not1 * quarter, quarter), :], t_rs1.at[b], first)

    def t_second(b):
        return t_copy(T_SECOND, b, t_rs2_out.at[b], t_rs2_in.at[b], second)

    def own_rows(b1, b2):
        return rows_at(core * half + b1 * quarter + b2 * eighth, eighth)

    def t_out(kind, b, b1, b2, dev):
        ref = ut_hbm.at[b, own_rows(b1, b2), :]
        return t_copy(kind, b, t_u.at[b] if kind in (T_OUT_FIRST, T_OUT_SECOND, T_CORE_OWN) else ref, ref, dev)

    def t_local(b):
        return pltpu.make_async_copy(t_u.at[b], ut_hbm.at[b, own_rows(bit1, bit2), :], tsem.at[2 + b])

    def t_load(b):
        return pltpu.make_async_copy(txt_hbm.at[b, own_rows(bit1, bit2), :], t_x.at[b], tsem.at[2 + batch + b])

    tile = min(512, dim)

    def text_product(b, who, store):
        def columns(n):
            at = rows_at(n * tile, tile)
            store(at, jnp.dot(o_all[rows_at(b * rows + who * half, half), :], tw[:, at], preferred_element_type=F32))

        loop(dim // tile, columns)

    def text_partial(b):
        if b == 0:
            tw_load.wait()
        t_load(b).start()

        def to_send(at, value):
            t_send[:, at] = value.astype(BF16)

        def to_own(at, value):
            t_own[:, at] = value

        text_product(b, far, to_send)
        t_core(b).start()
        text_product(b, core, to_own)

    def text_sum(b):
        t_core(b).wait()

        def add(n):
            at = rows_at(n * STRIP, STRIP)
            t_sum[b, at, :] = (t_own[at, :] + t_recv[b, at, :].astype(F32)).astype(BF16)

        loop(half // STRIP, add)
        t_first(b).start()

    def text_quarter(b):
        t_first(b).wait()
        t_rs2_out[b] = (t_sum[b, rows_at(bit1 * quarter + not2 * eighth, eighth), :].astype(F32) + t_rs1[b, rows_at(not2 * eighth, eighth), :].astype(F32)).astype(BF16)
        t_keep[b] = t_sum[b, rows_at(bit1 * quarter + bit2 * eighth, eighth), :].astype(F32) + t_rs1[b, rows_at(bit2 * eighth, eighth), :].astype(F32)
        t_second(b).start()

    def text_finish(b):
        t_second(b).wait()
        t_load(b).wait()
        branch = t_keep[b] + t_rs2_in[b].astype(F32) + row_of(vec_ref, b, PROJ_B)
        x1 = (t_x[b].astype(F32) + row_of(vec_ref, b, GATE1) * branch).astype(BF16)
        x1_ref[b] = x1
        t_u[b] = modulated(x1.astype(F32), vec_ref, b, SHIFT2, SCALE2)
        t_out(T_OUT_FIRST, b, bit1, bit2, first).start()
        t_out(T_OUT_SECOND, b, bit1, bit2, second).start()
        t_out(T_CORE_OWN, b, bit1, bit2, partner).start()
        t_local(b).start()

    def text_relay(b):
        t_out(T_OUT_FIRST, b, not1, bit2, first).wait_recv()
        t_out(T_OUT_RELAY, b, not1, bit2, second).start()
        t_out(T_CORE_FIRST, b, not1, bit2, partner).start()
        t_out(T_OUT_SECOND, b, bit1, not2, second).wait_recv()
        t_out(T_CORE_SECOND, b, bit1, not2, partner).start()

    def text_last(b):
        t_out(T_OUT_RELAY, b, not1, not2, second).wait_recv()
        t_out(T_CORE_RELAY, b, not1, not2, partner).start()

    def g_rows(m, who):
        return o_all.at[rows_at((batch + m) * rows + who * half, half), :]

    def g_mine(m):
        return og_hbm.at[m, :, rows_at(me * width, width)]

    def g_local(m):
        return pltpu.make_async_copy(g_rows(m, core), g_mine(m), gsem.at[m])

    def g_core(m):
        return remote(gsend, grecv, G_CORE, m, g_rows(m, far), g_mine(m), partner)

    def g_copy(kind, m, owner, dev):
        ref = og_hbm.at[m, :, rows_at(owner // 2 * (2 * width), 2 * width)]
        return remote(gsend, grecv, kind, m, ref, ref, dev)

    def gather_start(m):
        g_local(m).start()
        g_core(m).start()

    def gather_send(m):
        g_local(m).wait()
        g_core(m).wait()
        g_copy(G_FIRST, m, me, first).start()
        g_copy(G_SECOND, m, me, second).start()

    def gather_relay(m):
        g_copy(G_FIRST, m, first, first).wait_recv()
        g_copy(G_RELAY, m, first, second).start()

    qkv_first, attend_first = (batch + per_img) // 2, 1 + EARLY
    resume = blocks // 2 + attend_first
    steps = blocks // 2 + done_here
    known = dict(locals())

    def run(calls):
        for call in calls:
            name, *args = call.split()
            known[name](*map(int, args))

    def attended(a):
        early = ((a >= 1) & (a <= EARLY)).astype(jnp.int32)
        return a + early - EARLY * (a == attend_first).astype(jnp.int32)

    def attention_step(a, begins):
        n = attended(a)

        @pl.when(begins)
        def _():
            scores(n, 0, s0)

        scores(n, 1, s1)
        weigh(n, 0, s0)
        scores(n, 2, s2)
        weigh(n, 1, s1)
        scores(attended(jnp.minimum(a + 1, done_here - 1)), 0, s0)
        weigh(n, 2, s2)

    def step(i):
        for when, calls in enumerate(HOOKS[:steps]):
            if calls:
                @pl.when(i == when)
                def _():
                    run(calls)

        in_first = i < qkv_first
        in_second = (i >= qkv_first + attend_first) & (i < resume)

        @pl.when(in_first | in_second)
        def _():
            qkv_step(i - attend_first * in_second.astype(jnp.int32))

        @pl.when(jnp.logical_not(in_first | in_second))
        def _():
            late = (i >= resume).astype(jnp.int32)
            attention_step(i - late * (blocks // 2) - (1 - late) * qkv_first, (i == qkv_first) | (i == resume))

    loop(steps, step)

    o_out = pltpu.make_async_copy(o_all.at[batch * rows:, :], o_hbm, osem)
    o_out.start()
    run(HOOKS[steps])
    o_out.wait()
    kv_store.wait()
    for b in range(batch):
        t_local(b).wait()
        for kind, b1, b2, dev in ((T_OUT_FIRST, bit1, bit2, first), (T_OUT_SECOND, bit1, bit2, second), (T_OUT_RELAY, not1, bit2, second)):
            t_out(kind, b, b1, b2, dev).wait_send()
        for kind, b1, b2 in ((T_CORE_OWN, bit1, bit2), (T_CORE_FIRST, not1, bit2), (T_CORE_SECOND, bit1, not2), (T_CORE_RELAY, not1, not2)):
            t_out(kind, b, b1, b2, partner).wait()
    for j in (SHARED, COMMON):
        for kind, owner, dev in ((W_FIRST, me, first), (W_SECOND, me, second), (W_RELAY, first, second)):
            p_copy(kind, j, owner, dev).wait_send()
    w_own().wait()
    for kind, owner, core_kind in from_beside:
        z_copy(kind, owner).wait_send()
        for j in range(PIECES):
            p_copy(core_kind, j, owner, partner).wait()
    for m in range(READY):
        g_copy(G_FIRST, m, me, first).wait_send()
        g_copy(G_SECOND, m, me, second).wait_send()
        g_copy(G_RELAY, m, first, second).wait_send()
        g_copy(G_SECOND, m, second, second).wait_recv()
        g_copy(G_RELAY, m, diagonal, second).wait_recv()


HOOKS = (
    (),
    (),
    (),
    (),
    ('w_relay 0', 'w_second 0'),
    ('w_relay 1',),
    ('text_partial 0',),
    ('text_sum 0',),
    ('gather_start 0',),
    (),
    ('gather_send 0',),
    ('late_send', 'text_quarter 0', 'gather_start 1'),
    ('kv_send', 'w_last 1', 'gather_send 1'),
    ('late_rows', 'text_finish 0', 'text_partial 1', 'w_beside 0', 'w_last 0', 'text_sum 1'),
    (),
    ('gather_relay 1', 'text_quarter 1', 'gather_start 2', 'gather_send 2', 'text_relay 0'),
    ('w_beside 1', 'text_finish 1'),
    ('w_beside 2', 'w_second 1', 'gather_relay 0'),
    ('text_relay 1', 'gather_relay 2'),
    ('text_last 1', 'text_last 0'),
)


def front_call(txt, img, wt, wi, mt, mi, pw, tw, cond, small_t, small_i, ids_t, table, n_dev, rows):
    batch, txt_len, dim = txt.shape
    img_len = img.shape[1]
    total = txt_len + img_len
    width = pw.shape[0]
    heads = width // HEAD
    half, quarter, eighth = rows // 2, rows // 4, rows // 8
    assert heads == HEADS_HERE and batch == 2
    cfg = (batch, txt_len, img_len, rows)
    blocks = batch * (1 + img_len // rows)
    vmem = pl.BlockSpec(memory_space=pltpu.VMEM)
    anywhere = pl.BlockSpec(memory_space=pl.ANY)
    tall = [pltpu.VMEM((half, dim), BF16), pltpu.VMEM((batch, half, dim), BF16), pltpu.VMEM((half, dim), F32), pltpu.VMEM((batch, half, dim), BF16), pltpu.VMEM((batch, quarter, dim), BF16)]
    short = [pltpu.VMEM((batch, eighth, dim), dtype) for dtype in (BF16, BF16, F32, BF16, BF16)]
    return pl.pallas_call(
        functools.partial(front_kernel, cfg),
        in_specs=[anywhere] * 8 + [vmem, (vmem,) * len(small_t), (vmem,) * len(small_i), vmem, vmem],
        out_specs=[anywhere] * 5 + [vmem] * 3,
        out_shape=[
            jax.ShapeDtypeStruct((img_len, width), BF16),
            jax.ShapeDtypeStruct((3 * heads, total, HEAD), BF16),
            jax.ShapeDtypeStruct((n_dev, width, dim), BF16),
            jax.ShapeDtypeStruct((batch, txt_len, dim), BF16),
            jax.ShapeDtypeStruct((READY, half, dim), BF16),
            jax.ShapeDtypeStruct((batch, eighth, dim), BF16),
            jax.ShapeDtypeStruct((2 * batch, FC2_B + 1, dim), F32),
            jax.ShapeDtypeStruct((2, FC1_B + 1, dim), F32),
        ],
        scratch_shapes=[
            pltpu.VMEM((2, dim, 3 * width), BF16),
            pltpu.VMEM((2, dim, width), BF16),
            pltpu.VMEM((2, PROJ_B, width), F32),
            pltpu.VMEM((n_dev, 4 * batch, width), BF16),
            pltpu.VMEM((n_dev, blocks // 2, batch, width), F32),
            pltpu.VMEM((4, rows, dim), BF16),
            pltpu.VMEM((batch, half, dim), BF16),
            pltpu.VMEM((batch, half, dim), BF16),
            pltpu.VMEM((3 * heads, batch * total, HEAD), BF16),
            pltpu.VMEM((rows, total), F32),
            pltpu.VMEM((rows, total), F32),
            pltpu.VMEM((rows, total), F32),
            pltpu.VMEM((batch * txt_len + img_len, width), BF16),
            pltpu.VMEM((width, dim), BF16),
            *tall,
            *short,
            pltpu.SemaphoreType.DMA((2, 3)),
            pltpu.SemaphoreType.DMA((2,)),
            pltpu.SemaphoreType.DMA((4,)),
            pltpu.SemaphoreType.DMA,
            pltpu.SemaphoreType.DMA((6,)),
            pltpu.SemaphoreType.DMA((READY,)),
            *[pltpu.SemaphoreType.DMA((10, PIECES))] * 2,
            *[pltpu.SemaphoreType.DMA((10, batch))] * 2,
            *[pltpu.SemaphoreType.DMA((4, READY))] * 2,
            pltpu.SemaphoreType.DMA((2, n_dev)),
            pltpu.SemaphoreType.DMA((2, n_dev)),
        ],
        compiler_params=pltpu.CompilerParams(collective_id=2, has_side_effects=True, vmem_limit_bytes=VMEM_BYTES),
        name="front",
    )(txt, img, wt, wi, mt, mi, pw, tw, cond, small_t, small_i, ids_t, table)


(O_CORE, O_FIRST, O_SECOND, O_RELAY, U_CORE, PART_CORE, RS_FIRST, RS_SECOND, OUT_FIRST, OUT_SECOND, OUT_RELAY, CORE_OWN, CORE_FIRST, CORE_SECOND, CORE_RELAY) = range(15)
(L_O, L_X, L_OUT) = range(3)
SLOTS = 4
O_SLOTS = 6
SEMS = 8


def two(n):
    return n % 2


def block_kernel(cfg, o_hbm, og_hbm, kv_hbm, x_hbm, ut_hbm, x1t_hbm, wp_hbm, pw_hbm, w1t_hbm, w2t_hbm, w1i_hbm, w2i_hbm, vec_ref, fb_ref, out_hbm, o2_hbm,
                 kv, qs, os, wp, w1, w2, obuf, xbuf, x1buf, x1keep, u2, hid, psend, precv, own, chip_sum, rs1, keep2, rs2_out, rs2_in, outb,
                 asem, wsem, lsem, tsem, ssem, rsem):
    batch, txt_chunks, img_chunks, per_img, rows, tile = cfg
    half, quarter, eighth = rows // 2, rows // 4, rows // 8
    dim = wp.shape[0]
    ff = w1.shape[1]
    cols = o_hbm.shape[1]
    heads = cols // HEAD
    total = txt_chunks + img_chunks
    per_txt = txt_chunks // batch

    place = Place()
    me, core, partner, first, second, bit1, bit2 = place.me, place.core, place.partner, place.first, place.second, place.bit1, place.bit2
    not1, not2, far = place.not1, place.not2, place.far
    txt_len = ut_hbm.shape[1]
    place.enter([partner, first, second])

    def remote(kind, g, src, dst, dev):
        return pltpu.make_async_remote_copy(src_ref=src, dst_ref=dst, send_sem=ssem.at[kind, g % SEMS], recv_sem=rsem.at[kind, g % SEMS], device_id={'tp': dev}, device_id_type=MESH)

    def img_pos(g):
        k = g - txt_chunks
        return k // per_img, (k % per_img) * rows

    def chip_cols(dev):
        return rows_at((dev // 2) * (2 * cols), 2 * cols)

    def own_rows(b1, b2):
        return core * half + b1 * quarter + b2 * eighth

    def o_from(b):
        return (o_hbm, o2_hbm)[b]

    first_open = txt_chunks + og_hbm.shape[0]

    def o_ready(g):
        return pltpu.make_async_copy(og_hbm.at[g - txt_chunks], obuf.at[g % O_SLOTS], lsem.at[L_O, g % SEMS])

    def o_local(g, b):
        r0 = img_pos(g)[1]
        return pltpu.make_async_copy(o_from(b).at[rows_at(r0 + core * half, half), :], obuf.at[g % O_SLOTS, :, rows_at(me * cols, cols)], lsem.at[L_O, g % SEMS])

    def o_core(g, b):
        r0 = img_pos(g)[1]
        return remote(O_CORE, g, o_from(b).at[rows_at(r0 + far * half, half), :], obuf.at[g % O_SLOTS, :, rows_at(me * cols, cols)], partner)

    units = per_img * heads

    def q_load(u):
        r0 = txt_len + u // heads * rows
        return pltpu.make_async_copy(kv_hbm.at[u % heads, rows_at(r0, rows), :], qs.at[two(u)], asem.at[two(u)])

    def o_store(u):
        return pltpu.make_async_copy(os.at[two(u)], o2_hbm.at[rows_at(u // heads * rows, rows), rows_at(u % heads * HEAD, HEAD)], asem.at[2 + two(u)])

    def kv_load():
        return pltpu.make_async_copy(kv_hbm.at[heads:], kv, asem.at[4])

    def attend(u):
        q_load(u).wait()

        @pl.when(u + 1 < units)
        def _():
            q_load(u + 1).start()

        @pl.when(u >= 2)
        def _():
            o_store(u - 2).wait()

        k = kv[u % heads]
        v = kv[heads + u % heads]
        for r in range(0, rows, half):
            os[two(u), r:r + half, :] = weighted(scores_of(qs[two(u), r:r + half, :], k), v)
        o_store(u).start()

    def attend_pair(i):
        @pl.when(i == 0)
        def _():
            kv_load().wait()

        attend(2 * i)
        attend(2 * i + 1)

        @pl.when(i == units // 2 - 1)
        def _():
            o_store(units - 2).wait()
            o_store(units - 1).wait()

    def o_send(kind, g, owner, dev):
        ref = obuf.at[g % O_SLOTS, :, chip_cols(owner)]
        return remote(kind, g, ref, ref, dev)

    def x_load(g):
        b, r0 = img_pos(g)
        return pltpu.make_async_copy(x_hbm.at[b, rows_at(r0 + core * half, half), :], xbuf.at[two(g)], lsem.at[L_X, g % SEMS])

    def u_core(g):
        ref = u2.at[two(g), rows_at(core * half, half), :]
        return remote(U_CORE, g, ref, ref, partner)

    def part_core(g):
        return remote(PART_CORE, g, psend, precv.at[two(g)], partner)

    def rs_first(g):
        return remote(RS_FIRST, g, chip_sum.at[rows_at(not1 * quarter, quarter), :], rs1.at[two(g)], first)

    def rs_second(g):
        return remote(RS_SECOND, g, rs2_out.at[two(g)], rs2_in.at[g % SLOTS], second)

    def out_ref(g, b1, b2):
        return out_hbm.at[rows_at(g * rows + own_rows(b1, b2), eighth), :]

    def out_send(kind, g, b1, b2, dev):
        ref = out_ref(g, b1, b2)
        mine = kind in (OUT_FIRST, OUT_SECOND, CORE_OWN)
        return remote(kind, g, outb.at[g % SLOTS] if mine else ref, ref, dev)

    def out_local(g):
        return pltpu.make_async_copy(outb.at[g % SLOTS], out_ref(g, bit1, bit2), lsem.at[L_OUT, g % SEMS])

    def txt_load(g):
        b, r0 = g // per_txt, (g % per_txt) * rows
        return (pltpu.make_async_copy(ut_hbm.at[b, rows_at(r0, rows), :], u2.at[two(g)], tsem.at[0, two(g)]),
                pltpu.make_async_copy(x1t_hbm.at[g], x1keep.at[g % SLOTS], tsem.at[1, two(g)]))

    def w_load(k, src, dst):
        return pltpu.make_async_copy(src, dst, wsem.at[k])

    def wp_load(j, src):
        return pltpu.make_async_copy(src, wp.at[j * cols:(j + 1) * cols, :], wsem.at[2 + j])

    def select(g):
        txt = (g < txt_chunks).astype(jnp.int32)
        return txt * (g // per_txt) + (1 - txt) * (batch + (g - txt_chunks) // per_img)

    def start_o(g):
        @pl.when(g < first_open)
        def _():
            o_ready(g).start()

        for b in range(batch):
            @pl.when((g >= first_open) & (img_pos(g)[0] == b))
            def _():
                o_local(g, b).start()
                o_core(g, b).start()

    def send_o(g):
        o_local(g, 0).wait()
        o_core(g, 0).wait()
        o_send(O_FIRST, g, me, first).start()
        o_send(O_SECOND, g, me, second).start()

    def relay_o(g):
        o_send(O_FIRST, g, first, first).wait_recv()
        o_send(O_RELAY, g, first, second).start()

    def start_x(g):
        x_load(g).start()

    def project(g):
        @pl.when(g < first_open)
        def _():
            o_ready(g).wait()

        @pl.when(g >= first_open)
        def _():
            o_send(O_FIRST, g, me, first).wait_send()
            o_send(O_SECOND, g, me, second).wait_send()
            o_send(O_RELAY, g, first, second).wait_send()
            o_send(O_SECOND, g, second, second).wait_recv()
            o_send(O_RELAY, g, second, second).wait_recv()

        x_load(g).wait()

        @pl.when(g == txt_chunks)
        def _():
            for j in range(wp_hbm.shape[0]):
                wp_load(j, wp_hbm.at[j]).wait()

        sel = select(g)
        slot = g % SLOTS

        def columns(n):
            at = rows_at(n * tile, tile)
            acc = jnp.dot(obuf[g % O_SLOTS], wp[:, at], preferred_element_type=F32)
            branch = acc + row_of(vec_ref, sel, PROJ_B, at)
            x1buf[:, at] = (xbuf[two(g), :, at].astype(F32) + row_of(vec_ref, sel, GATE1, at) * branch).astype(BF16)

        loop(dim // tile, columns)

        def norm(n):
            at = rows_at(n * STRIP, STRIP)
            u2[two(g), rows_at(core * half + n * STRIP, STRIP), :] = modulated(x1buf[at, :].astype(F32), vec_ref, sel, SHIFT2, SCALE2)

        loop(half // STRIP, norm)
        u_core(g).start()
        x1keep[slot] = x1buf[rows_at(bit1 * quarter + bit2 * eighth, eighth), :]

    def mlp_hidden(g):
        @pl.when(g < txt_chunks)
        def _():
            for copy in txt_load(g):
                copy.wait()

        @pl.when(g >= txt_chunks)
        def _():
            u_core(g).wait()

        @pl.when(g == 0)
        def _():
            w_load(0, w1t_hbm, w1).wait()
            w_load(1, w2t_hbm, w2).wait()
            for j in range(wp_hbm.shape[0]):
                @pl.when(j != me)
                def _():
                    wp_load(j, wp_hbm.at[j]).start()

                @pl.when(j == me)
                def _():
                    wp_load(j, pw_hbm).start()

        @pl.when(g == txt_chunks)
        def _():
            w_load(0, w1i_hbm, w1).wait()
            w_load(1, w2i_hbm, w2).wait()

        path = (g >= txt_chunks).astype(jnp.int32)

        def hidden(n):
            at = rows_at(n * tile, tile)
            acc = jnp.dot(u2[two(g)], w1[:, at], preferred_element_type=F32)
            pre = acc + row_of(fb_ref, path, FC1_B, at)
            hid[:, at] = jax.nn.gelu(pre, approximate=True).astype(BF16)

        loop(ff // tile, hidden)

    def mlp_theirs(g):
        def theirs(n):
            at = rows_at(n * tile, tile)
            psend[:, at] = jnp.dot(hid[rows_at(far * half, half), :], w2[:, at], preferred_element_type=F32).astype(BF16)

        loop(dim // tile, theirs)
        part_core(g).start()

    def mlp_mine(g):
        def mine(n):
            at = rows_at(n * tile, tile)
            own[:, at] = jnp.dot(hid[rows_at(core * half, half), :], w2[:, at], preferred_element_type=F32)

        loop(dim // tile, mine)

        @pl.when(g == txt_chunks - 1)
        def _():
            w_load(0, w1i_hbm, w1).start()
            w_load(1, w2i_hbm, w2).start()

        part_core(g).wait()

        def add(n):
            at = rows_at(n * STRIP, STRIP)
            chip_sum[at, :] = (own[at, :] + precv[two(g), at, :].astype(F32)).astype(BF16)

        loop(half // STRIP, add)
        rs_first(g).start()

    def add_first(g):
        rs_first(g).wait()
        rs2_out[two(g)] = (chip_sum[rows_at(bit1 * quarter + not2 * eighth, eighth), :].astype(F32) + rs1[two(g), rows_at(not2 * eighth, eighth), :].astype(F32)).astype(BF16)
        rs_second(g).start()
        keep2[two(g)] = chip_sum[rows_at(bit1 * quarter + bit2 * eighth, eighth), :].astype(F32) + rs1[two(g), rows_at(bit2 * eighth, eighth), :].astype(F32)

    def finish(g):
        rs_second(g).wait()
        sel = select(g)
        branch = keep2[two(g)] + rs2_in[g % SLOTS].astype(F32) + row_of(vec_ref, sel, FC2_B)
        outb[g % SLOTS] = (x1keep[g % SLOTS].astype(F32) + row_of(vec_ref, sel, GATE2) * branch).astype(BF16)
        out_send(OUT_FIRST, g, bit1, bit2, first).start()
        out_send(OUT_SECOND, g, bit1, bit2, second).start()
        out_send(CORE_OWN, g, bit1, bit2, partner).start()
        out_local(g).start()

    def relay_out(g):
        out_send(OUT_FIRST, g, not1, bit2, first).wait_recv()
        out_send(OUT_RELAY, g, not1, bit2, second).start()
        out_send(CORE_FIRST, g, not1, bit2, partner).start()

    def second_out(g):
        out_send(OUT_SECOND, g, bit1, not2, second).wait_recv()
        out_send(CORE_SECOND, g, bit1, not2, partner).start()

    def relay_core(g):
        out_send(OUT_RELAY, g, not1, not2, second).wait_recv()
        out_send(CORE_RELAY, g, not1, not2, partner).start()

    def drain(g):
        out_local(g).wait()
        out_send(OUT_FIRST, g, bit1, bit2, first).wait_send()
        out_send(OUT_SECOND, g, bit1, bit2, second).wait_send()
        out_send(OUT_RELAY, g, not1, bit2, second).wait_send()
        out_send(CORE_OWN, g, bit1, bit2, partner).wait()
        out_send(CORE_FIRST, g, not1, bit2, partner).wait()
        out_send(CORE_SECOND, g, bit1, not2, partner).wait()
        out_send(CORE_RELAY, g, not1, not2, partner).wait()

    kv_load().start()
    q_load(0).start()
    w_load(0, w1t_hbm, w1).start()
    w_load(1, w2t_hbm, w2).start()
    for g in range(txt_chunks):
        for copy in txt_load(g):
            copy.start()

    stages = ((mlp_hidden, 0, 0), (relay_o, 2, first_open), (start_x, 2, txt_chunks), (finish, -3, 0), (start_o, 5, txt_chunks), (relay_out, -4, 0), (mlp_theirs, 0, 0), (second_out, -5, 0),
              (send_o, 5, first_open), (relay_core, -6, 0), (project, 1, txt_chunks), (add_first, -1, 0), (mlp_mine, 0, 0), (drain, -6, 0))
    most = max(ahead for _, ahead, _ in stages)
    least = min(ahead for _, ahead, _ in stages)

    def step(i):
        for stage, ahead, lowest in stages:
            g = i + txt_chunks - most + ahead

            @pl.when((g >= lowest) & (g < total))
            def _():
                stage(g)

        @pl.when((i >= ATTEND_FROM) & (i < ATTEND_FROM + units // 2))
        def _():
            attend_pair(i - ATTEND_FROM)

    loop(total - txt_chunks + most - least, step)


ATTEND_FROM = 1


def block_call(img_o, og, kv, x, u_txt, x1_txt, wp, pw, w1t, w2t, w1i, w2i, vecs, fb, rows):
    batch, img_len, dim = x.shape
    txt_len = u_txt.shape[1]
    ff = w1t.shape[1]
    txt_chunks = batch * (txt_len // rows)
    per_img = img_len // rows
    img_chunks = batch * per_img
    assert txt_chunks == 2
    half, quarter, eighth = rows // 2, rows // 4, rows // 8
    cfg = (batch, txt_chunks, img_chunks, per_img, rows, 512)
    total = txt_chunks + img_chunks
    anywhere = pl.BlockSpec(memory_space=pl.ANY)
    return pl.pallas_call(
        functools.partial(block_kernel, cfg),
        in_specs=[anywhere] * 12 + [pl.BlockSpec(memory_space=pltpu.VMEM)] * 2,
        out_specs=[anywhere, anywhere],
        out_shape=[jax.ShapeDtypeStruct((total * rows, dim), BF16), jax.ShapeDtypeStruct(img_o.shape, BF16)],
        scratch_shapes=[
            pltpu.VMEM((kv.shape[0] // 3 * 2,) + kv.shape[1:], BF16),
            pltpu.VMEM((2, rows, HEAD), BF16),
            pltpu.VMEM((2, rows, HEAD), BF16),
            pltpu.VMEM((dim, dim), BF16),
            pltpu.VMEM((dim, ff), BF16),
            pltpu.VMEM((ff, dim), BF16),
            pltpu.VMEM((O_SLOTS, half, dim), BF16),
            pltpu.VMEM((2, half, dim), BF16),
            pltpu.VMEM((half, dim), BF16),
            pltpu.VMEM((SLOTS, eighth, dim), BF16),
            pltpu.VMEM((2, rows, dim), BF16),
            pltpu.VMEM((rows, ff), BF16),
            pltpu.VMEM((half, dim), BF16),
            pltpu.VMEM((2, half, dim), BF16),
            pltpu.VMEM((half, dim), F32),
            pltpu.VMEM((half, dim), BF16),
            pltpu.VMEM((2, quarter, dim), BF16),
            pltpu.VMEM((2, eighth, dim), F32),
            pltpu.VMEM((2, eighth, dim), BF16),
            pltpu.VMEM((SLOTS, eighth, dim), BF16),
            pltpu.VMEM((SLOTS, eighth, dim), BF16),
            pltpu.SemaphoreType.DMA((5,)),
            pltpu.SemaphoreType.DMA((10,)),
            pltpu.SemaphoreType.DMA((3, SEMS)),
            pltpu.SemaphoreType.DMA((2, 2)),
            pltpu.SemaphoreType.DMA((15, SEMS)),
            pltpu.SemaphoreType.DMA((15, SEMS)),
        ],
        compiler_params=pltpu.CompilerParams(collective_id=0, has_side_effects=True, vmem_limit_bytes=VMEM_BYTES),
        name="block",
    )(img_o, og, kv, x, u_txt, x1_txt, wp, pw, w1t, w2t, w1i, w2i, vecs, fb)


def copy_kernel(pieces, flat_hbm, *rest):
    outs, (buf, isem, osem) = rest[:-3], rest[-3:]
    rows = buf.shape[1]
    loads = []
    for n, (which, b, r) in enumerate(pieces):
        load = pltpu.make_async_copy(flat_hbm.at[n * rows:(n + 1) * rows, :], buf.at[n], isem.at[n])
        load.start()
        loads.append(load)
    stores = []
    for n, (which, b, r) in enumerate(pieces):
        loads[n].wait()
        store = pltpu.make_async_copy(buf.at[n], outs[which].at[b, r:r + rows, :], osem.at[n])
        store.start()
        stores.append(store)
    for store in stores:
        store.wait()


def copy_call(flat, shapes, rows):
    pieces = [(which, b, r) for which, shape in enumerate(shapes) for b in range(shape[0]) for r in range(0, shape[1], rows)]
    anywhere = pl.BlockSpec(memory_space=pl.ANY)
    dim = flat.shape[1]
    return pl.pallas_call(
        functools.partial(copy_kernel, pieces),
        in_specs=[anywhere],
        out_specs=[anywhere] * len(shapes),
        out_shape=[jax.ShapeDtypeStruct(shape, flat.dtype) for shape in shapes],
        scratch_shapes=[
            pltpu.VMEM((len(pieces), rows, dim), flat.dtype),
            pltpu.SemaphoreType.DMA((len(pieces),)),
            pltpu.SemaphoreType.DMA((len(pieces),)),
        ],
        compiler_params=pltpu.CompilerParams(vmem_limit_bytes=VMEM_BYTES),
        name="copy_out",
    )(flat)


def local_block(img, txt, vec, ids, img_w, txt_w):
    n_dev = 8
    batch, txt_len = txt.shape[:2]
    rows = txt_len

    def by_kind(weight):
        return jnp.transpose(weight, (1, 0, 2))

    def small_of(w):
        return w[1], w[3], w[4], w[5], w[7], w[9], w[11]

    table = jnp.asarray(rope_table())
    ids_t = jnp.transpose(ids, (2, 0, 1))
    o, kv, proj_w, txt_u, og, txt_x1, vecs, small = front_call(txt, img, by_kind(txt_w[2]), by_kind(img_w[2]), by_kind(txt_w[0]), by_kind(img_w[0]), img_w[6], txt_w[6], vec, small_of(txt_w), small_of(img_w), ids_t, table, n_dev, rows)
    flat, _ = block_call(o, og, kv, img, txt_u, txt_x1, proj_w, img_w[6], txt_w[8], txt_w[10], img_w[8], img_w[10], vecs, small, rows)
    txt_out, img_out = copy_call(flat, (txt.shape, img.shape), rows)
    return img_out, txt_out


def solution(mesh):
    act_spec = P('dp', WHOLE, WHOLE)
    mapped = jax.shard_map(local_block, mesh=mesh, in_specs=(act_spec, act_spec, P('dp', WHOLE), act_spec, PATH_SPECS, PATH_SPECS), out_specs=(act_spec, act_spec), check_vma=False)

    def forward(img, txt, vec, ids, *weights):
        return mapped(img, txt, vec, ids, weights[:12], weights[12:])

    return forward
```

time: 511 us -> 494 us (0.967)
  Pallas kernels: 510 us -> 493 us
    pallas_call x1 -> x0, Pallas kernels: 17.4 us -> none  [mods_call(): pl.pallas_call(mods_kernel, in_specs=[vmem, (vmem,) * len(small_t), (vmem...]
where the time goes in v4:
time: 494 us
  Pallas kernels  493 us (100%)
    pallas_call x1, Pallas kernels, block_call(): pl.pallas_call(functools.partial(block_kernel, cfg), in_specs=[anywhere]...  354 us
    pallas_call x1, Pallas kernels, front_call(): pl.pallas_call(functools.partial(front_kernel, cfg), in_specs=[anywhere]...  120 us
    pallas_call x1, Pallas kernels, copy_call(): pl.pallas_call(functools.partial(copy_kernel, pieces), in_specs=[anywhere...  19.3 us

profile of v4, /device:TPU:0, one launch (start us, length us, event | category | flops | bytes accessed | tf_op | source)
XLA Modules:
  0.0 494.1 jit_solution(2410137090470519142)
XLA Ops:
  0.6 120.0 %front.1 = (bf16[2048,384]{1,0:T(8,128)(2,1)}, bf16[9,2304,128]{2,1,0:T(8,128)(2,1)}, bf16[8,384,3072]{2,1,0:T(8,128)(2,1)}, bf16[2,256,3072]{2,1,0:T(8,128)(2,1...) custom-call(bf16[2,256,3072]{2,1,0:T(8,128)(2,1)} %txt_hbm.1, ...), custom_call_target="tpu_custom_call" | custom-call | tf_op jit(solution)/shard_map/front/pallas_call | solution.py:626
  120.6 354.0 %block.1 = (bf16[4608,3072]{1,0:T(8,128)(2,1)}, bf16[2048,384]{1,0:T(8,128)(2,1)}) custom-call(bf16[2048,384]{1,0:T(8,128)(2,1)} %get-tuple-element.13.o_hbm, bf16[3,128,3072]{2,1,0:T(8,128)(2,1)} %get-tuple-element.14.og_hbm, bf16[9,2304,128]{2,1,0:T(8,128)(2,1)} %get-tuple-element.15.kv_hbm, bf16[2,2048,3072]{2,1,0:T(8,128)(2,1)} %x_hbm.1, ...), custom_call_target="tpu_custom_call" | custom-call | tf_op jit(solution)/shard_map/block/pallas_call | solution.py:1033
  474.6 19.3 %copy_out.1 = (bf16[2,256,3072]{2,1,0:T(8,128)(2,1)}, bf16[2,2048,3072]{2,1,0:T(8,128)(2,1)}) custom-call(bf16[4608,3072]{1,0:T(8,128)(2,1)} %get-tuple-element.21.flat_hbm), custom_call_target="tpu_custom_call" | custom-call | tf_op jit(solution)/shard_map/copy_out/pallas_call | solution.py:1094

commit v5 on v4

--- a/solution.py
+++ b/solution.py
@@ -240,13 +240,9 @@
 
     m_early[me] = jnp.concatenate([early_chunk(k, path) for k in (SHIFT1, SCALE1) for path in PATHS], axis=0)
     m_send(0)
-    for path in PATHS:
-        for j in range(3):
-            w_load(path, j).start()
-    for c in range(2):
-        late_load(c, c).start()
+    for j in range(3):
+        w_load(0, j).start()
     tw_load = pltpu.make_async_copy(tw_hbm, tw, tsem.at[1])
-    tw_load.start()
 
     def late_chunk(t):
         c = jnp.minimum(t, 7)
@@ -349,15 +345,24 @@
             vec_ref[sel, k:k + 1, j * width:(j + 1) * width] = rows_here[n:n + 1, :]
     x_wait(0)
     norm(0, ua)
-    for path in PATHS:
-        for j in range(3):
-            w_load(path, j).wait()
+    for j in range(3):
+        w_load(0, j).wait()
+    for c in range(2):
+        late_load(c, c).start()
+    for j in range(3):
+        w_load(1, j).start()
+    tw_load.start()
 
     def qkv_step(t):
         x_start(2 * t + 3)
         x_start(2 * t + 4)
         x_wait(2 * t + 1)
         x_wait(2 * t + 2)
+        @pl.when(t == 1)
+        def _():
+            for j in range(3):
+                w_load(1, j).wait()
+
         @pl.when(t < 8)
         def _():
             late_load(t, 0).wait()
@@ -674,7 +679,7 @@
 (O_CORE, O_FIRST, O_SECOND, O_RELAY, U_CORE, PART_CORE, RS_FIRST, RS_SECOND, OUT_FIRST, OUT_SECOND, OUT_RELAY, CORE_OWN, CORE_FIRST, CORE_SECOND, CORE_RELAY) = range(15)
 (L_O, L_X, L_OUT) = range(3)
 SLOTS = 4
-O_SLOTS = 6
+O_SLOTS = 7
 SEMS = 8
 
 
@@ -987,35 +992,40 @@
         out_send(CORE_SECOND, g, bit1, not2, partner).wait()
         out_send(CORE_RELAY, g, not1, not2, partner).wait()
 
-    kv_load().start()
-    q_load(0).start()
+    opened = txt_chunks + O_SLOTS - 1
+    for g in range(txt_chunks, opened):
+        start_o(jnp.int32(g))
     w_load(0, w1t_hbm, w1).start()
     w_load(1, w2t_hbm, w2).start()
     for g in range(txt_chunks):
         for copy in txt_load(g):
             copy.start()
 
-    stages = ((mlp_hidden, 0, 0), (relay_o, 2, first_open), (start_x, 2, txt_chunks), (finish, -3, 0), (start_o, 5, txt_chunks), (relay_out, -4, 0), (mlp_theirs, 0, 0), (second_out, -5, 0),
-              (send_o, 5, first_open), (relay_core, -6, 0), (project, 1, txt_chunks), (add_first, -1, 0), (mlp_mine, 0, 0), (drain, -6, 0))
+    kv_load().start()
+    q_load(0).start()
+    for g in range(first_open, opened):
+        send_o(jnp.int32(g))
+
+    stages = ((second_out, -5, 0), (attend_pair, 0, 0), (mlp_hidden, 0, 0), (start_o, 5, opened), (relay_o, 4, first_open), (start_x, 2, txt_chunks), (relay_out, -4, 0), (mlp_theirs, 0, 0),
+              (send_o, 5, opened), (add_first, -1, 0), (mlp_mine, 0, 0), (relay_core, -6, 0), (project, 1, txt_chunks), (drain, -6, 0), (finish, -2, 0))
     most = max(ahead for _, ahead, _ in stages)
     least = min(ahead for _, ahead, _ in stages)
 
     def step(i):
         for stage, ahead, lowest in stages:
-            g = i + txt_chunks - most + ahead
-
-            @pl.when((g >= lowest) & (g < total))
+            if stage is attend_pair:
+                g, lowest, highest = i - ATTEND_FROM, 0, units // 2
+            else:
+                g, highest = i + txt_chunks - most + ahead, total
+
+            @pl.when((g >= lowest) & (g < highest))
             def _():
                 stage(g)
 
-        @pl.when((i >= ATTEND_FROM) & (i < ATTEND_FROM + units // 2))
-        def _():
-            attend_pair(i - ATTEND_FROM)
-
     loop(total - txt_chunks + most - least, step)
 
 
-ATTEND_FROM = 1
+ATTEND_FROM = 3
 
 
 def block_call(img_o, og, kv, x, u_txt, x1_txt, wp, pw, w1t, w2t, w1i, w2i, vecs, fb, rows):

time: 494 us -> 482 us (0.976)
  Pallas kernels: 493 us -> 481 us
    pallas_call x1, Pallas kernels: 354 us -> 341 us  [block_call(): pl.pallas_call(functools.partial(block_kernel, cfg), in_specs=[anywhere]...]
where the time goes in v5:
time: 482 us
  Pallas kernels  481 us (100%)
    pallas_call x1, Pallas kernels, block_call(): pl.pallas_call(functools.partial(block_kernel, cfg), in_specs=[anywhere]...  341 us
    pallas_call x1, Pallas kernels, front_call(): pl.pallas_call(functools.partial(front_kernel, cfg), in_specs=[anywhere]...  121 us
    pallas_call x1, Pallas kernels, copy_call(): pl.pallas_call(functools.partial(copy_kernel, pieces), in_specs=[anywhere...  19.3 us

profile of v5, /device:TPU:0, one launch (start us, length us, event | category | flops | bytes accessed | tf_op | source)
XLA Modules:
  0.0 482.1 jit_solution(8040312764720255677)
XLA Ops:
  0.6 121.1 %front.1 = (bf16[2048,384]{1,0:T(8,128)(2,1)}, bf16[9,2304,128]{2,1,0:T(8,128)(2,1)}, bf16[8,384,3072]{2,1,0:T(8,128)(2,1)}, bf16[2,256,3072]{2,1,0:T(8,128)(2,1...) custom-call(bf16[2,256,3072]{2,1,0:T(8,128)(2,1)} %txt_hbm.1, ...), custom_call_target="tpu_custom_call" | custom-call | tf_op jit(solution)/shard_map/front/pallas_call | solution.py:631
  121.8 340.9 %block.1 = (bf16[4608,3072]{1,0:T(8,128)(2,1)}, bf16[2048,384]{1,0:T(8,128)(2,1)}) custom-call(bf16[2048,384]{1,0:T(8,128)(2,1)} %get-tuple-element.13.o_hbm, bf16[3,128,3072]{2,1,0:T(8,128)(2,1)} %get-tuple-element.14.og_hbm, bf16[9,2304,128]{2,1,0:T(8,128)(2,1)} %get-tuple-element.15.kv_hbm, bf16[2,2048,3072]{2,1,0:T(8,128)(2,1)} %x_hbm.1, ...), custom_call_target="tpu_custom_call" | custom-call | tf_op jit(solution)/shard_map/block/pallas_call | solution.py:1043
  462.7 19.3 %copy_out.1 = (bf16[2,256,3072]{2,1,0:T(8,128)(2,1)}, bf16[2,2048,3072]{2,1,0:T(8,128)(2,1)}) custom-call(bf16[4608,3072]{1,0:T(8,128)(2,1)} %get-tuple-element.21.flat_hbm), custom_call_target="tpu_custom_call" | custom-call | tf_op jit(solution)/shard_map/copy_out/pallas_call | solution.py:1104

commit v6 on v5

--- a/solution.py
+++ b/solution.py
@@ -73,12 +73,15 @@
     return centered * lax.rsqrt(row_mean(centered * centered) + NORM_EPS)
 
 
-def weighted(s, v):
+def softened(s):
     top = jnp.max(s, axis=-1, keepdims=True)
     p = jnp.exp2((s - top) * (HEAD ** -0.5 * LOG2E))
-    total = jnp.sum(p, axis=-1, keepdims=True)
-    o = jnp.dot(p.astype(BF16), v, preferred_element_type=F32)
-    return (o * (1.0 / total)).astype(BF16)
+    return p.astype(BF16), jnp.sum(p, axis=-1, keepdims=True)
+
+
+def weighted(s, v):
+    p, total = softened(s)
+    return (jnp.dot(p, v, preferred_element_type=F32) * (1.0 / total)).astype(BF16)
 
 
 def scores_of(q, k):
@@ -95,8 +98,9 @@
 (T_CORE, T_FIRST, T_SECOND, T_OUT_FIRST, T_OUT_SECOND, T_OUT_RELAY, T_CORE_OWN, T_CORE_FIRST, T_CORE_SECOND, T_CORE_RELAY) = range(10)
 SHARED, COMMON, MISSING = range(3)
 PIECES = 3
-READY = 3
-EARLY = 2
+READY = 4
+EARLY = 4
+FIRST_LATE = 5
 HEADS_HERE = 3
 
 
@@ -133,8 +137,8 @@
 
 
 def front_kernel(cfg, txt_hbm, img_hbm, wt_hbm, wi_hbm, mt_hbm, mi_hbm, pw_hbm, tw_hbm, cond_ref, small_t, small_i, ids_ref, tab_ref,
-                 o_hbm, kv_hbm, wp_hbm, ut_hbm, og_hbm, x1_ref, vec_ref, small_ref,
-                 w, m_w, m_b, m_early, m_late, xs, ua, ub, qkv, s0, s1, s2, o_all, tw, t_send, t_recv, t_own, t_sum, t_rs1, t_rs2_out, t_rs2_in, t_keep, t_x, t_u,
+                 o_hbm, kv_hbm, wp_hbm, ut_hbm, og_hbm, x1_ref, tu_ref, vec_ref, small_ref,
+                 w, m_w, m_b, m_early, m_late, xs, ua, ub, qkv, s0, s1, s2, probs, o_all, tw, t_send, t_recv, t_own, t_sum, t_rs1, t_rs2_out, t_rs2_in, t_keep, t_x, t_u,
                  wsem, msem, xsem, osem, tsem, gsem, psend, precv, tsend, trecv, gsend, grecv, msend, mrecv):
     batch, txt_len, img_len, rows = cfg
     half, quarter, eighth = rows // 2, rows // 4, rows // 8
@@ -200,8 +204,8 @@
                 late_load(c, path).start()
 
     def m_copy(part, d, send):
-        buf = (m_early, m_late)[part]
-        ref = buf.at[me if send else (me + n_dev - d) % n_dev, :8]
+        buf, at = ((m_early, slice(None)), (m_late, slice(FIRST_LATE)), (m_late, slice(FIRST_LATE, 8)))[part]
+        ref = buf.at[me if send else (me + n_dev - d) % n_dev, at]
         return pltpu.make_async_remote_copy(src_ref=ref, dst_ref=ref, send_sem=msend.at[part, d], recv_sem=mrecv.at[part, d], device_id={'tp': (me + d) % n_dev}, device_id_type=MESH)
 
     def m_send(part):
@@ -250,10 +254,10 @@
         acc = jnp.dot(silu, m_w[c % 2], preferred_element_type=F32) + m_b[path, pl.ds(k, 1), :]
         m_late[me, t] = acc.astype(BF16).astype(F32)
 
-    def late_rows():
-        m_wait(1)
+    def late_rows(part):
+        m_wait(1 + part)
         for j in range(n_dev):
-            for c in range(8):
+            for c in range(8)[slice(FIRST_LATE) if part == 0 else slice(FIRST_LATE, 8)]:
                 for b in range(batch):
                     vec_ref[c % 2 * batch + b, pl.ds(GATE1 + c // 2, 1), j * width:(j + 1) * width] = m_late[j, c, b:b + 1, :]
 
@@ -270,6 +274,9 @@
 
     def w_own():
         return remote(psend, precv, W_CORE, SHARED, pw_hbm, wp_hbm.at[me], partner)
+
+    def w_core():
+        w_own().start()
 
     def z_copy(kind, owner, j=SHARED):
         ref = wp_hbm.at[owner, piece_at(j), :]
@@ -305,7 +312,6 @@
     p_copy(W_FIRST, SHARED, me, first).start()
     p_copy(W_SECOND, SHARED, me, second).start()
     p_copy(W_FIRST, COMMON, me, first).start()
-    w_own().start()
 
     even = lax.broadcasted_iota(jnp.int32, (rows, HEAD), 1) % 2 == 0
     code = lax.broadcasted_iota(jnp.int32, (N_IDS, rows), 0)
@@ -316,7 +322,9 @@
         return (1 - img) * n + img * (batch + (n - batch) // per_img)
 
     def norm(n, u):
-        u[...] = modulated(xs[n % 4].astype(F32), vec_ref, select(n), SHIFT1, SCALE1).reshape(u.shape)
+        sel = select(n)
+        for r in range(0, rows, STRIP):
+            u[r // half, r % half:r % half + STRIP, :] = modulated(xs[n % 4, r:r + STRIP, :].astype(F32), vec_ref, sel, SHIFT1, SCALE1)
 
     def heads_of(n, u):
         b, r0 = position(n)
@@ -379,8 +387,8 @@
 
     kv_store = pltpu.make_async_copy(qkv.at[:, total:, :], kv_hbm, tsem.at[0])
 
-    def late_send():
-        m_send(1)
+    def late_send(part):
+        m_send(1 + part)
 
     def kv_send():
         kv_store.start()
@@ -394,7 +402,13 @@
         s[...] = scores_of(rows_of(n, h, rows, position(n)[1]), rows_of(n, heads + h, total, 0))
 
     def weigh(n, h, s):
-        o_all[rows_at(n * rows, rows), h * HEAD:(h + 1) * HEAD] = weighted(s[...], rows_of(n, 2 * heads + h, total, 0))
+        sums = []
+        for r in range(0, rows, STRIP):
+            p, total_p = softened(s[r:r + STRIP, :])
+            sums.append(total_p)
+            probs[r:r + STRIP, :] = p
+        o = jnp.dot(probs[...], rows_of(n, 2 * heads + h, total, 0), preferred_element_type=F32)
+        o_all[rows_at(n * rows, rows), h * HEAD:(h + 1) * HEAD] = (o * (1.0 / jnp.concatenate(sums, axis=0))).astype(BF16)
 
     def t_copy(kind, b, src, dst, dev):
         return remote(tsend, trecv, kind, b, src, dst, dev)
@@ -467,7 +481,11 @@
         branch = t_keep[b] + t_rs2_in[b].astype(F32) + row_of(vec_ref, b, PROJ_B)
         x1 = (t_x[b].astype(F32) + row_of(vec_ref, b, GATE1) * branch).astype(BF16)
         x1_ref[b] = x1
-        t_u[b] = modulated(x1.astype(F32), vec_ref, b, SHIFT2, SCALE2)
+        u = modulated(x1.astype(F32), vec_ref, b, SHIFT2, SCALE2)
+        if b == batch - 1:
+            tu_ref[...] = u
+            return
+        t_u[b] = u
         t_out(T_OUT_FIRST, b, bit1, bit2, first).start()
         t_out(T_OUT_SECOND, b, bit1, bit2, second).start()
         t_out(T_CORE_OWN, b, bit1, bit2, partner).start()
@@ -568,12 +586,11 @@
     run(HOOKS[steps])
     o_out.wait()
     kv_store.wait()
-    for b in range(batch):
-        t_local(b).wait()
-        for kind, b1, b2, dev in ((T_OUT_FIRST, bit1, bit2, first), (T_OUT_SECOND, bit1, bit2, second), (T_OUT_RELAY, not1, bit2, second)):
-            t_out(kind, b, b1, b2, dev).wait_send()
-        for kind, b1, b2 in ((T_CORE_OWN, bit1, bit2), (T_CORE_FIRST, not1, bit2), (T_CORE_SECOND, bit1, not2), (T_CORE_RELAY, not1, not2)):
-            t_out(kind, b, b1, b2, partner).wait()
+    t_local(0).wait()
+    for kind, b1, b2, dev in ((T_OUT_FIRST, bit1, bit2, first), (T_OUT_SECOND, bit1, bit2, second), (T_OUT_RELAY, not1, bit2, second)):
+        t_out(kind, 0, b1, b2, dev).wait_send()
+    for kind, b1, b2 in ((T_CORE_OWN, bit1, bit2), (T_CORE_FIRST, not1, bit2), (T_CORE_SECOND, bit1, not2), (T_CORE_RELAY, not1, not2)):
+        t_out(kind, 0, b1, b2, partner).wait()
     for j in (SHARED, COMMON):
         for kind, owner, dev in ((W_FIRST, me, first), (W_SECOND, me, second), (W_RELAY, first, second)):
             p_copy(kind, j, owner, dev).wait_send()
@@ -594,23 +611,23 @@
     (),
     (),
     (),
+    ('w_relay 0',),
     (),
-    ('w_relay 0', 'w_second 0'),
-    ('w_relay 1',),
-    ('text_partial 0',),
-    ('text_sum 0',),
-    ('gather_start 0',),
+    ('late_send 0', 'w_relay 1'),
+    ('w_core', 'text_partial 0'),
+    ('w_second 0',),
     (),
-    ('gather_send 0',),
-    ('late_send', 'text_quarter 0', 'gather_start 1'),
-    ('kv_send', 'w_last 1', 'gather_send 1'),
-    ('late_rows', 'text_finish 0', 'text_partial 1', 'w_beside 0', 'w_last 0', 'text_sum 1'),
-    (),
-    ('gather_relay 1', 'text_quarter 1', 'gather_start 2', 'gather_send 2', 'text_relay 0'),
-    ('w_beside 1', 'text_finish 1'),
-    ('w_beside 2', 'w_second 1', 'gather_relay 0'),
-    ('text_relay 1', 'gather_relay 2'),
-    ('text_last 1', 'text_last 0'),
+    ('text_sum 0', 'gather_start 1', 'gather_start 0'),
+    ('gather_start 3', 'gather_send 1'),
+    ('gather_send 0', 'gather_start 2'),
+    ('gather_send 3', 'text_quarter 0'),
+    ('late_send 1', 'gather_send 2', 'w_last 0'),
+    ('kv_send', 'late_rows 0', 'gather_relay 3', 'text_finish 0', 'w_second 1', 'gather_relay 1'),
+    ('text_partial 1', 'w_last 1'),
+    ('w_beside 0', 'w_beside 1', 'text_sum 1'),
+    ('text_relay 0',),
+    ('gather_relay 0', 'text_quarter 1', 'gather_relay 2'),
+    ('late_rows 1', 'w_beside 2', 'text_last 0', 'text_finish 1'),
 )
 
 
@@ -631,7 +648,7 @@
     return pl.pallas_call(
         functools.partial(front_kernel, cfg),
         in_specs=[anywhere] * 8 + [vmem, (vmem,) * len(small_t), (vmem,) * len(small_i), vmem, vmem],
-        out_specs=[anywhere] * 5 + [vmem] * 3,
+        out_specs=[anywhere] * 5 + [vmem] * 4,
         out_shape=[
             jax.ShapeDtypeStruct((img_len, width), BF16),
             jax.ShapeDtypeStruct((3 * heads, total, HEAD), BF16),
@@ -639,6 +656,7 @@
             jax.ShapeDtypeStruct((batch, txt_len, dim), BF16),
             jax.ShapeDtypeStruct((READY, half, dim), BF16),
             jax.ShapeDtypeStruct((batch, eighth, dim), BF16),
+            jax.ShapeDtypeStruct((eighth, dim), BF16),
             jax.ShapeDtypeStruct((2 * batch, FC2_B + 1, dim), F32),
             jax.ShapeDtypeStruct((2, FC1_B + 1, dim), F32),
         ],
@@ -655,6 +673,7 @@
             pltpu.VMEM((rows, total), F32),
             pltpu.VMEM((rows, total), F32),
             pltpu.VMEM((rows, total), F32),
+            pltpu.VMEM((rows, total), BF16),
             pltpu.VMEM((batch * txt_len + img_len, width), BF16),
             pltpu.VMEM((width, dim), BF16),
             *tall,
@@ -668,15 +687,15 @@
             *[pltpu.SemaphoreType.DMA((10, PIECES))] * 2,
             *[pltpu.SemaphoreType.DMA((10, batch))] * 2,
             *[pltpu.SemaphoreType.DMA((4, READY))] * 2,
-            pltpu.SemaphoreType.DMA((2, n_dev)),
-            pltpu.SemaphoreType.DMA((2, n_dev)),
+            *[pltpu.SemaphoreType.DMA((3, n_dev))] * 2,
         ],
         compiler_params=pltpu.CompilerParams(collective_id=2, has_side_effects=True, vmem_limit_bytes=VMEM_BYTES),
         name="front",
     )(txt, img, wt, wi, mt, mi, pw, tw, cond, small_t, small_i, ids_t, table)
 
 
-(O_CORE, O_FIRST, O_SECOND, O_RELAY, U_CORE, PART_CORE, RS_FIRST, RS_SECOND, OUT_FIRST, OUT_SECOND, OUT_RELAY, CORE_OWN, CORE_FIRST, CORE_SECOND, CORE_RELAY) = range(15)
+(O_CORE, O_FIRST, O_SECOND, O_RELAY, U_CORE, PART_CORE, RS_FIRST, RS_SECOND, OUT_FIRST, OUT_SECOND, OUT_RELAY, CORE_OWN, CORE_FIRST, CORE_SECOND, CORE_RELAY,
+ U_FIRST, U_SECOND, U_RELAY, U_OWN, U_CORE_FIRST, U_CORE_SECOND, U_CORE_RELAY) = range(22)
 (L_O, L_X, L_OUT) = range(3)
 SLOTS = 4
 O_SLOTS = 7
@@ -687,7 +706,7 @@
     return n % 2
 
 
-def block_kernel(cfg, o_hbm, og_hbm, kv_hbm, x_hbm, ut_hbm, x1t_hbm, wp_hbm, pw_hbm, w1t_hbm, w2t_hbm, w1i_hbm, w2i_hbm, vec_ref, fb_ref, out_hbm, o2_hbm,
+def block_kernel(cfg, o_hbm, og_hbm, kv_hbm, x_hbm, ut_hbm, x1t_hbm, tu_hbm, wp_hbm, pw_hbm, w1t_hbm, w2t_hbm, w1i_hbm, w2i_hbm, vec_ref, fb_ref, out_hbm, o2_hbm,
                  kv, qs, os, wp, w1, w2, obuf, xbuf, x1buf, x1keep, u2, hid, psend, precv, own, chip_sum, rs1, keep2, rs2_out, rs2_in, outb,
                  asem, wsem, lsem, tsem, ssem, rsem):
     batch, txt_chunks, img_chunks, per_img, rows, tile = cfg
@@ -808,10 +827,48 @@
     def out_local(g):
         return pltpu.make_async_copy(outb.at[g % SLOTS], out_ref(g, bit1, bit2), lsem.at[L_OUT, g % SEMS])
 
+    last_txt = txt_chunks - 1
+
     def txt_load(g):
-        b, r0 = g // per_txt, (g % per_txt) * rows
-        return (pltpu.make_async_copy(ut_hbm.at[b, rows_at(r0, rows), :], u2.at[two(g)], tsem.at[0, two(g)]),
-                pltpu.make_async_copy(x1t_hbm.at[g], x1keep.at[g % SLOTS], tsem.at[1, two(g)]))
+        return pltpu.make_async_copy(ut_hbm.at[g], u2.at[two(g)], tsem.at[0, g])
+
+    def x1_load(g):
+        return pltpu.make_async_copy(x1t_hbm.at[g], x1keep.at[g], tsem.at[1, g])
+
+    def u_rows(b1, b2):
+        return u2.at[two(last_txt), pl.ds(own_rows(b1, b2), eighth), :]
+
+    def u_local():
+        return pltpu.make_async_copy(tu_hbm, u_rows(bit1, bit2), tsem.at[0, last_txt])
+
+    def u_send(kind, b1, b2, dev):
+        ref = u_rows(b1, b2)
+        return remote(kind, last_txt, tu_hbm if kind in (U_FIRST, U_SECOND, U_OWN) else ref, ref, dev)
+
+    def u_start():
+        u_local().start()
+        u_send(U_FIRST, bit1, bit2, first).start()
+        u_send(U_SECOND, bit1, bit2, second).start()
+        u_send(U_OWN, bit1, bit2, partner).start()
+
+    def u_relay():
+        u_send(U_FIRST, not1, bit2, first).wait_recv()
+        u_send(U_RELAY, not1, bit2, second).start()
+        u_send(U_CORE_FIRST, not1, bit2, partner).start()
+        u_send(U_SECOND, bit1, not2, second).wait_recv()
+        u_send(U_CORE_SECOND, bit1, not2, partner).start()
+
+    def u_last():
+        u_send(U_RELAY, not1, not2, second).wait_recv()
+        u_send(U_CORE_RELAY, not1, not2, partner).start()
+
+    def u_wait():
+        u_local().wait()
+        u_send(U_FIRST, bit1, bit2, first).wait_send()
+        u_send(U_SECOND, bit1, bit2, second).wait_send()
+        u_send(U_RELAY, not1, bit2, second).wait_send()
+        for kind, b1, b2 in ((U_OWN, bit1, bit2), (U_CORE_FIRST, not1, bit2), (U_CORE_SECOND, bit1, not2), (U_CORE_RELAY, not1, not2)):
+            u_send(kind, b1, b2, partner).wait()
 
     def w_load(k, src, dst):
         return pltpu.make_async_copy(src, dst, wsem.at[k])
@@ -887,10 +944,17 @@
         x1keep[slot] = x1buf[rows_at(bit1 * quarter + bit2 * eighth, eighth), :]
 
     def mlp_hidden(g):
+        @pl.when(g < last_txt)
+        def _():
+            txt_load(g).wait()
+
+        @pl.when(g == last_txt)
+        def _():
+            u_wait()
+
         @pl.when(g < txt_chunks)
         def _():
-            for copy in txt_load(g):
-                copy.wait()
+            x1_load(g).wait()
 
         @pl.when(g >= txt_chunks)
         def _():
@@ -992,15 +1056,16 @@
         out_send(CORE_SECOND, g, bit1, not2, partner).wait()
         out_send(CORE_RELAY, g, not1, not2, partner).wait()
 
+    u_start()
     opened = txt_chunks + O_SLOTS - 1
     for g in range(txt_chunks, opened):
         start_o(jnp.int32(g))
     w_load(0, w1t_hbm, w1).start()
     w_load(1, w2t_hbm, w2).start()
     for g in range(txt_chunks):
-        for copy in txt_load(g):
-            copy.start()
-
+        x1_load(g).start()
+        if g < last_txt:
+            txt_load(g).start()
     kv_load().start()
     q_load(0).start()
     for g in range(first_open, opened):
@@ -1012,6 +1077,10 @@
     least = min(ahead for _, ahead, _ in stages)
 
     def step(i):
+        @pl.when(i == U_RELAY_STEP)
+        def _():
+            u_relay()
+
         for stage, ahead, lowest in stages:
             if stage is attend_pair:
                 g, lowest, highest = i - ATTEND_FROM, 0, units // 2
@@ -1022,13 +1091,18 @@
             def _():
                 stage(g)
 
+        @pl.when(i == U_RELAY_STEP + 1)
+        def _():
+            u_last()
+
     loop(total - txt_chunks + most - least, step)
 
 
 ATTEND_FROM = 3
-
-
-def block_call(img_o, og, kv, x, u_txt, x1_txt, wp, pw, w1t, w2t, w1i, w2i, vecs, fb, rows):
+U_RELAY_STEP = 2
+
+
+def block_call(img_o, og, kv, x, u_txt, x1_txt, tu, wp, pw, w1t, w2t, w1i, w2i, vecs, fb, rows):
     batch, img_len, dim = x.shape
     txt_len = u_txt.shape[1]
     ff = w1t.shape[1]
@@ -1042,7 +1116,7 @@
     anywhere = pl.BlockSpec(memory_space=pl.ANY)
     return pl.pallas_call(
         functools.partial(block_kernel, cfg),
-        in_specs=[anywhere] * 12 + [pl.BlockSpec(memory_space=pltpu.VMEM)] * 2,
+        in_specs=[anywhere] * 13 + [pl.BlockSpec(memory_space=pltpu.VMEM)] * 2,
         out_specs=[anywhere, anywhere],
         out_shape=[jax.ShapeDtypeStruct((total * rows, dim), BF16), jax.ShapeDtypeStruct(img_o.shape, BF16)],
         scratch_shapes=[
@@ -1071,12 +1145,11 @@
             pltpu.SemaphoreType.DMA((10,)),
             pltpu.SemaphoreType.DMA((3, SEMS)),
             pltpu.SemaphoreType.DMA((2, 2)),
-            pltpu.SemaphoreType.DMA((15, SEMS)),
-            pltpu.SemaphoreType.DMA((15, SEMS)),
+            *[pltpu.SemaphoreType.DMA((22, SEMS))] * 2,
         ],
         compiler_params=pltpu.CompilerParams(collective_id=0, has_side_effects=True, vmem_limit_bytes=VMEM_BYTES),
         name="block",
-    )(img_o, og, kv, x, u_txt, x1_txt, wp, pw, w1t, w2t, w1i, w2i, vecs, fb)
+    )(img_o, og, kv, x, u_txt, x1_txt, tu, wp, pw, w1t, w2t, w1i, w2i, vecs, fb)
 
 
 def copy_kernel(pieces, flat_hbm, *rest):
@@ -1129,8 +1202,8 @@
 
     table = jnp.asarray(rope_table())
     ids_t = jnp.transpose(ids, (2, 0, 1))
-    o, kv, proj_w, txt_u, og, txt_x1, vecs, small = front_call(txt, img, by_kind(txt_w[2]), by_kind(img_w[2]), by_kind(txt_w[0]), by_kind(img_w[0]), img_w[6], txt_w[6], vec, small_of(txt_w), small_of(img_w), ids_t, table, n_dev, rows)
-    flat, _ = block_call(o, og, kv, img, txt_u, txt_x1, proj_w, img_w[6], txt_w[8], txt_w[10], img_w[8], img_w[10], vecs, small, rows)
+    o, kv, proj_w, txt_u, og, txt_x1, txt_tu, vecs, small = front_call(txt, img, by_kind(txt_w[2]), by_kind(img_w[2]), by_kind(txt_w[0]), by_kind(img_w[0]), img_w[6], txt_w[6], vec, small_of(txt_w), small_of(img_w), ids_t, table, n_dev, rows)
+    flat, _ = block_call(o, og, kv, img, txt_u, txt_x1, txt_tu, proj_w, img_w[6], txt_w[8], txt_w[10], img_w[8], img_w[10], vecs, small, rows)
     txt_out, img_out = copy_call(flat, (txt.shape, img.shape), rows)
     return img_out, txt_out
 

time: 482 us -> 477 us (0.990)
  Pallas kernels: 481 us -> 476 us
    pallas_call x1, Pallas kernels: 121 us -> 112 us  [front_call(): pl.pallas_call(functools.partial(front_kernel, cfg), in_specs=[anywhere]...]
where the time goes in v6:
time: 477 us; the launch traced here: 476 us
  Pallas kernels  476 us (100%)
    pallas_call x1, Pallas kernels, block_call(): pl.pallas_call(functools.partial(block_kernel, cfg), in_specs=[anywhere]...  344 us
    pallas_call x1, Pallas kernels, front_call(): pl.pallas_call(functools.partial(front_kernel, cfg), in_specs=[anywhere]...  112 us
    pallas_call x1, Pallas kernels, copy_call(): pl.pallas_call(functools.partial(copy_kernel, pieces), in_specs=[anywhere...  19.3 us

profile of v6, /device:TPU:0, one launch (start us, length us, event | category | flops | bytes accessed | tf_op | source)
XLA Modules:
  0.0 476.3 jit_solution(7205312825574821384)
XLA Ops:
  0.6 112.3 %front.1 = (bf16[2048,384]{1,0:T(8,128)(2,1)}, bf16[9,2304,128]{2,1,0:T(8,128)(2,1)}, bf16[8,384,3072]{2,1,0:T(8,128)(2,1)}, bf16[2,256,3072]{2,1,0:T(8,128)(2,1...) custom-call(bf16[2,256,3072]{2,1,0:T(8,128)(2,1)} %txt_hbm.1, ...), custom_call_target="tpu_custom_call" | custom-call | tf_op jit(solution)/shard_map/front/pallas_call | solution.py:648
  112.9 344.0 %block.1 = (bf16[4608,3072]{1,0:T(8,128)(2,1)}, bf16[2048,384]{1,0:T(8,128)(2,1)}) custom-call(bf16[2048,384]{1,0:T(8,128)(2,1)} %get-tuple-element.14.o_hbm, bf16[4,128,3072]{2,1,0:T(8,128)(2,1)} %get-tuple-element.15.og_hbm, bf16[9,2304,128]{2,1,0:T(8,128)(2,1)} %get-tuple-element.16.kv_hbm, bf16[2,2048,3072]{2,1,0:T(8,128)(2,1)} %x_hbm.1, ...), custom_call_target="tpu_custom_call" | custom-call | tf_op jit(solution)/shard_map/block/pallas_call | solution.py:1117
  456.9 19.3 %copy_out.1 = (bf16[2,256,3072]{2,1,0:T(8,128)(2,1)}, bf16[2,2048,3072]{2,1,0:T(8,128)(2,1)}) custom-call(bf16[4608,3072]{1,0:T(8,128)(2,1)} %get-tuple-element.23.flat_hbm), custom_call_target="tpu_custom_call" | custom-call | tf_op jit(solution)/shard_map/copy_out/pallas_call | solution.py:1177

commit v7 on v6

--- a/solution.py
+++ b/solution.py
@@ -698,8 +698,9 @@
  U_FIRST, U_SECOND, U_RELAY, U_OWN, U_CORE_FIRST, U_CORE_SECOND, U_CORE_RELAY) = range(22)
 (L_O, L_X, L_OUT) = range(3)
 SLOTS = 4
-O_SLOTS = 7
-SEMS = 8
+O_SLOTS = 10
+OPENED = 1
+SEMS = 12
 
 
 def two(n):
@@ -707,7 +708,7 @@
 
 
 def block_kernel(cfg, o_hbm, og_hbm, kv_hbm, x_hbm, ut_hbm, x1t_hbm, tu_hbm, wp_hbm, pw_hbm, w1t_hbm, w2t_hbm, w1i_hbm, w2i_hbm, vec_ref, fb_ref, out_hbm, o2_hbm,
-                 kv, qs, os, wp, w1, w2, obuf, xbuf, x1buf, x1keep, u2, hid, psend, precv, own, chip_sum, rs1, keep2, rs2_out, rs2_in, outb,
+                 kv, qs, os, wp, w1, w2, obuf, xbuf, x1keep, u2, hid, psend, precv, own, chip_sum, rs1, keep2, rs2_out, rs2_in, outb,
                  asem, wsem, lsem, tsem, ssem, rsem):
     batch, txt_chunks, img_chunks, per_img, rows, tile = cfg
     half, quarter, eighth = rows // 2, rows // 4, rows // 8
@@ -765,7 +766,11 @@
     def kv_load():
         return pltpu.make_async_copy(kv_hbm.at[heads:], kv, asem.at[4])
 
-    def attend(u):
+    def attend(u, carry):
+        @pl.when(u == 0)
+        def _():
+            kv_load().wait()
+
         q_load(u).wait()
 
         @pl.when(u + 1 < units)
@@ -782,18 +787,14 @@
             os[two(u), r:r + half, :] = weighted(scores_of(qs[two(u), r:r + half, :], k), v)
         o_store(u).start()
 
-    def attend_pair(i):
-        @pl.when(i == 0)
-        def _():
-            kv_load().wait()
-
-        attend(2 * i)
-        attend(2 * i + 1)
-
-        @pl.when(i == units // 2 - 1)
-        def _():
-            o_store(units - 2).wait()
-            o_store(units - 1).wait()
+        @pl.when(u == units - 1)
+        def _():
+            o_store(u - 1).wait()
+            o_store(u).wait()
+        return carry
+
+    def attended(i):
+        return sum(count * (i > n).astype(jnp.int32) for n, count in enumerate(ATTEND) if count)
 
     def o_send(kind, g, owner, dev):
         ref = obuf.at[g % O_SLOTS, :, chip_cols(owner)]
@@ -804,8 +805,7 @@
         return pltpu.make_async_copy(x_hbm.at[b, rows_at(r0 + core * half, half), :], xbuf.at[two(g)], lsem.at[L_X, g % SEMS])
 
     def u_core(g):
-        ref = u2.at[two(g), rows_at(core * half, half), :]
-        return remote(U_CORE, g, ref, ref, partner)
+        return remote(U_CORE, g, u2.at[two(g), :half, :], u2.at[two(g), half:, :], partner)
 
     def part_core(g):
         return remote(PART_CORE, g, psend, precv.at[two(g)], partner)
@@ -829,21 +829,22 @@
 
     last_txt = txt_chunks - 1
 
-    def txt_load(g):
-        return pltpu.make_async_copy(ut_hbm.at[g], u2.at[two(g)], tsem.at[0, g])
+    def txt_load(g, who):
+        mine = who is core
+        return pltpu.make_async_copy(ut_hbm.at[g, rows_at(who * half, half), :], u2.at[two(g), slice(half) if mine else slice(half, rows), :], tsem.at[0 if mine else 2, g])
 
     def x1_load(g):
         return pltpu.make_async_copy(x1t_hbm.at[g], x1keep.at[g], tsem.at[1, g])
 
-    def u_rows(b1, b2):
-        return u2.at[two(last_txt), pl.ds(own_rows(b1, b2), eighth), :]
+    def u_rows(b1, b2, base=0):
+        return u2.at[two(last_txt), rows_at(base + b1 * quarter + b2 * eighth, eighth), :]
 
     def u_local():
         return pltpu.make_async_copy(tu_hbm, u_rows(bit1, bit2), tsem.at[0, last_txt])
 
     def u_send(kind, b1, b2, dev):
-        ref = u_rows(b1, b2)
-        return remote(kind, last_txt, tu_hbm if kind in (U_FIRST, U_SECOND, U_OWN) else ref, ref, dev)
+        src = tu_hbm if kind in (U_FIRST, U_SECOND, U_OWN) else u_rows(b1, b2)
+        return remote(kind, last_txt, src, u_rows(b1, b2, 0 if dev is not partner else half), dev)
 
     def u_start():
         u_local().start()
@@ -904,6 +905,8 @@
     def start_x(g):
         x_load(g).start()
 
+    wide = 2 * tile
+
     def project(g):
         @pl.when(g < first_open)
         def _():
@@ -928,25 +931,26 @@
         slot = g % SLOTS
 
         def columns(n):
-            at = rows_at(n * tile, tile)
+            at = rows_at(n * wide, wide)
             acc = jnp.dot(obuf[g % O_SLOTS], wp[:, at], preferred_element_type=F32)
             branch = acc + row_of(vec_ref, sel, PROJ_B, at)
-            x1buf[:, at] = (xbuf[two(g), :, at].astype(F32) + row_of(vec_ref, sel, GATE1, at) * branch).astype(BF16)
-
-        loop(dim // tile, columns)
+            xbuf[two(g), :, at] = (xbuf[two(g), :, at].astype(F32) + row_of(vec_ref, sel, GATE1, at) * branch).astype(BF16)
+
+        loop(dim // wide, columns)
 
         def norm(n):
             at = rows_at(n * STRIP, STRIP)
-            u2[two(g), rows_at(core * half + n * STRIP, STRIP), :] = modulated(x1buf[at, :].astype(F32), vec_ref, sel, SHIFT2, SCALE2)
+            u2[two(g), at, :] = modulated(xbuf[two(g), at, :].astype(F32), vec_ref, sel, SHIFT2, SCALE2)
 
         loop(half // STRIP, norm)
         u_core(g).start()
-        x1keep[slot] = x1buf[rows_at(bit1 * quarter + bit2 * eighth, eighth), :]
+        x1keep[slot] = xbuf[two(g), rows_at(bit1 * quarter + bit2 * eighth, eighth), :]
 
     def mlp_hidden(g):
         @pl.when(g < last_txt)
         def _():
-            txt_load(g).wait()
+            for who in (core, far):
+                txt_load(g, who).wait()
 
         @pl.when(g == last_txt)
         def _():
@@ -988,26 +992,22 @@
 
         loop(ff // tile, hidden)
 
-    def mlp_theirs(g):
-        def theirs(n):
+    def mlp_out(g):
+        def columns(n):
             at = rows_at(n * tile, tile)
-            psend[:, at] = jnp.dot(hid[rows_at(far * half, half), :], w2[:, at], preferred_element_type=F32).astype(BF16)
-
-        loop(dim // tile, theirs)
+            acc = jnp.dot(hid[...], w2[:, at], preferred_element_type=F32)
+            own[:, at] = acc[:half]
+            psend[:, at] = acc[half:].astype(BF16)
+
+        loop(dim // tile, columns)
         part_core(g).start()
-
-    def mlp_mine(g):
-        def mine(n):
-            at = rows_at(n * tile, tile)
-            own[:, at] = jnp.dot(hid[rows_at(core * half, half), :], w2[:, at], preferred_element_type=F32)
-
-        loop(dim // tile, mine)
 
         @pl.when(g == txt_chunks - 1)
         def _():
             w_load(0, w1i_hbm, w1).start()
             w_load(1, w2i_hbm, w2).start()
 
+    def mlp_sum(g):
         part_core(g).wait()
 
         def add(n):
@@ -1057,7 +1057,7 @@
         out_send(CORE_RELAY, g, not1, not2, partner).wait()
 
     u_start()
-    opened = txt_chunks + O_SLOTS - 1
+    opened = first_open + OPENED
     for g in range(txt_chunks, opened):
         start_o(jnp.int32(g))
     w_load(0, w1t_hbm, w1).start()
@@ -1065,14 +1065,15 @@
     for g in range(txt_chunks):
         x1_load(g).start()
         if g < last_txt:
-            txt_load(g).start()
+            for who in (core, far):
+                txt_load(g, who).start()
     kv_load().start()
     q_load(0).start()
     for g in range(first_open, opened):
         send_o(jnp.int32(g))
 
-    stages = ((second_out, -5, 0), (attend_pair, 0, 0), (mlp_hidden, 0, 0), (start_o, 5, opened), (relay_o, 4, first_open), (start_x, 2, txt_chunks), (relay_out, -4, 0), (mlp_theirs, 0, 0),
-              (send_o, 5, opened), (add_first, -1, 0), (mlp_mine, 0, 0), (relay_core, -6, 0), (project, 1, txt_chunks), (drain, -6, 0), (finish, -2, 0))
+    stages = ((finish, -3, 0), (start_o, 8, opened), (relay_out, -4, 0), (mlp_hidden, 0, 0), (send_o, 8, opened), (relay_core, -6, 0), (mlp_out, 0, 0), (relay_o, 7, first_open),
+              (start_x, 2, txt_chunks), (project, 1, txt_chunks), (second_out, -4, 0), (add_first, -1, 0), (mlp_sum, 0, 0), (drain, -6, 0), (attend, 0, 0))
     most = max(ahead for _, ahead, _ in stages)
     least = min(ahead for _, ahead, _ in stages)
 
@@ -1082,12 +1083,12 @@
             u_relay()
 
         for stage, ahead, lowest in stages:
-            if stage is attend_pair:
-                g, lowest, highest = i - ATTEND_FROM, 0, units // 2
-            else:
-                g, highest = i + txt_chunks - most + ahead, total
-
-            @pl.when((g >= lowest) & (g < highest))
+            if stage is attend:
+                lax.fori_loop(attended(i), attended(i + 1), attend, 0)
+                continue
+            g = i + txt_chunks - most + ahead
+
+            @pl.when((g >= lowest) & (g < total))
             def _():
                 stage(g)
 
@@ -1098,7 +1099,7 @@
     loop(total - txt_chunks + most - least, step)
 
 
-ATTEND_FROM = 3
+ATTEND = (2, 2, 2, 0, 0, 0, 0, 1, 2, 2, 3, 3, 3, 3, 1)
 U_RELAY_STEP = 2
 
 
@@ -1128,7 +1129,6 @@
             pltpu.VMEM((ff, dim), BF16),
             pltpu.VMEM((O_SLOTS, half, dim), BF16),
             pltpu.VMEM((2, half, dim), BF16),
-            pltpu.VMEM((half, dim), BF16),
             pltpu.VMEM((SLOTS, eighth, dim), BF16),
             pltpu.VMEM((2, rows, dim), BF16),
             pltpu.VMEM((rows, ff), BF16),
@@ -1144,7 +1144,7 @@
             pltpu.SemaphoreType.DMA((5,)),
             pltpu.SemaphoreType.DMA((10,)),
             pltpu.SemaphoreType.DMA((3, SEMS)),
-            pltpu.SemaphoreType.DMA((2, 2)),
+            pltpu.SemaphoreType.DMA((3, 2)),
             *[pltpu.SemaphoreType.DMA((22, SEMS))] * 2,
         ],
         compiler_params=pltpu.CompilerParams(collective_id=0, has_side_effects=True, vmem_limit_bytes=VMEM_BYTES),

time: 477 us -> 466 us (0.977)
  Pallas kernels: 476 us -> 465 us
    pallas_call x1, Pallas kernels: 344 us -> 333 us  [block_call(): pl.pallas_call(functools.partial(block_kernel, cfg), in_specs=[anywhere]...]
where the time goes in v7:
time: 466 us
  Pallas kernels  465 us (100%)
    pallas_call x1, Pallas kernels, block_call(): pl.pallas_call(functools.partial(block_kernel, cfg), in_specs=[anywhere]...  333 us
    pallas_call x1, Pallas kernels, front_call(): pl.pallas_call(functools.partial(front_kernel, cfg), in_specs=[anywhere]...  112 us
    pallas_call x1, Pallas kernels, copy_call(): pl.pallas_call(functools.partial(copy_kernel, pieces), in_specs=[anywhere...  19.3 us

profile of v7, /device:TPU:0, one launch (start us, length us, event | category | flops | bytes accessed | tf_op | source)
XLA Modules:
  0.0 465.8 jit_solution(15169774667118329544)
XLA Ops:
  0.6 112.3 %front.1 = (bf16[2048,384]{1,0:T(8,128)(2,1)}, bf16[9,2304,128]{2,1,0:T(8,128)(2,1)}, bf16[8,384,3072]{2,1,0:T(8,128)(2,1)}, bf16[2,256,3072]{2,1,0:T(8,128)(2,1...) custom-call(bf16[2,256,3072]{2,1,0:T(8,128)(2,1)} %txt_hbm.1, ...), custom_call_target="tpu_custom_call" | custom-call | tf_op jit(solution)/shard_map/front/pallas_call | solution.py:648
  112.9 333.5 %block.1 = (bf16[4608,3072]{1,0:T(8,128)(2,1)}, bf16[2048,384]{1,0:T(8,128)(2,1)}) custom-call(bf16[2048,384]{1,0:T(8,128)(2,1)} %get-tuple-element.14.o_hbm, bf16[4,128,3072]{2,1,0:T(8,128)(2,1)} %get-tuple-element.15.og_hbm, bf16[9,2304,128]{2,1,0:T(8,128)(2,1)} %get-tuple-element.16.kv_hbm, bf16[2,2048,3072]{2,1,0:T(8,128)(2,1)} %x_hbm.1, ...), custom_call_target="tpu_custom_call" | custom-call | tf_op jit(solution)/shard_map/block/pallas_call | solution.py:1118
  446.4 19.3 %copy_out.1 = (bf16[2,256,3072]{2,1,0:T(8,128)(2,1)}, bf16[2,2048,3072]{2,1,0:T(8,128)(2,1)}) custom-call(bf16[4608,3072]{1,0:T(8,128)(2,1)} %get-tuple-element.23.flat_hbm), custom_call_target="tpu_custom_call" | custom-call | tf_op jit(solution)/shard_map/copy_out/pallas_call | solution.py:1177

commit v8 on v7

--- a/solution.py
+++ b/solution.py
@@ -96,10 +96,10 @@
 (W_FIRST, W_SECOND, W_RELAY, W_CORE, W_CORE_FIRST, W_CORE_SECOND, W_CORE_RELAY, Z_FIRST, Z_SECOND, Z_RELAY) = range(10)
 (G_CORE, G_FIRST, G_SECOND, G_RELAY) = range(4)
 (T_CORE, T_FIRST, T_SECOND, T_OUT_FIRST, T_OUT_SECOND, T_OUT_RELAY, T_CORE_OWN, T_CORE_FIRST, T_CORE_SECOND, T_CORE_RELAY) = range(10)
-SHARED, COMMON, MISSING = range(3)
-PIECES = 3
-READY = 4
-EARLY = 4
+PIECES = 4
+SHARED = range(2)
+READY = 5
+EARLY = 5
 FIRST_LATE = 5
 HEADS_HERE = 3
 
@@ -191,8 +191,11 @@
     def w_load(path, j):
         return pltpu.make_async_copy((wt_hbm, wi_hbm)[path].at[j], w_columns(path, j), wsem.at[path, j])
 
+    def early_place(path, k):
+        return m_w.at[k] if path == 0 else w_columns(path, k)
+
     def early_load(path, k):
-        return pltpu.make_async_copy((mt_hbm, mi_hbm)[path].at[k], w_columns(path, k), wsem.at[path, k])
+        return pltpu.make_async_copy((mt_hbm, mi_hbm)[path].at[k], early_place(path, k), (msem if path == 0 else wsem.at[path]).at[k])
 
     def late_load(c, path):
         return pltpu.make_async_copy((mt_hbm, mi_hbm)[path].at[GATE1 + c // 2], m_w.at[c % 2], msem.at[c % 2])
@@ -222,6 +225,8 @@
             early_load(path, k).start()
     for n in range(3):
         x_copy(n, 0 if n < batch else 1).start()
+    for j in range(3):
+        w_load(0, j).start()
     v = cond_ref[...].astype(F32)
     silu = (v * (1.0 / (1.0 + jnp.exp(-v)))).astype(BF16)
     for path, (mod_b, qkv_b, q_gain, k_gain, proj_b, fc1_b, fc2_b) in enumerate((small_t, small_i)):
@@ -239,13 +244,11 @@
 
     def early_chunk(k, path):
         early_load(path, k).wait()
-        acc = jnp.dot(silu, w_columns(path, k)[...], preferred_element_type=F32)
+        acc = jnp.dot(silu, early_place(path, k)[...], preferred_element_type=F32)
         return (acc + m_b[path, k:k + 1, :]).astype(BF16)
 
     m_early[me] = jnp.concatenate([early_chunk(k, path) for k in (SHIFT1, SCALE1) for path in PATHS], axis=0)
     m_send(0)
-    for j in range(3):
-        w_load(0, j).start()
     tw_load = pltpu.make_async_copy(tw_hbm, tw, tsem.at[1])
 
     def late_chunk(t):
@@ -262,7 +265,7 @@
                     vec_ref[c % 2 * batch + b, pl.ds(GATE1 + c // 2, 1), j * width:(j + 1) * width] = m_late[j, c, b:b + 1, :]
 
     def piece_at(j):
-        return rows_at(((1 - j) * (2 * odd - 1) + 1) * piece, piece)
+        return rows_at((j + 2 * odd) % PIECES * piece, piece)
 
     def remote(sends, recvs, kind, j, src, dst, dev):
         return pltpu.make_async_remote_copy(src_ref=src, dst_ref=dst, send_sem=sends.at[kind, j], recv_sem=recvs.at[kind, j], device_id=ident(dev), device_id_type=MESH)
@@ -273,45 +276,44 @@
         return remote(psend, precv, kind, j, src, dst, dev)
 
     def w_own():
-        return remote(psend, precv, W_CORE, SHARED, pw_hbm, wp_hbm.at[me], partner)
+        return remote(psend, precv, W_CORE, 0, pw_hbm, wp_hbm.at[me], partner)
 
     def w_core():
         w_own().start()
 
-    def z_copy(kind, owner, j=SHARED):
-        ref = wp_hbm.at[owner, piece_at(j), :]
-        return remote(psend, precv, kind, SHARED, ref, ref, beside)
+    def z_copy(kind, owner, j, at):
+        ref = wp_hbm.at[owner, piece_at(at), :]
+        return remote(psend, precv, kind, j, ref, ref, beside)
 
     def w_relay(j):
         p_copy(W_FIRST, j, first, first).wait_recv()
         p_copy(W_RELAY, j, first, second).start()
         p_copy(W_CORE_FIRST, j, first, partner).start()
-        if j == SHARED:
-            p_copy(W_SECOND, COMMON, me, second).start()
-            z_copy(Z_FIRST, first).start()
+        z_copy(Z_FIRST, first, j, j).start()
+        if j == 0:
+            p_copy(W_SECOND, 1, me, second).start()
 
     def w_second(j):
         p_copy(W_SECOND, j, second, second).wait_recv()
         p_copy(W_CORE_SECOND, j, second, partner).start()
-        if j == SHARED:
-            z_copy(Z_SECOND, second).start()
+        z_copy(Z_SECOND, second, j, j).start()
 
     def w_last(j):
         p_copy(W_RELAY, j, diagonal, second).wait_recv()
         p_copy(W_CORE_RELAY, j, diagonal, partner).start()
-        if j == SHARED:
-            z_copy(Z_RELAY, diagonal).start()
+        z_copy(Z_RELAY, diagonal, j, j).start()
 
     from_beside = ((Z_FIRST, first, W_CORE_FIRST), (Z_SECOND, second, W_CORE_SECOND), (Z_RELAY, diagonal, W_CORE_RELAY))
 
     def w_beside(n):
-        kind, owner, core_kind = from_beside[n]
-        z_copy(kind, owner, MISSING).wait_recv()
-        p_copy(core_kind, MISSING, owner, partner).start()
-
-    p_copy(W_FIRST, SHARED, me, first).start()
-    p_copy(W_SECOND, SHARED, me, second).start()
-    p_copy(W_FIRST, COMMON, me, first).start()
+        kind, owner, core_kind = from_beside[n % 3]
+        j = n // 3
+        z_copy(kind, owner, j, j + 2).wait_recv()
+        p_copy(core_kind, j + 2, owner, partner).start()
+
+    p_copy(W_FIRST, 0, me, first).start()
+    p_copy(W_SECOND, 0, me, second).start()
+    p_copy(W_FIRST, 1, me, first).start()
 
     even = lax.broadcasted_iota(jnp.int32, (rows, HEAD), 1) % 2 == 0
     code = lax.broadcasted_iota(jnp.int32, (N_IDS, rows), 0)
@@ -399,16 +401,18 @@
         return qkv[c, rows_at(position(n)[0] * total + r0, size), :]
 
     def scores(n, h, s):
-        s[...] = scores_of(rows_of(n, h, rows, position(n)[1]), rows_of(n, heads + h, total, 0))
+        s[...] = scores_of(rows_of(n, heads + h, total, 0), rows_of(n, h, rows, position(n)[1]))
 
     def weigh(n, h, s):
-        sums = []
-        for r in range(0, rows, STRIP):
-            p, total_p = softened(s[r:r + STRIP, :])
-            sums.append(total_p)
-            probs[r:r + STRIP, :] = p
-        o = jnp.dot(probs[...], rows_of(n, 2 * heads + h, total, 0), preferred_element_type=F32)
-        o_all[rows_at(n * rows, rows), h * HEAD:(h + 1) * HEAD] = (o * (1.0 / jnp.concatenate(sums, axis=0))).astype(BF16)
+        top = jnp.max(s[...], axis=0, keepdims=True)
+        keys = total // 9
+        sums = 0.0
+        for r in range(0, total, keys):
+            p = jnp.exp2((s[r:r + keys, :] - top) * (HEAD ** -0.5 * LOG2E))
+            sums += jnp.sum(p, axis=0, keepdims=True)
+            probs[r:r + keys, :] = p.astype(BF16)
+        o = lax.dot_general(rows_of(n, 2 * heads + h, total, 0), probs[...], (((0,), (0,)), ((), ())), preferred_element_type=F32)
+        o_all[rows_at(n * rows, rows), h * HEAD:(h + 1) * HEAD] = (o * (1.0 / sums)).T.astype(BF16)
 
     def t_copy(kind, b, src, dst, dev):
         return remote(tsend, trecv, kind, b, src, dst, dev)
@@ -591,12 +595,13 @@
         t_out(kind, 0, b1, b2, dev).wait_send()
     for kind, b1, b2 in ((T_CORE_OWN, bit1, bit2), (T_CORE_FIRST, not1, bit2), (T_CORE_SECOND, bit1, not2), (T_CORE_RELAY, not1, not2)):
         t_out(kind, 0, b1, b2, partner).wait()
-    for j in (SHARED, COMMON):
+    for j in SHARED:
         for kind, owner, dev in ((W_FIRST, me, first), (W_SECOND, me, second), (W_RELAY, first, second)):
             p_copy(kind, j, owner, dev).wait_send()
     w_own().wait()
     for kind, owner, core_kind in from_beside:
-        z_copy(kind, owner).wait_send()
+        for j in SHARED:
+            z_copy(kind, owner, j, j).wait_send()
         for j in range(PIECES):
             p_copy(core_kind, j, owner, partner).wait()
     for m in range(READY):
@@ -610,24 +615,24 @@
 HOOKS = (
     (),
     (),
-    (),
     ('w_relay 0',),
     (),
-    ('late_send 0', 'w_relay 1'),
-    ('w_core', 'text_partial 0'),
-    ('w_second 0',),
-    (),
-    ('text_sum 0', 'gather_start 1', 'gather_start 0'),
-    ('gather_start 3', 'gather_send 1'),
-    ('gather_send 0', 'gather_start 2'),
-    ('gather_send 3', 'text_quarter 0'),
-    ('late_send 1', 'gather_send 2', 'w_last 0'),
-    ('kv_send', 'late_rows 0', 'gather_relay 3', 'text_finish 0', 'w_second 1', 'gather_relay 1'),
-    ('text_partial 1', 'w_last 1'),
-    ('w_beside 0', 'w_beside 1', 'text_sum 1'),
-    ('text_relay 0',),
-    ('gather_relay 0', 'text_quarter 1', 'gather_relay 2'),
-    ('late_rows 1', 'w_beside 2', 'text_last 0', 'text_finish 1'),
+    ('w_relay 1',),
+    ('late_send 0',),
+    ('text_partial 0',),
+    ('text_sum 0', 'w_last 1', 'gather_start 0'),
+    ('w_last 0', 'gather_start 1'),
+    ('w_beside 0', 'gather_send 0'),
+    ('gather_start 2', 'gather_start 3', 'gather_send 1'),
+    ('w_second 0', 'text_quarter 0', 'gather_start 4'),
+    ('gather_send 3', 'gather_send 2'),
+    ('gather_relay 1', 'gather_send 4'),
+    ('late_send 1', 'w_beside 2', 'gather_relay 0'),
+    ('kv_send', 'late_rows 0', 'gather_relay 4', 'w_second 1', 'w_beside 5', 'text_finish 0'),
+    ('text_partial 1', 'gather_relay 2', 'text_sum 1'),
+    ('w_beside 1', 'text_relay 0', 'w_beside 3', 'gather_relay 3', 'w_core'),
+    ('text_quarter 1', 'w_beside 4'),
+    ('late_rows 1', 'text_last 0', 'text_finish 1'),
 )
 
 
@@ -670,10 +675,10 @@
             pltpu.VMEM((batch, half, dim), BF16),
             pltpu.VMEM((batch, half, dim), BF16),
             pltpu.VMEM((3 * heads, batch * total, HEAD), BF16),
-            pltpu.VMEM((rows, total), F32),
-            pltpu.VMEM((rows, total), F32),
-            pltpu.VMEM((rows, total), F32),
-            pltpu.VMEM((rows, total), BF16),
+            pltpu.VMEM((total, rows), F32),
+            pltpu.VMEM((total, rows), F32),
+            pltpu.VMEM((total, rows), F32),
+            pltpu.VMEM((total, rows), BF16),
             pltpu.VMEM((batch * txt_len + img_len, width), BF16),
             pltpu.VMEM((width, dim), BF16),
             *tall,
@@ -1072,8 +1077,8 @@
     for g in range(first_open, opened):
         send_o(jnp.int32(g))
 
-    stages = ((finish, -3, 0), (start_o, 8, opened), (relay_out, -4, 0), (mlp_hidden, 0, 0), (send_o, 8, opened), (relay_core, -6, 0), (mlp_out, 0, 0), (relay_o, 7, first_open),
-              (start_x, 2, txt_chunks), (project, 1, txt_chunks), (second_out, -4, 0), (add_first, -1, 0), (mlp_sum, 0, 0), (drain, -6, 0), (attend, 0, 0))
+    stages = ((finish, -3, 0), (start_o, 8, opened), (relay_out, -4, 0), (second_out, -5, 0), (mlp_hidden, 0, 0), (relay_o, 7, first_open), (start_x, 2, txt_chunks), (send_o, 8, opened),
+              (mlp_out, 0, 0), (project, 1, txt_chunks), (add_first, -1, 0), (drain, -6, 0), (relay_core, -5, 0), (mlp_sum, 0, 0), (attend, 0, 0))
     most = max(ahead for _, ahead, _ in stages)
     least = min(ahead for _, ahead, _ in stages)
 

time: 466 us -> 465 us (level)
  no operation moved by 1% of the time
where the time goes in v8:
time: 465 us
  Pallas kernels  464 us (100%)
    pallas_call x1, Pallas kernels, block_call(): pl.pallas_call(functools.partial(block_kernel, cfg), in_specs=[anywhere]...  330 us
    pallas_call x1, Pallas kernels, front_call(): pl.pallas_call(functools.partial(front_kernel, cfg), in_specs=[anywhere]...  115 us
    pallas_call x1, Pallas kernels, copy_call(): pl.pallas_call(functools.partial(copy_kernel, pieces), in_specs=[anywhere...  19.3 us

profile of v8, /device:TPU:0, one launch (start us, length us, event | category | flops | bytes accessed | tf_op | source)
XLA Modules:
  0.0 465.2 jit_solution(14803674475398668513)
XLA Ops:
  0.6 114.6 %front.1 = (bf16[2048,384]{1,0:T(8,128)(2,1)}, bf16[9,2304,128]{2,1,0:T(8,128)(2,1)}, bf16[8,384,3072]{2,1,0:T(8,128)(2,1)}, bf16[2,256,3072]{2,1,0:T(8,128)(2,1...) custom-call(bf16[2,256,3072]{2,1,0:T(8,128)(2,1)} %txt_hbm.1, ...), custom_call_target="tpu_custom_call" | custom-call | tf_op jit(solution)/shard_map/front/pallas_call | solution.py:653
  115.3 330.4 %block.1 = (bf16[4608,3072]{1,0:T(8,128)(2,1)}, bf16[2048,384]{1,0:T(8,128)(2,1)}) custom-call(bf16[2048,384]{1,0:T(8,128)(2,1)} %get-tuple-element.14.o_hbm, bf16[5,128,3072]{2,1,0:T(8,128)(2,1)} %get-tuple-element.15.og_hbm, bf16[9,2304,128]{2,1,0:T(8,128)(2,1)} %get-tuple-element.16.kv_hbm, bf16[2,2048,3072]{2,1,0:T(8,128)(2,1)} %x_hbm.1, ...), custom_call_target="tpu_custom_call" | custom-call | tf_op jit(solution)/shard_map/block/pallas_call | solution.py:1123
  445.7 19.3 %copy_out.1 = (bf16[2,256,3072]{2,1,0:T(8,128)(2,1)}, bf16[2,2048,3072]{2,1,0:T(8,128)(2,1)}) custom-call(bf16[4608,3072]{1,0:T(8,128)(2,1)} %get-tuple-element.23.flat_hbm), custom_call_target="tpu_custom_call" | custom-call | tf_op jit(solution)/shard_map/copy_out/pallas_call | solution.py:1182

commit v9 on v8

--- a/solution.py
+++ b/solution.py
@@ -98,8 +98,8 @@
 (T_CORE, T_FIRST, T_SECOND, T_OUT_FIRST, T_OUT_SECOND, T_OUT_RELAY, T_CORE_OWN, T_CORE_FIRST, T_CORE_SECOND, T_CORE_RELAY) = range(10)
 PIECES = 4
 SHARED = range(2)
-READY = 5
-EARLY = 5
+READY = 4
+EARLY = 4
 FIRST_LATE = 5
 HEADS_HERE = 3
 
@@ -429,6 +429,10 @@
     def own_rows(b1, b2):
         return rows_at(core * half + b1 * quarter + b2 * eighth, eighth)
 
+    def t_parts(b):
+        return [t_copy(kind, b, t_sum.at[b, rows_at(b1 * quarter + b2 * eighth, eighth), :], dst, dev) for kind, b1, b2, dst, dev in (
+            (T_FIRST, not1, bit2, t_rs1.at[b, :eighth], first), (T_SECOND, bit1, not2, t_rs2_in.at[b], second), (T_OUT_FIRST, not1, not2, t_rs1.at[b, eighth:], diagonal))]
+
     def t_out(kind, b, b1, b2, dev):
         ref = ut_hbm.at[b, own_rows(b1, b2), :]
         return t_copy(kind, b, t_u.at[b] if kind in (T_OUT_FIRST, T_OUT_SECOND, T_CORE_OWN) else ref, ref, dev)
@@ -471,7 +475,11 @@
             t_sum[b, at, :] = (t_own[at, :] + t_recv[b, at, :].astype(F32)).astype(BF16)
 
         loop(half // STRIP, add)
-        t_first(b).start()
+        if b < batch - 1:
+            t_first(b).start()
+            return
+        for part in t_parts(b):
+            part.start()
 
     def text_quarter(b):
         t_first(b).wait()
@@ -480,8 +488,11 @@
         t_second(b).start()
 
     def text_finish(b):
-        t_second(b).wait()
+        for part in [t_second(b)] if b < batch - 1 else t_parts(b):
+            part.wait()
         t_load(b).wait()
+        if b == batch - 1:
+            t_keep[b] = t_sum[b, rows_at(bit1 * quarter + bit2 * eighth, eighth), :].astype(F32) + t_rs1[b, :eighth].astype(F32) + t_rs1[b, eighth:].astype(F32)
         branch = t_keep[b] + t_rs2_in[b].astype(F32) + row_of(vec_ref, b, PROJ_B)
         x1 = (t_x[b].astype(F32) + row_of(vec_ref, b, GATE1) * branch).astype(BF16)
         x1_ref[b] = x1
@@ -565,11 +576,12 @@
         weigh(n, 2, s2)
 
     def step(i):
-        for when, calls in enumerate(HOOKS[:steps]):
-            if calls:
-                @pl.when(i == when)
-                def _():
-                    run(calls)
+        for start, stop in ((0, resume), (resume, steps)):
+            @pl.when((i >= start) & (i < stop))
+            def _():
+                for when, calls in enumerate(HOOKS[start:stop], start):
+                    if calls:
+                        pl.when(i == when)(functools.partial(run, calls))
 
         in_first = i < qkv_first
         in_second = (i >= qkv_first + attend_first) & (i < resume)
@@ -616,23 +628,23 @@
     (),
     (),
     ('w_relay 0',),
-    (),
+    ('w_second 0',),
     ('w_relay 1',),
     ('late_send 0',),
-    ('text_partial 0',),
-    ('text_sum 0', 'w_last 1', 'gather_start 0'),
-    ('w_last 0', 'gather_start 1'),
-    ('w_beside 0', 'gather_send 0'),
-    ('gather_start 2', 'gather_start 3', 'gather_send 1'),
-    ('w_second 0', 'text_quarter 0', 'gather_start 4'),
-    ('gather_send 3', 'gather_send 2'),
-    ('gather_relay 1', 'gather_send 4'),
-    ('late_send 1', 'w_beside 2', 'gather_relay 0'),
-    ('kv_send', 'late_rows 0', 'gather_relay 4', 'w_second 1', 'w_beside 5', 'text_finish 0'),
-    ('text_partial 1', 'gather_relay 2', 'text_sum 1'),
-    ('w_beside 1', 'text_relay 0', 'w_beside 3', 'gather_relay 3', 'w_core'),
-    ('text_quarter 1', 'w_beside 4'),
-    ('late_rows 1', 'text_last 0', 'text_finish 1'),
+    (),
+    ('gather_start 0',),
+    ('gather_send 0', 'w_beside 0'),
+    ('gather_start 2', 'gather_start 1'),
+    ('gather_send 2', 'gather_start 3', 'text_partial 0', 'w_beside 1', 'w_last 0', 'gather_send 3'),
+    ('text_sum 0', 'gather_send 1', 'w_second 1', 'gather_relay 2'),
+    ('w_core',),
+    ('late_send 1', 'text_quarter 0', 'gather_relay 0', 'w_beside 3', 'w_last 1'),
+    ('kv_send', 'late_rows 0', 'gather_relay 3', 'text_finish 0'),
+    ('gather_relay 1',),
+    ('text_partial 1', 'text_relay 0', 'text_sum 1', 'w_beside 2'),
+    ('text_last 0',),
+    ('w_beside 4',),
+    ('late_rows 1', 'w_beside 5', 'text_finish 1'),
 )
 
 
@@ -1077,8 +1089,8 @@
     for g in range(first_open, opened):
         send_o(jnp.int32(g))
 
-    stages = ((finish, -3, 0), (start_o, 8, opened), (relay_out, -4, 0), (second_out, -5, 0), (mlp_hidden, 0, 0), (relay_o, 7, first_open), (start_x, 2, txt_chunks), (send_o, 8, opened),
-              (mlp_out, 0, 0), (project, 1, txt_chunks), (add_first, -1, 0), (drain, -6, 0), (relay_core, -5, 0), (mlp_sum, 0, 0), (attend, 0, 0))
+    stages = ((finish, -3, 0), (start_o, 8, opened), (relay_out, -4, 0), (mlp_hidden, 0, 0), (send_o, 8, opened), (relay_core, -6, 0), (mlp_out, 0, 0), (relay_o, 7, first_open),
+              (start_x, 2, txt_chunks), (project, 1, txt_chunks), (second_out, -4, 0), (add_first, -1, 0), (mlp_sum, 0, 0), (drain, -6, 0), (attend, 0, 0))
     most = max(ahead for _, ahead, _ in stages)
     least = min(ahead for _, ahead, _ in stages)
 

time: 465 us -> 465 us (level)
  no operation moved by 1% of the time
where the time goes in v9:
time: 465 us
  Pallas kernels  464 us (100%)
    pallas_call x1, Pallas kernels, block_call(): pl.pallas_call(functools.partial(block_kernel, cfg), in_specs=[anywhere]...  333 us
    pallas_call x1, Pallas kernels, front_call(): pl.pallas_call(functools.partial(front_kernel, cfg), in_specs=[anywhere]...  112 us
    pallas_call x1, Pallas kernels, copy_call(): pl.pallas_call(functools.partial(copy_kernel, pieces), in_specs=[anywhere...  19.3 us

profile of v9, /device:TPU:0, one launch (start us, length us, event | category | flops | bytes accessed | tf_op | source)
XLA Modules:
  0.0 464.7 jit_solution(10433973190634050374)
XLA Ops:
  0.6 111.6 %front.1 = (bf16[2048,384]{1,0:T(8,128)(2,1)}, bf16[9,2304,128]{2,1,0:T(8,128)(2,1)}, bf16[8,384,3072]{2,1,0:T(8,128)(2,1)}, bf16[2,256,3072]{2,1,0:T(8,128)(2,1...) custom-call(bf16[2,256,3072]{2,1,0:T(8,128)(2,1)} %txt_hbm.1, ...), custom_call_target="tpu_custom_call" | custom-call | tf_op jit(solution)/shard_map/front/pallas_call | solution.py:665
  112.3 333.0 %block.1 = (bf16[4608,3072]{1,0:T(8,128)(2,1)}, bf16[2048,384]{1,0:T(8,128)(2,1)}) custom-call(bf16[2048,384]{1,0:T(8,128)(2,1)} %get-tuple-element.14.o_hbm, bf16[4,128,3072]{2,1,0:T(8,128)(2,1)} %get-tuple-element.15.og_hbm, bf16[9,2304,128]{2,1,0:T(8,128)(2,1)} %get-tuple-element.16.kv_hbm, bf16[2,2048,3072]{2,1,0:T(8,128)(2,1)} %x_hbm.1, ...), custom_call_target="tpu_custom_call" | custom-call | tf_op jit(solution)/shard_map/block/pallas_call | solution.py:1135
  445.3 19.3 %copy_out.1 = (bf16[2,256,3072]{2,1,0:T(8,128)(2,1)}, bf16[2,2048,3072]{2,1,0:T(8,128)(2,1)}) custom-call(bf16[4608,3072]{1,0:T(8,128)(2,1)} %get-tuple-element.23.flat_hbm), custom_call_target="tpu_custom_call" | custom-call | tf_op jit(solution)/shard_map/copy_out/pallas_call | solution.py:1194

commit v10 on v9

--- a/solution.py
+++ b/solution.py
@@ -630,21 +630,21 @@
     ('w_relay 0',),
     ('w_second 0',),
     ('w_relay 1',),
-    ('late_send 0',),
+    ('late_send 0', 'w_last 0'),
     (),
-    ('gather_start 0',),
-    ('gather_send 0', 'w_beside 0'),
+    ('gather_start 0', 'w_second 1'),
+    ('gather_send 0', 'w_beside 0', 'w_last 1'),
     ('gather_start 2', 'gather_start 1'),
-    ('gather_send 2', 'gather_start 3', 'text_partial 0', 'w_beside 1', 'w_last 0', 'gather_send 3'),
-    ('text_sum 0', 'gather_send 1', 'w_second 1', 'gather_relay 2'),
-    ('w_core',),
-    ('late_send 1', 'text_quarter 0', 'gather_relay 0', 'w_beside 3', 'w_last 1'),
-    ('kv_send', 'late_rows 0', 'gather_relay 3', 'text_finish 0'),
+    ('gather_send 2', 'gather_start 3', 'text_partial 0', 'w_beside 1', 'gather_send 3'),
+    ('text_sum 0', 'gather_send 1', 'gather_relay 2'),
+    ('w_core', 'w_beside 3'),
+    ('late_send 1', 'text_quarter 0', 'gather_relay 0'),
+    ('kv_send', 'late_rows 0', 'gather_relay 3', 'text_finish 0', 'w_beside 2'),
     ('gather_relay 1',),
-    ('text_partial 1', 'text_relay 0', 'text_sum 1', 'w_beside 2'),
-    ('text_last 0',),
-    ('w_beside 4',),
-    ('late_rows 1', 'w_beside 5', 'text_finish 1'),
+    ('text_partial 1', 'text_relay 0', 'text_sum 1', 'w_beside 4'),
+    ('text_last 0', 'late_rows 1'),
+    (),
+    ('w_beside 5', 'text_finish 1'),
 )
 
 

time: 465 us -> 465 us (level)
  no operation moved by 1% of the time
where the time goes in v10:
time: 465 us
  Pallas kernels  464 us (100%)
    pallas_call x1, Pallas kernels, block_call(): pl.pallas_call(functools.partial(block_kernel, cfg), in_specs=[anywhere]...  333 us
    pallas_call x1, Pallas kernels, front_call(): pl.pallas_call(functools.partial(front_kernel, cfg), in_specs=[anywhere]...  112 us
    pallas_call x1, Pallas kernels, copy_call(): pl.pallas_call(functools.partial(copy_kernel, pieces), in_specs=[anywhere...  19.3 us

profile of v10, /device:TPU:0, one launch (start us, length us, event | category | flops | bytes accessed | tf_op | source)
XLA Modules:
  0.0 464.8 jit_solution(5880095513596413321)
XLA Ops:
  0.6 111.7 %front.1 = (bf16[2048,384]{1,0:T(8,128)(2,1)}, bf16[9,2304,128]{2,1,0:T(8,128)(2,1)}, bf16[8,384,3072]{2,1,0:T(8,128)(2,1)}, bf16[2,256,3072]{2,1,0:T(8,128)(2,1...) custom-call(bf16[2,256,3072]{2,1,0:T(8,128)(2,1)} %txt_hbm.1, ...), custom_call_target="tpu_custom_call" | custom-call | tf_op jit(solution)/shard_map/front/pallas_call | solution.py:665
  112.3 333.0 %block.1 = (bf16[4608,3072]{1,0:T(8,128)(2,1)}, bf16[2048,384]{1,0:T(8,128)(2,1)}) custom-call(bf16[2048,384]{1,0:T(8,128)(2,1)} %get-tuple-element.14.o_hbm, bf16[4,128,3072]{2,1,0:T(8,128)(2,1)} %get-tuple-element.15.og_hbm, bf16[9,2304,128]{2,1,0:T(8,128)(2,1)} %get-tuple-element.16.kv_hbm, bf16[2,2048,3072]{2,1,0:T(8,128)(2,1)} %x_hbm.1, ...), custom_call_target="tpu_custom_call" | custom-call | tf_op jit(solution)/shard_map/block/pallas_call | solution.py:1135
  445.4 19.3 %copy_out.1 = (bf16[2,256,3072]{2,1,0:T(8,128)(2,1)}, bf16[2,2048,3072]{2,1,0:T(8,128)(2,1)}) custom-call(bf16[4608,3072]{1,0:T(8,128)(2,1)} %get-tuple-element.23.flat_hbm), custom_call_target="tpu_custom_call" | custom-call | tf_op jit(solution)/shard_map/copy_out/pallas_call | solution.py:1194
